TPU v7x, 32 devices: a whole 2x2x4 slice. The times are simulated.
32 devices in a mesh: fsdp: 4 (over x, core), seq: 8 (over z, y).
Axes of the slice: x: 2, y: 2, z: 4, core: 2. Of those that a mesh axis runs over, the one named last changes fastest.
Arguments:
- layer_in: bfloat16 [12288, 1024], P(('fsdp', 'seq'))
- cotangent: bfloat16 [12288, 1024], P(('fsdp', 'seq')), may hold values from -6 to 6
- doc_ids: int32 [4, 3072], P('fsdp'), may hold values from 0 to 5, never falling along the last dimension, each value on 1 to 1024 neighbouring positions
- valid_len: int32 [4], P('fsdp'), may hold values from 1536 to 3072
- attn_weights: bfloat16 [4096, 1024], P(('fsdp', 'seq'))
- mlp_weights: bfloat16 [8192, 1024], P(('fsdp', 'seq'))
- param_vector: bfloat16 [12288], P(('fsdp', 'seq'))
Outputs:
- layer_out: bfloat16 [12288, 1024], P(('fsdp', 'seq'))
- input_grad: float32 [12288, 1024], P(('fsdp', 'seq'))
- attn_grad: float32 [4096, 1024], P(('fsdp', 'seq'))
- mlp_grad: float32 [8192, 1024], P(('fsdp', 'seq'))
- vector_grad: float32 [12288], P(('fsdp', 'seq'))
- rms_values: float32 [4], replicated
Inputs may be any that keep to these rules, and one draw needn't show every extreme that they name: `doc_ids`: in each row the numbers never fall and every number is used; a document is a run of 1 to 1024 tokens, and one run in each row has exactly 1024.
All inputs are finite; a program needn't handle non-finite values.
Results may differ from a plain program's by a relative error of at most 0.012.
The roundings to bfloat16 on the way count: a program that leaves them out, or rounds other values in their place, can miss the bound.
Values may be sent and summed in bfloat16 or wider, within the bound.
A program may use at most 192 MiB of HBM per device.

v0:
```python
import jax
import jax.numpy as jnp
from jax import lax
from jax.sharding import PartitionSpec as P

H = 16


EPSILON = 1e-05
ROOT_HALF = 0.7071067811865476
INV_ROOT_TWO_PI = 0.3989422804014327


def norm_forward(values, norm_gain, norm_shift):
    row_mean = jnp.mean(values, axis=1, keepdims=True)
    centered = values - row_mean
    inverse = lax.rsqrt(jnp.mean(centered * centered, axis=1, keepdims=True) + EPSILON)
    scaled = centered * inverse
    return (scaled * norm_gain + norm_shift, scaled, inverse)


def norm_backward(gradient, scaled, inverse, norm_gain):
    grad_scaled = gradient * norm_gain
    grad_mean = jnp.mean(grad_scaled, axis=1, keepdims=True)
    grad_along = jnp.mean(grad_scaled * scaled, axis=1, keepdims=True)
    grad_rows = inverse * (grad_scaled - grad_mean - scaled * grad_along)
    return (grad_rows, jnp.sum(gradient * scaled, axis=0), jnp.sum(gradient, axis=0))


def gelu_slope(entries):
    return 0.5 * (1.0 + lax.erf(entries * ROOT_HALF)) + entries * INV_ROOT_TWO_PI * jnp.exp(
        -0.5 * entries * entries
    )


def attend_block(queries, key_rows, query_doc, key_doc, score_scale):
    scores = (
        jnp.einsum("qhd,khd->hqk", queries, key_rows, preferred_element_type=jnp.float32)
        * score_scale
    )
    same_doc = query_doc[:, None] == key_doc[None, :]
    return jnp.where(same_doc[None], scores, -1e30)


def contract_rows(left, right):
    return lax.dot_general(
        left, right, (((0,), (0,)), ((), ())), preferred_element_type=jnp.float32
    )


def contract_cols(left, right):
    return lax.dot_general(
        left, right, (((1,), (1,)), ((), ())), preferred_element_type=jnp.float32
    )


def per_device(layer_in, cotangent, doc_ids, valid_len, attn_weights, mlp_weights, param_vector):
    seq_count = lax.axis_size("seq")
    seq_index = lax.axis_index("seq")
    tokens, model_width = layer_in.shape
    head_size = model_width // H
    local_heads = H // seq_count
    score_scale = head_size ** (-0.5)
    attn_full, mlp_full, vector_full = (
        lax.all_gather(attn_weights, ("fsdp", "seq"), axis=0, tiled=True),
        lax.all_gather(mlp_weights, ("fsdp", "seq"), axis=0, tiled=True),
        lax.all_gather(param_vector, ("fsdp", "seq"), axis=0, tiled=True),
    )
    hidden = mlp_full.shape[0] // 2
    vector_wide = vector_full.astype(jnp.float32)
    pieces = [
        vector_wide[slot_index * model_width : (slot_index + 1) * model_width]
        for slot_index in range(8)
    ]
    bias_q, bias_v, bias_o, gain_one, shift_one, bias_two, gain_two, shift_two = pieces
    bias_up = vector_wide[8 * model_width :]
    qkv_weights = attn_full[: 3 * model_width].reshape(3, model_width, model_width)
    out_weights = attn_full[3 * model_width :]
    in_weights = mlp_full[:hidden]
    down_weights = mlp_full[hidden:]
    segment_doc = doc_ids[0]
    seg_len = segment_doc.shape[0]
    block_rows = min(512, seg_len)
    block_count = seg_len // block_rows
    doc_blocks = segment_doc.reshape(block_count, block_rows)
    positions = seq_index * tokens + lax.iota(jnp.int32, tokens)
    valid_rows = (positions < valid_len[0]).astype(jnp.float32)[:, None]
    zero_row = jnp.zeros((1, model_width), jnp.float32)
    qkv_bias = jnp.concatenate([bias_q[None], zero_row, bias_v[None]], axis=0)
    projected = (
        jnp.einsum("td,ide->tie", layer_in, qkv_weights, preferred_element_type=jnp.float32)
        + qkv_bias[None]
    )
    qkv_split = projected.astype(jnp.bfloat16).reshape(tokens, 3, seq_count, local_heads, head_size)
    head_piece = lax.all_to_all(qkv_split, "seq", split_axis=2, concat_axis=0, tiled=True)
    queries = head_piece[:, 0, 0]
    attend_key_rows = head_piece[:, 1, 0]
    attend_value_rows = head_piece[:, 2, 0]
    head_count = queries.shape[1]
    query_blocks = queries.reshape(block_count, block_rows, head_count, head_size)

    def one_block(block_pair):
        query_part, doc_part = block_pair
        scores = attend_block(query_part, attend_key_rows, doc_part, segment_doc, score_scale)
        top_score = jnp.max(scores, axis=-1, keepdims=True)
        exponent = jnp.exp(scores - top_score)
        row_total = jnp.sum(exponent, axis=-1, keepdims=True)
        weights_low = (exponent / row_total).astype(jnp.bfloat16)
        mixed_part = jnp.einsum(
            "hqk,khd->qhd", weights_low, attend_value_rows, preferred_element_type=jnp.float32
        )
        return (mixed_part, (top_score + jnp.log(row_total))[..., 0])

    mixed_rows, log_total = lax.map(one_block, (query_blocks, doc_blocks))
    mixed_rows = mixed_rows.reshape(seg_len, 1, head_count, head_size).astype(jnp.bfloat16)
    log_total = jnp.transpose(log_total, (0, 2, 1)).reshape(seg_len, 1, head_count)
    token_mixed = lax.all_to_all(mixed_rows, "seq", split_axis=0, concat_axis=1, tiled=True)
    attn_mixed = token_mixed.reshape(tokens, model_width)
    branch = jnp.dot(attn_mixed, out_weights, preferred_element_type=jnp.float32) + bias_o
    resid_one = layer_in.astype(jnp.float32) + branch
    normed, scaled_one, inverse_one = norm_forward(resid_one, gain_one, shift_one)
    normed_low = normed.astype(jnp.bfloat16)
    upper = contract_cols(normed_low, in_weights) + bias_up
    active_low = jax.nn.gelu(upper, approximate=False).astype(jnp.bfloat16)
    mlp_branch = jnp.dot(active_low, down_weights, preferred_element_type=jnp.float32) + bias_two
    resid_two = normed + mlp_branch
    layer_values, scaled_two, inverse_two = norm_forward(resid_two, gain_two, shift_two)
    squares = jnp.stack(
        [
            jnp.sum(valid_rows * resid_one * resid_one),
            jnp.sum(valid_rows * branch * branch),
            jnp.sum(valid_rows * resid_two * resid_two),
            jnp.sum(valid_rows * mlp_branch * mlp_branch),
        ]
    )
    square_sums, valid_total = lax.psum((squares, jnp.sum(valid_rows)), ("fsdp", "seq"))
    rms_values = jnp.sqrt(square_sums / (valid_total * model_width))
    grad_out = cotangent.astype(jnp.float32)
    grad_resid_two, grad_gain_two, grad_shift_two = norm_backward(
        grad_out, scaled_two, inverse_two, gain_two
    )
    grad_mlp_low = grad_resid_two.astype(jnp.bfloat16)
    grad_bias_two = jnp.sum(grad_mlp_low.astype(jnp.float32), axis=0)
    grad_down = contract_rows(active_low, grad_mlp_low)
    grad_active = contract_cols(grad_mlp_low, down_weights)
    grad_upper_low = (grad_active * gelu_slope(upper)).astype(jnp.bfloat16)
    grad_bias_up = jnp.sum(grad_upper_low.astype(jnp.float32), axis=0)
    grad_in = contract_rows(grad_upper_low, normed_low)
    grad_normed = grad_resid_two + jnp.dot(
        grad_upper_low, in_weights, preferred_element_type=jnp.float32
    )
    grad_mlp_full = jnp.concatenate([grad_in, grad_down], axis=0)
    mlp_shard = None
    grad_resid_one, grad_gain_one, grad_shift_one = norm_backward(
        grad_normed, scaled_one, inverse_one, gain_one
    )
    grad_branch_low = grad_resid_one.astype(jnp.bfloat16)
    grad_bias_o = jnp.sum(grad_branch_low.astype(jnp.float32), axis=0)
    grad_out_weights = contract_rows(attn_mixed, grad_branch_low)
    grad_mixed_low = contract_cols(grad_branch_low, out_weights).astype(jnp.bfloat16)
    grad_split = grad_mixed_low.reshape(tokens, 1, seq_count, local_heads, head_size)
    grad_heads = lax.all_to_all(grad_split, "seq", split_axis=2, concat_axis=0, tiled=True)
    head_inputs = head_piece[:, :, 0]
    head_grad = grad_heads[:, 0, 0]
    queries = head_inputs[:, 0]
    key_rows = head_inputs[:, 1]
    value_rows = head_inputs[:, 2]
    query_blocks = queries.reshape(block_count, block_rows, local_heads, head_size)
    grad_blocks = head_grad.reshape(block_count, block_rows, local_heads, head_size)
    log_blocks = log_total.reshape(block_count, block_rows, local_heads)

    def back_block(running, block_inputs):
        grad_keys, grad_values = running
        query_part, grad_part, log_part, doc_part = block_inputs
        scores = attend_block(query_part, key_rows, doc_part, segment_doc, score_scale)
        probs = jnp.exp(scores - jnp.transpose(log_part)[:, :, None])
        grad_probs = jnp.einsum(
            "qhd,khd->hqk", grad_part, value_rows, preferred_element_type=jnp.float32
        )
        row_inner = jnp.sum(grad_probs * probs, axis=-1, keepdims=True)
        grad_scores = (probs * (grad_probs - row_inner)).astype(jnp.bfloat16)
        grad_query = (
            jnp.einsum("hqk,khd->qhd", grad_scores, key_rows, preferred_element_type=jnp.float32)
            * score_scale
        )
        grad_keys = (
            grad_keys
            + jnp.einsum(
                "hqk,qhd->khd", grad_scores, query_part, preferred_element_type=jnp.float32
            )
            * score_scale
        )
        grad_values = grad_values + jnp.einsum(
            "hqk,qhd->khd",
            probs.astype(jnp.bfloat16),
            grad_part,
            preferred_element_type=jnp.float32,
        )
        return ((grad_keys, grad_values), grad_query)

    zeros_head = jnp.zeros((seg_len, local_heads, head_size), jnp.float32)
    (grad_keys, grad_values), grad_queries = lax.scan(
        back_block, (zeros_head, zeros_head), (query_blocks, grad_blocks, log_blocks, doc_blocks)
    )
    grad_queries = grad_queries.reshape(seg_len, local_heads, head_size)
    head_grads = jnp.stack([grad_queries, grad_keys, grad_values], axis=1).astype(jnp.bfloat16)[
        :, :, None
    ]
    token_grads = lax.all_to_all(head_grads, "seq", split_axis=0, concat_axis=2, tiled=True)
    grad_qkv = token_grads.reshape(tokens, 3, model_width)
    input_grad = grad_resid_one + jnp.einsum(
        "tie,ide->td", grad_qkv, qkv_weights, preferred_element_type=jnp.float32
    )
    grad_qkv_weights = jnp.einsum(
        "td,tie->ide", layer_in, grad_qkv, preferred_element_type=jnp.float32
    )
    grad_bias_qkv = jnp.sum(grad_qkv.astype(jnp.float32), axis=0)
    grad_vector = jnp.concatenate(
        [
            grad_bias_qkv[0],
            grad_bias_qkv[2],
            grad_bias_o,
            grad_gain_one,
            grad_shift_one,
            grad_bias_two,
            grad_gain_two,
            grad_shift_two,
            grad_bias_up,
        ]
    )
    grad_attn_full = jnp.concatenate(
        [grad_qkv_weights.reshape(3 * model_width, model_width), grad_out_weights], axis=0
    )
    attn_shard, mlp_shard, vector_shard = (
        lax.psum_scatter(grad_attn_full, ("fsdp", "seq"), scatter_dimension=0, tiled=True),
        lax.psum_scatter(grad_mlp_full, ("fsdp", "seq"), scatter_dimension=0, tiled=True),
        lax.psum_scatter(grad_vector, ("fsdp", "seq"), scatter_dimension=0, tiled=True),
    )
    return (
        layer_values.astype(jnp.bfloat16),
        input_grad,
        attn_shard,
        mlp_shard,
        vector_shard,
        rms_values,
    )


def solution(mesh):
    in_specs = (
        P(("fsdp", "seq"), None),
        P(("fsdp", "seq"), None),
        P("fsdp", None),
        P("fsdp"),
        P(("fsdp", "seq"), None),
        P(("fsdp", "seq"), None),
        P(("fsdp", "seq")),
    )
    out_specs = (
        P(("fsdp", "seq"), None),
        P(("fsdp", "seq"), None),
        P(("fsdp", "seq"), None),
        P(("fsdp", "seq"), None),
        P(("fsdp", "seq")),
        P(),
    )
    return jax.shard_map(
        per_device, mesh=mesh, in_specs=in_specs, out_specs=out_specs, check_vma=False
    )
```

profile of v0, /device:TPU:0, one launch (start us, length us, event | category | flops | bytes accessed | tf_op | source)
XLA Modules:
  0.0 1757.3 jit_solution(14414181553958919189)
XLA Ops:
  8.6 71.2 %all-gather = bf16[32,1,384]{2,1,0:T(2,128)(2,1)S(1)} all-gather(bf16[1,1,384]{2,1,0:T(2,128)(2,1)S(1)} %reshape.250), channel_id=1, replica_groups=mesh['fsdp'=4,'seq'=8] {'fsdp','seq'}, dimensions={0}, use_global_device_ids=true | all-gather | bytes 25344 | tf_op jit(solution)/shard_map/all_gather | solution.py:67
  80.6 10.3 all-gather.4.cloned.1.call-done
  97.0 3.9 add_convert_fusion
  105.8 4.0 all-to-all-start
  111.7 77.5 %all-to-all-done = bf16[384,3,8,2,64]{0,4,3,1,2:T(8,128)(2,1)S(1)} async-done(((bf16[384,3,8,2,64]{0,4,3,1,2:T(8,128)(2,1)}), bf16[384,3,8,2,64]{0,4,3,1,2:T(8,128)(2,1)S(1)}, u32[]{:S(2)}, u32[]{:S(2)}) %all-to-all-start) | async-done | bytes 2359328 | tf_op jit(solution)/shard_map/all_to_all | solution.py:95
  194.6 75.9 %while.27 = (s32[]{:T(128)}, bf16[6,512,2,64]{1,3,2,0:T(8,128)(2,1)S(1)}, f32[6,2,512]{2,1,0:T(2,128)S(1)}, s32[6,512]{1,0:T(8,128)S(1)}, s32[1,3072]{1,0:T(1,12...) while((s32[]{:T(128)}, ...), condition=%wide.region_3.4_spmd, body=%wide.region_0.3_spmd.sunk | while | flops 844626944 | bytes 49203344 | solution.py:114
  195.6 4.2 fusion.147
  199.7 3.6 fusion.148
  203.4 3.8 fusion.149
  208.2 4.2 fusion.147
  212.4 3.6 fusion.148
  216.1 3.8 fusion.149
  220.9 4.2 fusion.147
  228.7 3.8 fusion.149
  233.5 4.2 fusion.147
  241.4 3.8 fusion.149
  246.2 4.2 fusion.147
  254.0 3.8 fusion.149
  258.8 4.2 fusion.147
  266.7 3.8 fusion.149
  273.6 4.6 all-to-all-start.1
  279.6 18.7 %all-to-all-done.1 = bf16[8,2,24576]{2,1,0:T(2,128)(2,1)S(1)} async-done(((bf16[8,2,24576]{2,1,0:T(2,128)(2,1)}), bf16[8,2,24576]{2,1,0:T(2,128)(2,1)S(1)}, u32[]{:S(2)}, u32[]{:S(2)}) %all-to-all-start.1) | async-done | bytes 786464 | tf_op jit(solution)/shard_map/all_to_all | solution.py:117
  301.4 3.8 fusion.107
  305.6 32.3 %fusion.51 = (bf16[384,4096]{1,0:T(8,128)(2,1)S(1)}, f32[384,4096]{1,0:T(8,128)}) fusion(f32[4096]{0:T(1024)S(1)} %slice.97, bf16[8192,1024]{1,0:T(8,128)(2,1)} %all-gather.6.cloned.1.call-done, f32[384,1024]{1,0:T(8,128)S(1)} %get-tuple-element.323, f32[1024]{0:T(1024)S(1)} %copy-done.35, f32[1024]{0:T(1024)S(1)} %copy-done.23, ...), kind=kOutput, calls=%fused_computation.64 | convolution fusion | flops 3327000576 | bytes 19426304 | tf_op jit(solution)/shard_map/dot_general | solution.py:52
  338.0 4.4 fusion.78
  346.7 9.8 convert_reduce_fusion
  356.5 8.3 multiply_reduce_fusion.1
  370.9 4.2 all-to-all-start.2
  375.1 4.6 copy.106
  379.7 4.9 squeeze.44
  403.1 176.9 %while.28 = (s32[]{:T(128)}, f32[3072,2,64]{0,2,1:T(8,128)S(1)}, f32[3072,2,64]{0,2,1:T(8,128)}, bf16[6,512,2,64]{1,3,2,0:T(8,128)(2,1)}, bf16[6,512,2,64]{1,3,2...) while((s32[]{:T(128)}, f32[3072,2,64]{0,2,1:T(8,128)S(1)}, ...), condition=%wide.region_14.15_spmd.clone, body=%wide.region_12.14_spmd.clone.sunk | while | flops 2064055296 | bytes 122730720 | solution.py:202
  407.3 4.7 fusion.161
  412.1 8.4 multiply_reduce_fusion.7
  420.4 7.5 multiply_convert_fusion.2
  436.7 4.7 fusion.161
  441.5 8.4 multiply_reduce_fusion.7
  449.8 7.5 multiply_convert_fusion.2
  466.1 4.7 fusion.161
  470.9 8.4 multiply_reduce_fusion.7
  479.2 7.5 multiply_convert_fusion.2
  495.5 4.7 fusion.161
  500.3 8.4 multiply_reduce_fusion.7
  508.6 7.5 multiply_convert_fusion.2
  524.9 4.7 fusion.161
  529.7 8.4 multiply_reduce_fusion.7
  538.0 7.5 multiply_convert_fusion.2
  554.3 4.7 fusion.161
  559.1 8.4 multiply_reduce_fusion.7
  567.4 7.5 multiply_convert_fusion.2
  584.4 8.0 copy.119
  592.5 8.0 reshape.268
  604.1 4.6 fusion.96
  608.7 49.3 %all-to-all-done.3 = bf16[8,2,73728]{2,1,0:T(2,128)(2,1)S(1)} async-done(((bf16[8,2,73728]{2,1,0:T(2,128)(2,1)}), bf16[8,2,73728]{2,1,0:T(2,128)(2,1)S(1)}, u32[]{:S(2)}, u32[]{:S(2)}) %all-to-all-start.3) | async-done | bytes 2359328 | tf_op jit(solution)/shard_map/all_to_all | solution.py:209
  658.0 5.3 reshape.269
  663.3 10.2 copy.133
  677.1 7.2 pad_maximum_fusion.1
  685.7 6.5 fusion.99
  692.2 7.2 fusion.102
  699.4 12.6 pad_maximum_fusion
  715.4 8.3 copy.132
  726.4 44.2 %all-reduce.1 = (f32[12288]{0:T(1024)S(1)}, f32[4]{0:T(128)S(1)}, f32[]{:T(128)}) all-reduce(f32[12288]{0:T(1024)S(1)} %constant_dynamic-update-slice_fusion, f32[4]{0:T(128)S(1)} %pad_maximum_fusion.4, f32[]{:T(128)} %fusion.95), channel_id=4, replica_groups=mesh['fsdp'=4,'seq'=8] {'fsdp','seq'}, use_global_device_ids=true, to_apply=%region_25.26.clone | all-reduce | flops 12293 | bytes 98344
  772.4 7.1 bitcast_add_fusion
  779.5 263.2 %reduce-scatter.3.cloned.1.call-done = f32[128,1024]{1,0:T(8,128)} async-done(((f32[4096,1024]{1,0:T(8,128)}), f32[128,1024]{1,0:T(8,128)}) %reduce-scatter.3.cloned.1.call-update) | async-done | bytes 524304 | tf_op jit(solution)/shard_map/reduce_scatter | solution.py:235
  1042.7 707.8 %reduce-scatter.5.cloned.1.call-done = f32[256,1024]{1,0:T(8,128)} async-done(((f32[8192,1024]{1,0:T(8,128)}), f32[256,1024]{1,0:T(8,128)}) %reduce-scatter.5.cloned.1.call-update) | async-done | bytes 1048592 | tf_op jit(solution)/shard_map/reduce_scatter | solution.py:236
  (257 shorter events, 149.1 us)
Async XLA Ops:
  7.2 83.8 %all-gather.4.cloned.1.call-start = ((), (), s32[]{:S(2)}) async-start(), calls=%async_computation.6 | async-start | bytes 8650752 | tf_op jit(solution)/shard_map/all_gather | solution.py:65
  80.6 16.4 copy-start.17
  94.4 2.6 copy-start.7
  101.0 10.1 copy-start.16
  105.8 83.5 %all-to-all-start = ((bf16[384,3,8,2,64]{0,4,3,1,2:T(8,128)(2,1)}), bf16[384,3,8,2,64]{0,4,3,1,2:T(8,128)(2,1)S(1)}, u32[]{:S(2)}, u32[]{:S(2)}) async-start(bf16[384,3,8,2,64]{0,4,3,1,2:T(8,128)(2,1)} %copy.105), calls=%async_computation | async-start | bytes 4718592 | tf_op jit(solution)/shard_map/all_to_all | solution.py:95
  109.8 195.8 %all-gather.6.cloned.1.call-start = ((), (), s32[]{:S(2)}) async-start(), calls=%async_computation.7 | async-start | bytes 17301504 | tf_op jit(solution)/shard_map/all_gather | solution.py:66
  189.2 5.3 copy-start.1
  199.7 3.7 copy-start.20
  212.4 3.7 copy-start.20
  225.1 3.7 copy-start.20
  237.7 3.7 copy-start.20
  250.4 3.7 copy-start.20
  263.0 3.7 copy-start.20
  270.6 30.9 %copy-start.18 = (bf16[384,1024]{1,0:T(8,128)(2,1)S(1)}, bf16[384,1024]{1,0:T(8,128)(2,1)}, u32[]{:S(2)}) copy-start(bf16[384,1024]{1,0:T(8,128)(2,1)} %param.11) | copy-start | bytes 2359300
  270.6 30.9 %copy-start.38 = (f32[1024]{0:T(1024)S(1)}, f32[1024]{0:T(1024)}, u32[]{:S(2)}) copy-start(f32[1024]{0:T(1024)} %get-tuple-element.344) | copy-start | bytes 12292
  273.6 24.7 %all-to-all-start.1 = ((bf16[8,2,24576]{2,1,0:T(2,128)(2,1)}), bf16[8,2,24576]{2,1,0:T(2,128)(2,1)S(1)}, u32[]{:S(2)}, u32[]{:S(2)}) async-start(bf16[8,2,24576]{2,1,0:T(2,128)(2,1)} %reshape.266), calls=%async_computation.1 | async-start | bytes 1572864 | tf_op jit(solution)/shard_map/all_to_all | solution.py:117
  300.3 5.2 copy-start.23
  300.4 5.2 copy-start.35
  305.2 59.6 %copy-start.4 = (f32[384,1024]{1,0:T(8,128)}, f32[384,1024]{1,0:T(8,128)S(1)}, u32[]{:S(2)}) copy-start(f32[384,1024]{1,0:T(8,128)S(1)} %get-tuple-element.323) | copy-start | bytes 4718596
  305.2 59.6 %copy-start.25 = (f32[384]{0:T(512)}, f32[384]{0:T(512)S(1)}, u32[]{:S(2)}) copy-start(f32[384]{0:T(512)S(1)} %broadcast_multiply_fusion.5) | copy-start | bytes 4612
  305.5 59.3 %copy-start.27 = (f32[384]{0:T(512)}, f32[384]{0:T(512)S(1)}, u32[]{:S(2)}) copy-start(f32[384]{0:T(512)S(1)} %add_rsqrt_fusion.1) | copy-start | bytes 4612
  305.6 32.4 %copy-start.37 = (f32[1024]{0:T(1024)S(1)}, f32[1024]{0:T(1024)}, u32[]{:S(2)}) copy-start(f32[1024]{0:T(1024)} %get-tuple-element.341) | copy-start | bytes 12292
  305.6 32.4 %copy-start.41 = (bf16[8192,1024]{1,0:T(8,128)(2,1)S(1)}, bf16[8192,1024]{1,0:T(8,128)(2,1)}, u32[]{:S(2)}) copy-start(bf16[8192,1024]{1,0:T(8,128)(2,1)} %all-gather.6.cloned.1.call-done) | copy-start | bytes 50331652
  305.6 32.4 %copy-start.42 = (f32[384,1024]{1,0:T(8,128)S(1)}, f32[384,1024]{1,0:T(8,128)}, u32[]{:S(2)}) copy-start(f32[384,1024]{1,0:T(8,128)} %get-tuple-element.347) | copy-start | bytes 4718596
  337.9 4.5 copy-start.9
  338.0 4.8 copy-start.13
  338.0 4.8 copy-start.22
  338.0 6.5 copy-start.33
  346.7 9.8 copy-start.5
  356.5 8.3 copy-start.10
  365.9 1.1 copy-start.8
  370.9 24.1 %all-to-all-start.2 = ((bf16[384,1,8,2,64]{0,4,3,1,2:T(8,128)(2,1)}), bf16[384,1,8,2,64]{0,4,3,1,2:T(8,128)(2,1)}, u32[]{:S(2)}, u32[]{:S(2)}) async-start(bf16[384,1,8,2,64]{0,4,3,1,2:T(8,128)(2,1)} %bitcast.24), calls=%async_computation.2 | async-start | bytes 1572864 | tf_op jit(solution)/shard_map/all_to_all | solution.py:162
  404.5 2.9 copy-start.14
  412.1 8.4 copy-start.15
  433.9 2.9 copy-start.14
  441.5 8.4 copy-start.15
  463.3 2.9 copy-start.14
  470.9 8.4 copy-start.15
  492.6 2.9 copy-start.14
  500.3 8.4 copy-start.15
  522.0 2.9 copy-start.14
  529.7 8.4 copy-start.15
  551.4 2.9 copy-start.14
  559.1 8.4 copy-start.15
  592.4 11.7 copy-start.12
  600.4 57.5 %all-to-all-start.3 = ((bf16[8,2,73728]{2,1,0:T(2,128)(2,1)}), bf16[8,2,73728]{2,1,0:T(2,128)(2,1)S(1)}, u32[]{:S(2)}, u32[]{:S(2)}) async-start(bf16[8,2,73728]{2,1,0:T(2,128)(2,1)} %reshape.268), calls=%async_computation.3 | async-start | bytes 4718592 | tf_op jit(solution)/shard_map/all_to_all | solution.py:209
  604.0 438.6 %reduce-scatter.3.cloned.1.call-start = ((), (), s32[]{:S(2)}) async-start(), calls=%async_computation.8 | async-start | bytes 17301504 | tf_op jit(solution)/shard_map/reduce_scatter | solution.py:235
  608.7 64.9 %copy-start.19 = (bf16[384,1024]{1,0:T(8,128)(2,1)S(1)}, bf16[384,1024]{1,0:T(8,128)(2,1)}, u32[]{:S(2)}) copy-start(bf16[384,1024]{1,0:T(8,128)(2,1)} %param.11) | copy-start | bytes 2359300
  673.5 3.5 copy-start.2
  673.5 3.5 copy-start
  684.2 1.4 copy-start.6
  684.3 7.9 copy-start.24
  684.3 7.9 copy-start.26
  684.3 7.9 copy-start.28
  684.3 7.9 copy-start.36
  684.3 1066.2 %reduce-scatter.5.cloned.1.call-start = ((), (), s32[]{:S(2)}) async-start(), calls=%async_computation.9 | async-start | bytes 34603008 | tf_op jit(solution)/shard_map/reduce_scatter | solution.py:236
  712.0 14.2 copy-start.31
  712.0 14.2 copy-start.40
  712.0 14.2 copy-start.39
  712.0 14.2 copy-start.34
  712.1 14.3 copy-start.30
  712.1 14.3 copy-start.29
  712.1 14.3 copy-start.32
  712.1 60.4 %copy-start.3 = (bf16[8,384,3,1,2,64]{1,5,4,0,2,3:T(8,128)(2,1)S(1)}, bf16[8,384,3,1,2,64]{1,5,4,0,2,3:T(8,128)(2,1)}, u32[]{:S(2)}) copy-start(bf16[8,384,3,1,2,64]{1,5,4,0,2,3:T(8,128)(2,1)} %copy-done.2) | copy-start | bytes 7077892
  (2 other events, 1.6 us)
Sparse Core Ops, SparseCore 0:
  11.0 79.9 all-gather.3
  113.7 142.0 all-gather.5
  684.4 358.2 reduce-scatter.2
  1045.4 705.0 reduce-scatter.4
where the time goes:
time: 1760 us
  waiting for transfers between devices  1130 us (64%)
  matrix products  267 us (15%)
  blocking collectives  115 us (7%)
  other arithmetic  112 us (6%)
  local copies, waits for them, and re-layouts  97.5 us (6%)
    reduce_scatter x1, waiting for transfers between devices, per_device(): lax.psum_scatter(grad_mlp_full, ('fsdp', 'seq'), scatter_dimension=0, til...  708 us
    reduce_scatter x1, waiting for transfers between devices, per_device(): lax.psum_scatter(grad_attn_full, ('fsdp', 'seq'), scatter_dimension=0, ti...  263 us
    all_to_all x1, waiting for transfers between devices, per_device(): lax.all_to_all(qkv_split, 'seq', split_axis=2, concat_axis=0, tiled=True)  77.5 us
    all_gather x1, blocking collectives, per_device(): lax.all_gather(param_vector, ('fsdp', 'seq'), axis=0, tiled=True)  71.2 us
    dot_general x6, matrix products, back_block(): jnp.einsum('qhd,khd->hqk', grad_part, value_rows, preferred_element_type=...  50.2 us
    all_to_all x1, waiting for transfers between devices, per_device(): lax.all_to_all(head_grads, 'seq', split_axis=0, concat_axis=2, tiled=True)  49.3 us
    convert_element_type x6, other arithmetic, back_block(): grad_scores = (probs * (grad_probs - row_inner)).astype(jnp.bfloat16)  44.8 us
    dot_general x3, matrix products, contract_cols(): lax.dot_general(left, right, (((1,), (1,)), ((), ())), preferred_element_...  44.8 us
  transfers between devices with their start and end apart: 8, of which 7 were waited for; matrix products, arithmetic and copies ran while one was open for 9% of the time, Pallas kernels for 0%

commit v1 on v0

--- a/solution.py
+++ b/solution.py
@@ -2,6 +2,7 @@
 import jax.numpy as jnp
 from jax import lax
 from jax.sharding import PartitionSpec as P
+
 
 H = 16
 
@@ -42,6 +43,11 @@
     return jnp.where(same_doc[None], scores, -1e30)
 
 
+def scatter_sum(values):
+    partial = lax.psum_scatter(values, "fsdp", scatter_dimension=0, tiled=True)
+    return lax.psum_scatter(partial, "seq", scatter_dimension=0, tiled=True)
+
+
 def contract_rows(left, right):
     return lax.dot_general(
         left, right, (((0,), (0,)), ((), ())), preferred_element_type=jnp.float32
@@ -54,7 +60,7 @@
     )
 
 
-def per_device(layer_in, cotangent, doc_ids, valid_len, attn_weights, mlp_weights, param_vector):
+def layer_body(layer_in, cotangent, doc_ids, valid_len, attn_weights, mlp_weights, param_vector):
     seq_count = lax.axis_size("seq")
     seq_index = lax.axis_index("seq")
     tokens, model_width = layer_in.shape
@@ -150,7 +156,7 @@
         grad_upper_low, in_weights, preferred_element_type=jnp.float32
     )
     grad_mlp_full = jnp.concatenate([grad_in, grad_down], axis=0)
-    mlp_shard = None
+    mlp_shard = scatter_sum(grad_mlp_full)
     grad_resid_one, grad_gain_one, grad_shift_one = norm_backward(
         grad_normed, scaled_one, inverse_one, gain_one
     )
@@ -232,9 +238,7 @@
         [grad_qkv_weights.reshape(3 * model_width, model_width), grad_out_weights], axis=0
     )
     attn_shard, mlp_shard, vector_shard = (
-        lax.psum_scatter(grad_attn_full, ("fsdp", "seq"), scatter_dimension=0, tiled=True),
-        lax.psum_scatter(grad_mlp_full, ("fsdp", "seq"), scatter_dimension=0, tiled=True),
-        lax.psum_scatter(grad_vector, ("fsdp", "seq"), scatter_dimension=0, tiled=True),
+        scatter_sum(grad_attn_full), mlp_shard, scatter_sum(grad_vector)
     )
     return (
         layer_values.astype(jnp.bfloat16),
@@ -265,5 +269,5 @@
         P(),
     )
     return jax.shard_map(
-        per_device, mesh=mesh, in_specs=in_specs, out_specs=out_specs, check_vma=False
-    )
+        layer_body, mesh=mesh, in_specs=in_specs, out_specs=out_specs, check_vma=False
+    )

time: 1760 us -> 1300 us (0.74)
  waiting for transfers between devices: 1130 us -> 617 us
  blocking collectives: 115 us -> 162 us
    reduce_scatter x2 -> x4, waiting for transfers between devices: 971 us -> 457 us  [the longest x2 328 us: scatter_sum(): partial = lax.psum_scatter(values, 'fsdp', scatter_dimension=0, tiled=True)]
    psum x0 -> x1, blocking collectives: none -> 41.9 us  [layer_body(): lax.psum((squares, jnp.sum(valid_rows)), ('fsdp', 'seq'))]
    unnamed x1 -> x2, blocking collectives: 44.2 us -> 49.2 us
  transfers between devices with their start and end apart: 8 -> 10, of which waited for: 7 -> 8; matrix products, arithmetic and copies ran while one was open for 9% -> 13% of each run, Pallas kernels for 0% -> 0%
where the time goes in v1:
time: 1300 us; the launch traced here: 1280 us
  waiting for transfers between devices  617 us (47%)
  matrix products  258 us (20%)
  blocking collectives  162 us (12%)
  other arithmetic  113 us (9%)
  local copies, waits for them, and re-layouts  98.6 us (8%)
  between operations  18 us (1%)
  starting transfers between devices  16.8 us (1%)
    reduce_scatter x2, waiting for transfers between devices, scatter_sum(): partial = lax.psum_scatter(values, 'fsdp', scatter_dimension=0, tiled=True)  328 us
    reduce_scatter x2, waiting for transfers between devices, scatter_sum(): return lax.psum_scatter(partial, 'seq', scatter_dimension=0, tiled=True)  128 us
    all_to_all x1, waiting for transfers between devices, layer_body(): lax.all_to_all(qkv_split, 'seq', split_axis=2, concat_axis=0, tiled=True)  77.5 us
    all_gather x1, blocking collectives, layer_body(): lax.all_gather(param_vector, ('fsdp', 'seq'), axis=0, tiled=True)  71.2 us
    dot_general x6, matrix products, back_block(): jnp.einsum('qhd,khd->hqk', grad_part, value_rows, preferred_element_type=...  50.2 us
    all_to_all x1, waiting for transfers between devices, layer_body(): lax.all_to_all(head_grads, 'seq', split_axis=0, concat_axis=2, tiled=True)  49.3 us
    unnamed x2, blocking collectives  49.2 us
    convert_element_type x6, other arithmetic, back_block(): grad_scores = (probs * (grad_probs - row_inner)).astype(jnp.bfloat16)  44.8 us
  transfers between devices with their start and end apart: 10, of which 8 were waited for; matrix products, arithmetic and copies ran while one was open for 13% of the time, Pallas kernels for 0%

profile of v1, /device:TPU:0, one launch (start us, length us, event | category | flops | bytes accessed | tf_op | source)
XLA Modules:
  0.0 1284.6 jit_solution(134698613702304153)
XLA Ops:
  8.6 71.2 %all-gather = bf16[32,1,384]{2,1,0:T(2,128)(2,1)S(1)} all-gather(bf16[1,1,384]{2,1,0:T(2,128)(2,1)S(1)} %reshape.250), channel_id=1, replica_groups=mesh['fsdp'=4,'seq'=8] {'fsdp','seq'}, dimensions={0}, use_global_device_ids=true | all-gather | bytes 25344 | tf_op jit(solution)/shard_map/all_gather | solution.py:73
  80.6 10.3 all-gather.4.cloned.1.call-done
  97.2 3.9 add_convert_fusion
  105.9 4.0 all-to-all-start
  111.9 77.5 %all-to-all-done = bf16[384,3,8,2,64]{0,4,3,1,2:T(8,128)(2,1)S(1)} async-done(((bf16[384,3,8,2,64]{0,4,3,1,2:T(8,128)(2,1)}), bf16[384,3,8,2,64]{0,4,3,1,2:T(8,128)(2,1)S(1)}, u32[]{:S(2)}, u32[]{:S(2)}) %all-to-all-start) | async-done | bytes 2359328 | tf_op jit(solution)/shard_map/all_to_all | solution.py:101
  194.8 75.9 %while.27 = (s32[]{:T(128)}, bf16[6,512,2,64]{1,3,2,0:T(8,128)(2,1)S(1)}, f32[6,2,512]{2,1,0:T(2,128)S(1)}, s32[6,512]{1,0:T(8,128)S(1)}, s32[1,3072]{1,0:T(1,12...) while((s32[]{:T(128)}, ...), condition=%wide.region_3.4_spmd, body=%wide.region_0.3_spmd.sunk | while | flops 844626944 | bytes 49203344 | solution.py:120
  195.7 4.2 fusion.147
  203.5 3.8 fusion.149
  208.3 4.2 fusion.147
  216.2 3.8 fusion.149
  221.0 4.2 fusion.147
  228.9 3.8 fusion.149
  233.7 4.2 fusion.147
  241.5 3.8 fusion.149
  246.3 4.2 fusion.147
  254.2 3.8 fusion.149
  259.0 4.2 fusion.147
  266.8 3.8 fusion.149
  273.7 4.5 all-to-all-start.1
  279.6 18.7 %all-to-all-done.1 = bf16[8,2,24576]{2,1,0:T(2,128)(2,1)S(1)} async-done(((bf16[8,2,24576]{2,1,0:T(2,128)(2,1)}), bf16[8,2,24576]{2,1,0:T(2,128)(2,1)S(1)}, u32[]{:S(2)}, u32[]{:S(2)}) %all-to-all-start.1) | async-done | bytes 786464 | tf_op jit(solution)/shard_map/all_to_all | solution.py:123
  305.6 21.8 %fusion.51 = (bf16[384,4096]{1,0:T(8,128)(2,1)S(1)}, f32[384,4096]{1,0:T(8,128)}) fusion(f32[4096]{0:T(1024)S(1)} %slice.97, bf16[8192,1024]{1,0:T(8,128)(2,1)} %all-gather.6.cloned.1.call-done, f32[384,1024]{1,0:T(8,128)S(1)} %get-tuple-element.322, f32[1024]{0:T(1024)S(1)} %copy-done.35, f32[1024]{0:T(1024)S(1)} %copy-done.23, ...), kind=kOutput, calls=%fused_computation.64 | convolution fusion | flops 3327000576 | bytes 19426304 | tf_op jit(solution)/shard_map/dot_general | solution.py:58
  327.5 4.4 fusion.78
  336.1 9.8 convert_reduce_fusion
  345.9 8.3 multiply_reduce_fusion.1
  360.3 4.2 all-to-all-start.2
  364.5 4.5 copy.106
  369.0 4.9 squeeze.44
  392.4 176.7 %while.28 = (s32[]{:T(128)}, f32[3072,2,64]{0,2,1:T(8,128)S(1)}, f32[3072,2,64]{0,2,1:T(8,128)}, bf16[6,512,2,64]{1,3,2,0:T(8,128)(2,1)}, bf16[6,512,2,64]{1,3,2...) while((s32[]{:T(128)}, f32[3072,2,64]{0,2,1:T(8,128)S(1)}, ...), condition=%wide.region_14.15_spmd.clone, body=%wide.region_12.14_spmd.clone.sunk | while | flops 2064055296 | bytes 122730720 | solution.py:208
  396.4 4.7 fusion.161
  401.2 8.4 multiply_reduce_fusion.7
  409.5 7.5 multiply_convert_fusion.2
  425.8 4.7 fusion.161
  430.6 8.4 multiply_reduce_fusion.7
  438.9 7.5 multiply_convert_fusion.2
  455.2 4.7 fusion.161
  460.0 8.4 multiply_reduce_fusion.7
  468.3 7.5 multiply_convert_fusion.2
  484.6 4.7 fusion.161
  489.4 8.4 multiply_reduce_fusion.7
  497.7 7.5 multiply_convert_fusion.2
  514.0 4.7 fusion.161
  518.8 8.4 multiply_reduce_fusion.7
  527.1 7.5 multiply_convert_fusion.2
  543.4 4.7 fusion.161
  548.2 8.4 multiply_reduce_fusion.7
  556.5 7.5 multiply_convert_fusion.2
  573.6 8.0 copy.119
  581.6 8.0 reshape.270
  593.2 4.6 fusion.96
  597.8 49.3 %all-to-all-done.3 = bf16[8,2,73728]{2,1,0:T(2,128)(2,1)S(1)} async-done(((bf16[8,2,73728]{2,1,0:T(2,128)(2,1)}), bf16[8,2,73728]{2,1,0:T(2,128)(2,1)S(1)}, u32[]{:S(2)}, u32[]{:S(2)}) %all-to-all-start.3) | async-done | bytes 2359328 | tf_op jit(solution)/shard_map/all_to_all | solution.py:215
  647.1 5.3 reshape.271
  652.4 10.2 copy.133
  666.2 7.2 pad_maximum_fusion.1
  674.8 6.5 fusion.99
  681.3 8.5 fusion.102
  689.9 13.7 %pad_maximum_fusion = f32[8192,1024]{1,0:T(8,128)} fusion(f32[4096,1024]{1,0:T(8,128)S(1)} %fusion.99, f32[4096,1024]{1,0:T(8,128)S(1)} %fusion.102), kind=kLoop, calls=%fused_computation.50 | loop fusion | flops 8388608 | bytes 67108864 | tf_op jit(solution)/shard_map/concatenate | solution.py:158
  703.6 93.6 %reduce-scatter.5.cloned.1.call-done = f32[1024,1024]{1,0:T(8,128)} async-done(((f32[4096,1024]{1,0:T(8,128)}), f32[1024,1024]{1,0:T(8,128)}) %reduce-scatter.5.cloned.1.call-update) | async-done | bytes 4194320 | tf_op jit(solution)/shard_map/reduce_scatter | solution.py:47
  797.2 234.7 %reduce-scatter.9.cloned.1.call-done = f32[2048,1024]{1,0:T(8,128)} async-done(((f32[8192,1024]{1,0:T(8,128)}), f32[2048,1024]{1,0:T(8,128)}) %reduce-scatter.9.cloned.1.call-update) | async-done | bytes 8388624 | tf_op jit(solution)/shard_map/reduce_scatter | solution.py:47
  1037.8 41.9 %all-reduce.2 = (f32[4]{0:T(128)S(1)}, f32[]{:T(128)}) all-reduce(f32[4]{0:T(128)S(1)} %pad_maximum_fusion.4, f32[]{:T(128)} %fusion.95), channel_id=1, replica_groups=mesh['fsdp'=4,'seq'=8] {'fsdp','seq'}, use_global_device_ids=true, to_apply=%region_33.34 | all-reduce | flops 5 | bytes 40 | tf_op jit(solution)/shard_map/psum | solution.py:142
  1080.9 8.3 copy.132
  1091.9 11.6 all-reduce
  1103.5 37.6 %all-reduce.1 = f32[3072]{0:T(1024)S(1)} all-reduce(f32[3072]{0:T(1024)S(1)} %dynamic-slice.1), channel_id=7, replica_groups=mesh['fsdp'=4,'seq'=8] {'seq'}, use_global_device_ids=true, to_apply=%region_28.29.clone | all-reduce | flops 3072 | bytes 24576
  1141.8 7.0 bitcast_add_fusion
  1148.8 128.4 %reduce-scatter.11.cloned.1.call-done = f32[256,1024]{1,0:T(8,128)} async-done(((f32[2048,1024]{1,0:T(8,128)}), f32[256,1024]{1,0:T(8,128)}) %reduce-scatter.11.cloned.1.call-update) | async-done | bytes 1048592 | tf_op jit(solution)/shard_map/reduce_scatter | solution.py:48
  (272 shorter events, 161.6 us)
Async XLA Ops:
  7.2 83.8 %all-gather.4.cloned.1.call-start = ((), (), s32[]{:S(2)}) async-start(), calls=%async_computation.8 | async-start | bytes 8650752 | tf_op jit(solution)/shard_map/all_gather | solution.py:71
  80.6 16.6 %copy-start.17 = (bf16[384,1024]{1,0:T(8,128)(2,1)S(1)}, bf16[384,1024]{1,0:T(8,128)(2,1)}, u32[]{:S(2)}) copy-start(bf16[384,1024]{1,0:T(8,128)(2,1)} %param.11) | copy-start | bytes 2359300
  101.1 10.1 copy-start.16
  105.9 83.5 %all-to-all-start = ((bf16[384,3,8,2,64]{0,4,3,1,2:T(8,128)(2,1)}), bf16[384,3,8,2,64]{0,4,3,1,2:T(8,128)(2,1)S(1)}, u32[]{:S(2)}, u32[]{:S(2)}) async-start(bf16[384,3,8,2,64]{0,4,3,1,2:T(8,128)(2,1)} %copy.105), calls=%async_computation | async-start | bytes 4718592 | tf_op jit(solution)/shard_map/all_to_all | solution.py:101
  109.9 195.7 %all-gather.6.cloned.1.call-start = ((), (), s32[]{:S(2)}) async-start(), calls=%async_computation.9 | async-start | bytes 17301504 | tf_op jit(solution)/shard_map/all_gather | solution.py:72
  189.4 5.3 copy-start.1
  199.9 3.7 copy-start.20
  212.5 3.7 copy-start.20
  225.2 3.7 copy-start.20
  237.8 3.7 copy-start.20
  250.5 3.7 copy-start.20
  263.1 3.7 copy-start.20
  270.7 30.8 %copy-start.18 = (bf16[384,1024]{1,0:T(8,128)(2,1)S(1)}, bf16[384,1024]{1,0:T(8,128)(2,1)}, u32[]{:S(2)}) copy-start(bf16[384,1024]{1,0:T(8,128)(2,1)} %param.11) | copy-start | bytes 2359300
  270.7 30.8 %copy-start.38 = (f32[1024]{0:T(1024)S(1)}, f32[1024]{0:T(1024)}, u32[]{:S(2)}) copy-start(f32[1024]{0:T(1024)} %get-tuple-element.343) | copy-start | bytes 12292
  273.7 24.6 %all-to-all-start.1 = ((bf16[8,2,24576]{2,1,0:T(2,128)(2,1)}), bf16[8,2,24576]{2,1,0:T(2,128)(2,1)S(1)}, u32[]{:S(2)}, u32[]{:S(2)}) async-start(bf16[8,2,24576]{2,1,0:T(2,128)(2,1)} %reshape.268), calls=%async_computation.1 | async-start | bytes 1572864 | tf_op jit(solution)/shard_map/all_to_all | solution.py:123
  300.4 5.2 copy-start.23
  300.4 5.2 copy-start.35
  305.2 49.0 %copy-start.4 = (f32[384,1024]{1,0:T(8,128)}, f32[384,1024]{1,0:T(8,128)S(1)}, u32[]{:S(2)}) copy-start(f32[384,1024]{1,0:T(8,128)S(1)} %get-tuple-element.322) | copy-start | bytes 4718596
  305.2 49.0 %copy-start.25 = (f32[384]{0:T(512)}, f32[384]{0:T(512)S(1)}, u32[]{:S(2)}) copy-start(f32[384]{0:T(512)S(1)} %broadcast_multiply_fusion.5) | copy-start | bytes 4612
  305.5 48.7 %copy-start.27 = (f32[384]{0:T(512)}, f32[384]{0:T(512)S(1)}, u32[]{:S(2)}) copy-start(f32[384]{0:T(512)S(1)} %add_rsqrt_fusion.1) | copy-start | bytes 4612
  305.6 21.8 %copy-start.37 = (f32[1024]{0:T(1024)S(1)}, f32[1024]{0:T(1024)}, u32[]{:S(2)}) copy-start(f32[1024]{0:T(1024)} %get-tuple-element.340) | copy-start | bytes 12292
  305.6 21.8 %copy-start.41 = (bf16[8192,1024]{1,0:T(8,128)(2,1)S(1)}, bf16[8192,1024]{1,0:T(8,128)(2,1)}, u32[]{:S(2)}) copy-start(bf16[8192,1024]{1,0:T(8,128)(2,1)} %all-gather.6.cloned.1.call-done) | copy-start | bytes 50331652
  305.6 21.8 %copy-start.44 = (f32[384,1024]{1,0:T(8,128)S(1)}, f32[384,1024]{1,0:T(8,128)}, u32[]{:S(2)}) copy-start(f32[384,1024]{1,0:T(8,128)} %get-tuple-element.346) | copy-start | bytes 4718596
  327.4 4.5 copy-start.9
  327.4 4.7 copy-start.13
  327.4 4.7 copy-start.22
  327.5 6.5 copy-start.33
  336.1 9.8 copy-start.5
  345.9 8.3 copy-start.10
  360.3 24.1 %all-to-all-start.2 = ((bf16[384,1,8,2,64]{0,4,3,1,2:T(8,128)(2,1)}), bf16[384,1,8,2,64]{0,4,3,1,2:T(8,128)(2,1)}, u32[]{:S(2)}, u32[]{:S(2)}) async-start(bf16[384,1,8,2,64]{0,4,3,1,2:T(8,128)(2,1)} %bitcast.24), calls=%async_computation.2 | async-start | bytes 1572864 | tf_op jit(solution)/shard_map/all_to_all | solution.py:168
  393.5 2.9 copy-start.14
  401.2 8.4 copy-start.15
  422.9 2.9 copy-start.14
  430.6 8.4 copy-start.15
  452.3 2.9 copy-start.14
  460.0 8.4 copy-start.15
  481.7 2.9 copy-start.14
  489.4 8.4 copy-start.15
  511.1 2.9 copy-start.14
  518.8 8.4 copy-start.15
  548.2 8.4 copy-start.15
  581.6 11.7 copy-start.12
  589.6 57.5 %all-to-all-start.3 = ((bf16[8,2,73728]{2,1,0:T(2,128)(2,1)}), bf16[8,2,73728]{2,1,0:T(2,128)(2,1)S(1)}, u32[]{:S(2)}, u32[]{:S(2)}) async-start(bf16[8,2,73728]{2,1,0:T(2,128)(2,1)} %reshape.270), calls=%async_computation.3 | async-start | bytes 4718592 | tf_op jit(solution)/shard_map/all_to_all | solution.py:215
  593.2 204.0 %reduce-scatter.5.cloned.1.call-start = ((), (), s32[]{:S(2)}) async-start(), calls=%async_computation.10 | async-start | bytes 20971520 | tf_op jit(solution)/shard_map/reduce_scatter | solution.py:47
  597.8 64.8 %copy-start.19 = (bf16[384,1024]{1,0:T(8,128)(2,1)S(1)}, bf16[384,1024]{1,0:T(8,128)(2,1)}, u32[]{:S(2)}) copy-start(bf16[384,1024]{1,0:T(8,128)(2,1)} %param.11) | copy-start | bytes 2359300
  662.7 3.5 copy-start.2
  662.7 3.5 copy-start
  673.4 7.9 copy-start.24
  673.4 7.9 copy-start.26
  673.4 7.9 copy-start.28
  673.4 7.9 copy-start.36
  673.4 358.5 %reduce-scatter.9.cloned.1.call-start = ((), (), s32[]{:S(2)}) async-start(), calls=%async_computation.12 | async-start | bytes 41943040 | tf_op jit(solution)/shard_map/reduce_scatter | solution.py:47
  703.6 445.2 %reduce-scatter.7.cloned.1.call-start = ((), (), s32[]{:S(2)}) async-start(), calls=%async_computation.11 | async-start | bytes 4718592 | tf_op jit(solution)/shard_map/reduce_scatter | solution.py:48
  797.2 234.9 %copy-start.43 = (u32[32]{0:T(128)S(1)}, u32[32]{0:T(128)}, u32[]{:S(2)}) copy-start(u32[32]{0:T(128)} %constant.139) | copy-start | bytes 388
  797.2 235.5 %copy-start.42 = (u32[32]{0:T(128)S(1)}, u32[32]{0:T(128)}, u32[]{:S(2)}) copy-start(u32[32]{0:T(128)} %constant.135) | copy-start | bytes 388
  797.2 480.0 %reduce-scatter.11.cloned.1.call-start = ((), (), s32[]{:S(2)}) async-start(), calls=%async_computation.13 | async-start | bytes 9437184 | tf_op jit(solution)/shard_map/reduce_scatter | solution.py:48
  1032.0 59.8 %copy-start.31 = (f32[1024]{0:T(1024)S(1)}, f32[1024]{0:T(1024)}, u32[]{:S(2)}) copy-start(f32[1024]{0:T(1024)} %get-tuple-element.317) | copy-start | bytes 12292
  1032.0 59.8 %copy-start.40 = (f32[1024]{0:T(1024)S(1)}, f32[1024]{0:T(1024)}, u32[]{:S(2)}) copy-start(f32[1024]{0:T(1024)} %get-tuple-element.263) | copy-start | bytes 12292
  1032.0 59.8 %copy-start.39 = (f32[1024]{0:T(1024)S(1)}, f32[1024]{0:T(1024)}, u32[]{:S(2)}) copy-start(f32[1024]{0:T(1024)} %get-tuple-element.269) | copy-start | bytes 12292
  1032.0 59.8 %copy-start.34 = (f32[1024]{0:T(1024)S(1)}, f32[1024]{0:T(1024)}, u32[]{:S(2)}) copy-start(f32[1024]{0:T(1024)} %get-tuple-element.315) | copy-start | bytes 12292
  1032.0 59.8 %copy-start.30 = (f32[1024]{0:T(1024)S(1)}, f32[1024]{0:T(1024)}, u32[]{:S(2)}) copy-start(f32[1024]{0:T(1024)} %get-tuple-element.265) | copy-start | bytes 12292
  1032.0 59.8 %copy-start.29 = (f32[1024]{0:T(1024)S(1)}, f32[1024]{0:T(1024)}, u32[]{:S(2)}) copy-start(f32[1024]{0:T(1024)} %get-tuple-element.272) | copy-start | bytes 12292
  1032.0 59.8 %copy-start.32 = (f32[4096]{0:T(1024)S(1)}, f32[4096]{0:T(1024)}, u32[]{:S(2)}) copy-start(f32[4096]{0:T(1024)} %get-tuple-element.350) | copy-start | bytes 49156
  1032.1 109.7 %copy-start.3 = (bf16[8,384,3,1,2,64]{1,5,4,0,2,3:T(8,128)(2,1)S(1)}, bf16[8,384,3,1,2,64]{1,5,4,0,2,3:T(8,128)(2,1)}, u32[]{:S(2)}) copy-start(bf16[8,384,3,1,2,64]{1,5,4,0,2,3:T(8,128)(2,1)} %copy-done.2) | copy-start | bytes 7077892
  (6 other events, 9.7 us)
Sparse Core Ops, SparseCore 0:
  11.0 79.9 all-gather.3
  113.8 142.0 all-gather.5
  673.5 123.6 reduce-scatter.4
  799.6 232.3 reduce-scatter.8
  1036.0 89.8 reduce-scatter.6
  1129.9 147.2 reduce-scatter.10

commit v2 on v1

--- a/solution.py
+++ b/solution.py
@@ -46,6 +46,10 @@
 def scatter_sum(values):
     partial = lax.psum_scatter(values, "fsdp", scatter_dimension=0, tiled=True)
     return lax.psum_scatter(partial, "seq", scatter_dimension=0, tiled=True)
+
+
+def attn_sum(values):
+    return lax.psum_scatter(values, "fsdp", scatter_dimension=0, tiled=True)[0]
 
 
 def contract_rows(left, right):
@@ -84,6 +88,7 @@
     out_weights = attn_full[3 * model_width :]
     in_weights = mlp_full[:hidden]
     down_weights = mlp_full[hidden:]
+    segment_in = lax.all_gather(layer_in, "seq", axis=0, tiled=True)
     segment_doc = doc_ids[0]
     seg_len = segment_doc.shape[0]
     block_rows = min(512, seg_len)
@@ -162,7 +167,17 @@
     )
     grad_branch_low = grad_resid_one.astype(jnp.bfloat16)
     grad_bias_o = jnp.sum(grad_branch_low.astype(jnp.float32), axis=0)
-    grad_out_weights = contract_rows(attn_mixed, grad_branch_low)
+    fsdp_count = lax.axis_size("fsdp")
+    block_height = 4 * model_width // (fsdp_count * seq_count)
+    out_blocks = model_width // (seq_count * block_height)
+    out_rows = lax.psum_scatter(
+        contract_rows(attn_mixed, grad_branch_low).reshape(
+            out_blocks, seq_count, block_height, model_width
+        ),
+        "seq",
+        scatter_dimension=1,
+        tiled=True,
+    )[:, 0]
     grad_mixed_low = contract_cols(grad_branch_low, out_weights).astype(jnp.bfloat16)
     grad_split = grad_mixed_low.reshape(tokens, 1, seq_count, local_heads, head_size)
     grad_heads = lax.all_to_all(grad_split, "seq", split_axis=2, concat_axis=0, tiled=True)
@@ -209,16 +224,23 @@
         back_block, (zeros_head, zeros_head), (query_blocks, grad_blocks, log_blocks, doc_blocks)
     )
     grad_queries = grad_queries.reshape(seg_len, local_heads, head_size)
-    head_grads = jnp.stack([grad_queries, grad_keys, grad_values], axis=1).astype(jnp.bfloat16)[
-        :, :, None
-    ]
+    head_grads = jnp.stack([grad_queries, grad_keys, grad_values], axis=1).astype(jnp.bfloat16)
+    head_weight_grads = jnp.einsum(
+        "td,tihe->dihe", segment_in, head_grads, preferred_element_type=jnp.float32
+    )
+    qkv_blocks = 3 * out_blocks
+    head_width = local_heads * head_size
+    by_row = jnp.transpose(head_weight_grads.reshape(model_width, 3, head_width), (1, 0, 2))
+    row_blocks = lax.all_to_all(
+        by_row.reshape(qkv_blocks, seq_count, block_height, head_width),
+        "seq", split_axis=1, concat_axis=1, tiled=True,
+    )
+    qkv_rows = jnp.transpose(row_blocks, (0, 2, 1, 3)).reshape(qkv_blocks, block_height, model_width)
+    head_grads = head_grads[:, :, None]
     token_grads = lax.all_to_all(head_grads, "seq", split_axis=0, concat_axis=2, tiled=True)
     grad_qkv = token_grads.reshape(tokens, 3, model_width)
     input_grad = grad_resid_one + jnp.einsum(
         "tie,ide->td", grad_qkv, qkv_weights, preferred_element_type=jnp.float32
-    )
-    grad_qkv_weights = jnp.einsum(
-        "td,tie->ide", layer_in, grad_qkv, preferred_element_type=jnp.float32
     )
     grad_bias_qkv = jnp.sum(grad_qkv.astype(jnp.float32), axis=0)
     grad_vector = jnp.concatenate(
@@ -234,11 +256,11 @@
             grad_bias_up,
         ]
     )
-    grad_attn_full = jnp.concatenate(
-        [grad_qkv_weights.reshape(3 * model_width, model_width), grad_out_weights], axis=0
-    )
+    grad_attn_rows = jnp.concatenate([qkv_rows, out_rows], axis=0)
     attn_shard, mlp_shard, vector_shard = (
-        scatter_sum(grad_attn_full), mlp_shard, scatter_sum(grad_vector)
+        attn_sum(grad_attn_rows),
+        mlp_shard,
+        scatter_sum(grad_vector),
     )
     return (
         layer_values.astype(jnp.bfloat16),

time: 1300 us -> 973 us (0.75)
  waiting for transfers between devices: 617 us -> 169 us
  blocking collectives: 162 us -> 269 us
  local copies, waits for them, and re-layouts: 98.6 us -> 114 us
    reduce_scatter x2 -> x1, waiting for transfers between devices: 328 us -> 26.2 us  [scatter_sum(): partial = lax.psum_scatter(values, 'fsdp', scatter_dimension=0, tiled=True)]
    reduce_scatter x2 -> x1, waiting for transfers between devices: 128 us -> 0.01 us  [scatter_sum(): return lax.psum_scatter(partial, 'seq', scatter_dimension=0, tiled=True)]
    psum x1, blocking collectives: 41.9 us -> 110 us  [layer_body(): lax.psum((squares, jnp.sum(valid_rows)), ('fsdp', 'seq'))]
    all_to_all x1, waiting for transfers between devices: 49.3 us -> 0.01 us  [layer_body(): lax.all_to_all(head_grads, 'seq', split_axis=0, concat_axis=2, tiled=True)]
    all_to_all x0 -> x1, blocking collectives: none -> 38.2 us  [layer_body(): lax.all_to_all(by_row.reshape(qkv_blocks, seq_count, block_height, head_w...]
    all_to_all x1, waiting for transfers between devices: 2.67 us -> 22.2 us  [layer_body(): lax.all_to_all(grad_split, 'seq', split_axis=2, concat_axis=0, tiled=True)]
    unnamed x104 -> x89, local copies, waits for them, and re-layouts: 29.9 us -> 32 us
  transfers between devices with their start and end apart: 10 -> 11, of which waited for: 8 -> 5; matrix products, arithmetic and copies ran while one was open for 13% -> 49% of each run, Pallas kernels for 0% -> 0%
where the time goes in v2:
time: 973 us; the launch traced here: 961 us
  blocking collectives  269 us (28%)
  matrix products  256 us (26%)
  waiting for transfers between devices  169 us (17%)
  other arithmetic  115 us (12%)
  local copies, waits for them, and re-layouts  114 us (12%)
  starting transfers between devices  19.3 us (2%)
  between operations  17.8 us (2%)
    psum x1, blocking collectives, layer_body(): lax.psum((squares, jnp.sum(valid_rows)), ('fsdp', 'seq'))  110 us
    all_to_all x1, waiting for transfers between devices, layer_body(): lax.all_to_all(qkv_split, 'seq', split_axis=2, concat_axis=0, tiled=True)  77.5 us
    all_gather x1, blocking collectives, layer_body(): lax.all_gather(param_vector, ('fsdp', 'seq'), axis=0, tiled=True)  71.2 us
    dot_general x6, matrix products, back_block(): jnp.einsum('qhd,khd->hqk', grad_part, value_rows, preferred_element_type=...  51.2 us
    unnamed x2, blocking collectives  50.2 us
    convert_element_type x6, other arithmetic, back_block(): grad_scores = (probs * (grad_probs - row_inner)).astype(jnp.bfloat16)  47.8 us
    dot_general x12, matrix products, attend_block(): jnp.einsum('qhd,khd->hqk', queries, key_rows, preferred_element_type=jnp....  42.2 us
    all_to_all x1, blocking collectives, layer_body(): lax.all_to_all(by_row.reshape(qkv_blocks, seq_count, block_height, head_w...  38.2 us
  transfers between devices with their start and end apart: 11, of which 5 were waited for; matrix products, arithmetic and copies ran while one was open for 49% of the time, Pallas kernels for 0%

profile of v2, /device:TPU:0, one launch (start us, length us, event | category | flops | bytes accessed | tf_op | source)
XLA Modules:
  0.0 961.4 jit_solution(2051825744472724721)
XLA Ops:
  8.6 71.2 %all-gather = bf16[32,1,384]{2,1,0:T(2,128)(2,1)S(1)} all-gather(bf16[1,1,384]{2,1,0:T(2,128)(2,1)S(1)} %reshape.266), channel_id=1, replica_groups=mesh['fsdp'=4,'seq'=8] {'fsdp','seq'}, dimensions={0}, use_global_device_ids=true | all-gather | bytes 25344 | tf_op jit(solution)/shard_map/all_gather | solution.py:77
  80.6 10.4 %all-gather.5.cloned.1.call-done = bf16[4096,1024]{1,0:T(8,128)(2,1)} async-done(((bf16[128,1024]{1,0:T(8,128)(2,1)}), bf16[4096,1024]{1,0:T(8,128)(2,1)}) %all-gather.5.cloned.1.call-update) | async-done | bytes 8388624 | tf_op jit(solution)/shard_map/all_gather | solution.py:75
  97.1 3.9 add_convert_fusion
  105.7 4.0 all-to-all-start
  111.7 77.5 %all-to-all-done = bf16[384,3,8,2,64]{0,4,3,1,2:T(8,128)(2,1)S(1)} async-done(((bf16[384,3,8,2,64]{0,4,3,1,2:T(8,128)(2,1)}), bf16[384,3,8,2,64]{0,4,3,1,2:T(8,128)(2,1)S(1)}, u32[]{:S(2)}, u32[]{:S(2)}) %all-to-all-start) | async-done | bytes 2359328 | tf_op jit(solution)/shard_map/all_to_all | solution.py:106
  193.2 79.3 %while.27 = (s32[]{:T(128)}, bf16[6,512,2,64]{1,3,2,0:T(8,128)(2,1)S(1)}, f32[6,2,512]{2,1,0:T(2,128)}, s32[6,512]{1,0:T(8,128)S(1)}, s32[1,3072]{1,0:T(1,128)S(...) while((s32[]{:T(128)}, ...), condition=%wide.region_3.4_spmd, body=%wide.region_0.3_spmd.sunk | while | flops 844626944 | bytes 49203344 | solution.py:125
  194.2 4.2 fusion.152
  202.0 3.8 fusion.154
  207.4 4.2 fusion.152
  215.2 3.8 fusion.154
  220.6 4.2 fusion.152
  228.5 3.8 fusion.154
  233.9 4.2 fusion.152
  241.7 3.8 fusion.154
  247.1 4.2 fusion.152
  254.9 3.8 fusion.154
  260.3 4.2 fusion.152
  268.1 3.8 fusion.154
  275.6 4.3 all-to-all-start.1
  282.6 30.7 %all-to-all-done.1 = bf16[8,2,24576]{2,1,0:T(2,128)(2,1)S(1)} async-done(((bf16[8,2,24576]{2,1,0:T(2,128)(2,1)}), bf16[8,2,24576]{2,1,0:T(2,128)(2,1)S(1)}, u32[]{:S(2)}, u32[]{:S(2)}) %all-to-all-start.1) | async-done | bytes 786464 | tf_op jit(solution)/shard_map/all_to_all | solution.py:128
  315.6 4.1 fusion.113
  320.0 21.7 %fusion.51 = (bf16[384,4096]{1,0:T(8,128)(2,1)S(1)}, f32[384,4096]{1,0:T(8,128)}) fusion(f32[4096]{0:T(1024)S(1)} %slice.97, bf16[8192,1024]{1,0:T(8,128)(2,1)} %all-gather.7.cloned.1.call-done, f32[384,1024]{1,0:T(8,128)S(1)} %get-tuple-element.340, f32[1024]{0:T(1024)S(1)} %copy-done.28, f32[1024]{0:T(1024)S(1)} %copy-done.21, ...), kind=kOutput, calls=%fused_computation.63 | convolution fusion | flops 3327000576 | bytes 19426304 | tf_op jit(solution)/shard_map/dot_general | solution.py:62
  341.8 4.6 fusion.85
  350.6 8.0 convert_reduce_fusion
  358.6 4.6 multiply_reduce_fusion.1
  369.2 6.5 fusion.105
  375.7 7.2 fusion.108
  382.9 12.7 %pad_maximum_fusion = f32[8192,1024]{1,0:T(8,128)} fusion(f32[4096,1024]{1,0:T(8,128)S(1)} %fusion.105, f32[4096,1024]{1,0:T(8,128)S(1)} %fusion.108), kind=kLoop, calls=%fused_computation.50 | loop fusion | flops 8388608 | bytes 67108864 | tf_op jit(solution)/shard_map/concatenate | solution.py:163
  400.7 4.2 all-to-all-start.2
  405.0 4.6 copy.116
  409.6 4.9 squeeze.50
  422.3 22.2 %all-to-all-done.2 = bf16[384,1,8,2,64]{0,4,3,1,2:T(8,128)(2,1)} async-done(((bf16[384,1,8,2,64]{0,4,3,1,2:T(8,128)(2,1)}), bf16[384,1,8,2,64]{0,4,3,1,2:T(8,128)(2,1)}, u32[]{:S(2)}, u32[]{:S(2)}) %all-to-all-start.2) | async-done | bytes 786464 | tf_op jit(solution)/shard_map/all_to_all | solution.py:183
  452.6 189.3 %while.28 = (s32[]{:T(128)}, f32[3072,2,64]{0,2,1:T(8,128)S(1)}, f32[3072,2,64]{0,2,1:T(8,128)}, bf16[6,512,2,64]{1,3,2,0:T(8,128)(2,1)}, bf16[6,512,2,64]{1,3,2...) while((s32[]{:T(128)}, f32[3072,2,64]{0,2,1:T(8,128)S(1)}, ...), condition=%wide.region_14.15_spmd.clone, body=%wide.region_12.14_spmd.clone.sunk | while | flops 2064055296 | bytes 122730720 | solution.py:223
  458.0 4.7 fusion.166
  462.8 8.4 multiply_reduce_fusion.7
  471.1 7.8 multiply_convert_fusion.2
  489.2 4.7 fusion.166
  493.9 8.4 multiply_reduce_fusion.7
  502.3 9.9 %multiply_convert_fusion.2 = bf16[2,512,3072]{2,1,0:T(8,128)(2,1)S(1)} fusion(f32[2,512,3072]{2,1,0:T(8,128)} %get-tuple-element.498, f32[2,512,3072]{2,1,0:T(8,128)S(1)} %fusion.164, f32[2,512]{1,0:T(2,128)S(1)} %get-tuple-element.499, f32[2,512]{1,0:T(2,128)S(1)} %dynamic-slice_bitcast_fusion.2, pred[512,3072]{1,0:T(8,128)(4,1)S(1)} %broadcast_compare_fusion.5), kind=kLoop, calls=%fused_computation.17.clone.1 | loop fusion | flops 18874368 | bytes 33038336 | tf_op jit(solution)/shard_map/while/body/eval_jaxpr/convert_element_type | solution.py:202
  522.5 4.8 fusion.166
  527.3 9.4 multiply_reduce_fusion.7
  536.7 7.5 multiply_convert_fusion.2
  554.3 4.7 fusion.166
  559.1 8.4 multiply_reduce_fusion.7
  567.5 7.5 multiply_convert_fusion.2
  585.1 4.7 fusion.166
  589.9 8.4 multiply_reduce_fusion.7
  598.2 7.7 multiply_convert_fusion.2
  616.1 4.7 fusion.166
  620.9 8.4 multiply_reduce_fusion.7
  629.2 7.5 multiply_convert_fusion.2
  647.5 7.1 fusion.57
  656.6 38.2 %all_to_all.68 = f32[3,8,128,128]{3,2,0,1:T(8,128)S(1)} all-to-all(f32[3,8,128,128]{3,2,0,1:T(8,128)S(1)} %copy.135), channel_id=1, replica_groups=mesh['fsdp'=4,'seq'=8] {'seq'}, dimensions={1} | all-to-all | bytes 3145728 | tf_op jit(solution)/shard_map/all_to_all | solution.py:234
  700.7 26.2 %reduce-scatter.9.cloned.1.call-done = f32[2048,1024]{1,0:T(8,128)} async-done(((f32[8192,1024]{1,0:T(8,128)}), f32[2048,1024]{1,0:T(8,128)}) %reduce-scatter.9.cloned.1.call-update) | async-done | bytes 8388624 | tf_op jit(solution)/shard_map/reduce_scatter | solution.py:47
  729.5 8.2 copy.129
  737.6 7.9 reshape.287
  745.6 5.5 all-to-all-start.3
  757.0 109.9 %all-reduce.2 = (f32[4]{0:T(128)S(1)}, f32[]{:T(128)}) all-reduce(f32[4]{0:T(128)S(1)} %pad_maximum_fusion.4, f32[]{:T(128)} %fusion.101), channel_id=1, replica_groups=mesh['fsdp'=4,'seq'=8] {'fsdp','seq'}, use_global_device_ids=true, to_apply=%region_33.34 | all-reduce | flops 5 | bytes 40 | tf_op jit(solution)/shard_map/psum | solution.py:147
  868.1 5.3 reshape.288
  873.4 11.8 %copy.146 = bf16[8,384,3,1,2,64]{1,5,4,0,2,3:T(8,128)(2,1)} copy(bf16[8,384,3,1,2,64]{5,4,2,1,0,3:T(2,128)(2,1)} %bitcast.210) | data formatting | bytes 4718592 | tf_op jit(solution)/shard_map/all_to_all | solution.py:240
  885.2 7.3 copy.145
  893.5 12.4 %all-reduce = f32[12288]{0:T(1024)S(1)} all-reduce(f32[12288]{0:T(1024)S(1)} %constant_dynamic-update-slice_fusion), channel_id=6, replica_groups=mesh['fsdp'=4,'seq'=8] {'fsdp'}, use_global_device_ids=true, to_apply=%region_27.28.clone | all-reduce | flops 12288 | bytes 98304
  906.0 37.8 %all-reduce.1 = f32[3072]{0:T(1024)S(1)} all-reduce(f32[3072]{0:T(1024)S(1)} %dynamic-slice.1), channel_id=7, replica_groups=mesh['fsdp'=4,'seq'=8] {'seq'}, use_global_device_ids=true, to_apply=%region_28.29.clone | all-reduce | flops 3072 | bytes 24576
  944.4 7.7 bitcast_add_fusion
  (266 shorter events, 174.5 us)
Async XLA Ops:
  7.2 83.8 %all-gather.5.cloned.1.call-start = ((), (), s32[]{:S(2)}) async-start(), calls=%async_computation.9 | async-start | bytes 8650752 | tf_op jit(solution)/shard_map/all_gather | solution.py:75
  79.8 0.7 copy-start.18
  80.6 16.5 %copy-start.16 = (bf16[384,1024]{1,0:T(8,128)(2,1)S(1)}, bf16[384,1024]{1,0:T(8,128)(2,1)}, u32[]{:S(2)}) copy-start(bf16[384,1024]{1,0:T(8,128)(2,1)} %param.11) | copy-start | bytes 2359300
  94.4 2.7 copy-start.2
  104.0 7.0 copy-start.13
  105.7 83.5 %all-to-all-start = ((bf16[384,3,8,2,64]{0,4,3,1,2:T(8,128)(2,1)}), bf16[384,3,8,2,64]{0,4,3,1,2:T(8,128)(2,1)S(1)}, u32[]{:S(2)}, u32[]{:S(2)}) async-start(bf16[384,3,8,2,64]{0,4,3,1,2:T(8,128)(2,1)} %copy.115), calls=%async_computation | async-start | bytes 4718592 | tf_op jit(solution)/shard_map/all_to_all | solution.py:106
  109.7 210.2 %all-gather.7.cloned.1.call-start = ((), (), s32[]{:S(2)}) async-start(), calls=%async_computation.10 | async-start | bytes 17301504 | tf_op jit(solution)/shard_map/all_gather | solution.py:76
  189.2 1.9 copy-start
  198.4 3.7 copy-start.15
  211.6 3.7 copy-start.15
  224.8 3.7 copy-start.15
  238.0 3.7 copy-start.15
  251.2 3.7 copy-start.15
  264.4 3.7 copy-start.15
  272.6 41.8 %copy-start.19 = (s32[6,512]{1,0:T(8,128)}, s32[6,512]{1,0:T(8,128)S(1)}, u32[]{:S(2)}) copy-start(s32[6,512]{1,0:T(8,128)S(1)} %get-tuple-element.599) | copy-start | bytes 36868
  275.6 39.9 %copy-start.17 = (bf16[384,1024]{1,0:T(8,128)(2,1)S(1)}, bf16[384,1024]{1,0:T(8,128)(2,1)}, u32[]{:S(2)}) copy-start(bf16[384,1024]{1,0:T(8,128)(2,1)} %param.11) | copy-start | bytes 2359300
  275.6 39.9 %copy-start.30 = (f32[1024]{0:T(1024)S(1)}, f32[1024]{0:T(1024)}, u32[]{:S(2)}) copy-start(f32[1024]{0:T(1024)} %get-tuple-element.365) | copy-start | bytes 12292
  275.6 37.7 %all-to-all-start.1 = ((bf16[8,2,24576]{2,1,0:T(2,128)(2,1)}), bf16[8,2,24576]{2,1,0:T(2,128)(2,1)S(1)}, u32[]{:S(2)}, u32[]{:S(2)}) async-start(bf16[8,2,24576]{2,1,0:T(2,128)(2,1)} %reshape.285), calls=%async_computation.1 | async-start | bytes 1572864 | tf_op jit(solution)/shard_map/all_to_all | solution.py:128
  279.9 367.6 %all-gather.9.cloned.1.call-start = ((), (), s32[]{:S(2)}) async-start(), calls=%async_computation.11 | async-start | bytes 7077888 | tf_op jit(solution)/shard_map/all_gather | solution.py:91
  280.7 415.8 %reduce-scatter.5.cloned.1.call-start = ((), (), s32[]{:S(2)}) async-start(), calls=%async_computation.12 | async-start | bytes 4718592 | tf_op jit(solution)/shard_map/reduce_scatter | solution.py:173
  315.5 4.1 copy-start.7
  315.5 4.4 copy-start.21
  315.5 4.4 copy-start.28
  319.6 43.6 %copy-start.1 = (f32[384,1024]{1,0:T(8,128)}, f32[384,1024]{1,0:T(8,128)S(1)}, u32[]{:S(2)}) copy-start(f32[384,1024]{1,0:T(8,128)S(1)} %get-tuple-element.340) | copy-start | bytes 4718596
  320.0 21.7 %copy-start.29 = (f32[1024]{0:T(1024)S(1)}, f32[1024]{0:T(1024)}, u32[]{:S(2)}) copy-start(f32[1024]{0:T(1024)} %get-tuple-element.362) | copy-start | bytes 12292
  320.0 21.7 %copy-start.33 = (bf16[8192,1024]{1,0:T(8,128)(2,1)S(1)}, bf16[8192,1024]{1,0:T(8,128)(2,1)}, u32[]{:S(2)}) copy-start(bf16[8192,1024]{1,0:T(8,128)(2,1)} %all-gather.7.cloned.1.call-done) | copy-start | bytes 50331652
  320.0 21.7 %copy-start.36 = (f32[384,1024]{1,0:T(8,128)S(1)}, f32[384,1024]{1,0:T(8,128)}, u32[]{:S(2)}) copy-start(f32[384,1024]{1,0:T(8,128)} %get-tuple-element.368) | copy-start | bytes 4718596
  341.7 4.7 copy-start.5
  341.7 4.9 copy-start.9
  341.8 4.9 copy-start.20
  341.8 6.7 copy-start.26
  358.6 4.6 copy-start.6
  363.2 2.3 copy-start.8
  364.3 1.1 copy-start.3
  368.7 358.2 %reduce-scatter.9.cloned.1.call-start = ((), (), s32[]{:S(2)}) async-start(), calls=%async_computation.14 | async-start | bytes 41943040 | tf_op jit(solution)/shard_map/reduce_scatter | solution.py:47
  395.6 1.4 copy-start.4
  400.7 43.8 %all-to-all-start.2 = ((bf16[384,1,8,2,64]{0,4,3,1,2:T(8,128)(2,1)}), bf16[384,1,8,2,64]{0,4,3,1,2:T(8,128)(2,1)}, u32[]{:S(2)}, u32[]{:S(2)}) async-start(bf16[384,1,8,2,64]{0,4,3,1,2:T(8,128)(2,1)} %bitcast.24), calls=%async_computation.2 | async-start | bytes 1572864 | tf_op jit(solution)/shard_map/all_to_all | solution.py:183
  405.0 547.2 %reduce-scatter.7.cloned.1.call-start = ((), (), s32[]{:S(2)}) async-start(), calls=%async_computation.13 | async-start | bytes 2621440 | tf_op jit(solution)/shard_map/reduce_scatter | solution.py:52
  420.0 32.7 %copy-start.14 = (s32[1,3072]{1,0:T(1,128)S(1)}, s32[1,3072]{1,0:T(1,128)}, u32[]{:S(2)}) copy-start(s32[1,3072]{1,0:T(1,128)} %param.13) | copy-start | bytes 36868
  455.1 2.9 copy-start.10
  462.8 8.4 copy-start.11
  486.3 2.9 copy-start.10
  493.9 8.4 copy-start.11
  519.6 2.9 copy-start.10
  527.3 9.4 copy-start.11
  551.5 2.9 copy-start.10
  559.1 8.4 copy-start.11
  582.2 2.9 copy-start.10
  589.9 8.4 copy-start.11
  613.2 2.9 copy-start.10
  620.9 8.4 copy-start.11
  644.5 2.0 copy-start.12
  700.6 253.5 %reduce-scatter.11.cloned.1.call-start = ((), (), s32[]{:S(2)}) async-start(), calls=%async_computation.15 | async-start | bytes 9437184 | tf_op jit(solution)/shard_map/reduce_scatter | solution.py:48
  737.6 13.5 %copy-start.35 = (u32[32]{0:T(128)S(1)}, u32[32]{0:T(128)}, u32[]{:S(2)}) copy-start(u32[32]{0:T(128)} %constant.139) | copy-start | bytes 388
  737.6 14.1 %copy-start.34 = (u32[32]{0:T(128)S(1)}, u32[32]{0:T(128)}, u32[]{:S(2)}) copy-start(u32[32]{0:T(128)} %constant.135) | copy-start | bytes 388
  745.6 122.5 %all-to-all-start.3 = ((bf16[8,2,73728]{2,1,0:T(2,128)(2,1)}), bf16[8,2,73728]{2,1,0:T(2,128)(2,1)S(1)}, u32[]{:S(2)}, u32[]{:S(2)}) async-start(bf16[8,2,73728]{2,1,0:T(2,128)(2,1)} %reshape.287), calls=%async_computation.3 | async-start | bytes 4718592 | tf_op jit(solution)/shard_map/all_to_all | solution.py:240
  885.1 8.3 copy-start.24
  885.1 8.3 copy-start.32
  885.1 8.3 copy-start.31
  885.1 8.3 copy-start.27
  885.1 8.3 copy-start.23
  885.2 8.3 copy-start.22
  885.2 8.3 copy-start.25
Sparse Core Ops, SparseCore 0:
  11.0 79.9 all-gather.4
  113.6 142.0 all-gather.6
  282.9 103.1 all-gather.8
  389.6 102.8 reduce-scatter.4
  494.9 231.9 reduce-scatter.8
  729.3 31.1 reduce-scatter.6
  764.7 181.3 reduce-scatter.10

commit v3 on v2

--- a/solution.py
+++ b/solution.py
@@ -131,6 +131,7 @@
     resid_one = layer_in.astype(jnp.float32) + branch
     normed, scaled_one, inverse_one = norm_forward(resid_one, gain_one, shift_one)
     normed_low = normed.astype(jnp.bfloat16)
+    normed_seg = lax.all_gather(normed_low, "seq", axis=0, tiled=True)
     upper = contract_cols(normed_low, in_weights) + bias_up
     active_low = jax.nn.gelu(upper, approximate=False).astype(jnp.bfloat16)
     mlp_branch = jnp.dot(active_low, down_weights, preferred_element_type=jnp.float32) + bias_two
@@ -152,22 +153,41 @@
     )
     grad_mlp_low = grad_resid_two.astype(jnp.bfloat16)
     grad_bias_two = jnp.sum(grad_mlp_low.astype(jnp.float32), axis=0)
-    grad_down = contract_rows(active_low, grad_mlp_low)
     grad_active = contract_cols(grad_mlp_low, down_weights)
     grad_upper_low = (grad_active * gelu_slope(upper)).astype(jnp.bfloat16)
     grad_bias_up = jnp.sum(grad_upper_low.astype(jnp.float32), axis=0)
-    grad_in = contract_rows(grad_upper_low, normed_low)
     grad_normed = grad_resid_two + jnp.dot(
         grad_upper_low, in_weights, preferred_element_type=jnp.float32
     )
-    grad_mlp_full = jnp.concatenate([grad_in, grad_down], axis=0)
-    mlp_shard = scatter_sum(grad_mlp_full)
+    fsdp_count = lax.axis_size("fsdp")
+    mlp_height = 2 * hidden // (fsdp_count * seq_count)
+    mlp_groups = hidden // (seq_count * mlp_height)
+
+    def own_rows(rows):
+        blocks = rows.reshape((mlp_groups, seq_count, mlp_height) + rows.shape[1:])
+        picked = lax.dynamic_index_in_dim(blocks, seq_index, axis=1, keepdims=False)
+        return picked.reshape((mlp_groups * mlp_height,) + rows.shape[1:])
+
+    grad_mlp_seg = lax.all_gather(grad_mlp_low, "seq", axis=0, tiled=True)
+    upper_own = contract_cols(normed_seg, own_rows(in_weights)) + own_rows(bias_up)
+    active_own = jax.nn.gelu(upper_own, approximate=False).astype(jnp.bfloat16)
+    grad_active_own = contract_cols(grad_mlp_seg, own_rows(down_weights))
+    grad_upper_own = (grad_active_own * gelu_slope(upper_own)).astype(jnp.bfloat16)
+    grad_in_own = contract_rows(grad_upper_own, normed_seg)
+    grad_down_own = contract_rows(active_own, grad_mlp_seg)
+    mlp_stack = jnp.concatenate(
+        [
+            grad_in_own.reshape(mlp_groups, mlp_height, model_width),
+            grad_down_own.reshape(mlp_groups, mlp_height, model_width),
+        ],
+        axis=0,
+    )
+    mlp_shard = lax.psum_scatter(mlp_stack, "fsdp", scatter_dimension=0, tiled=True)[0]
     grad_resid_one, grad_gain_one, grad_shift_one = norm_backward(
         grad_normed, scaled_one, inverse_one, gain_one
     )
     grad_branch_low = grad_resid_one.astype(jnp.bfloat16)
     grad_bias_o = jnp.sum(grad_branch_low.astype(jnp.float32), axis=0)
-    fsdp_count = lax.axis_size("fsdp")
     block_height = 4 * model_width // (fsdp_count * seq_count)
     out_blocks = model_width // (seq_count * block_height)
     out_rows = lax.psum_scatter(

time: 973 us -> 963 us (0.990)
  matrix products: 256 us -> 340 us
  blocking collectives: 269 us -> 186 us
    psum x1, blocking collectives: 110 us -> 68.1 us  [layer_body(): lax.psum((squares, jnp.sum(valid_rows)), ('fsdp', 'seq'))]
    all_to_all x1 -> x0, blocking collectives: 38.2 us -> none  [layer_body(): lax.all_to_all(by_row.reshape(qkv_blocks, seq_count, block_height, head_w...]
    reduce_scatter x2 -> x1, waiting for transfers between devices: 26.2 us -> 0.01 us  [layer_body(): lax.psum_scatter(mlp_stack, 'fsdp', scatter_dimension=0, tiled=True)[0]]
    dot_general x3, matrix products: 16.9 us -> 39.7 us  [contract_rows(): lax.dot_general(left, right, (((0,), (0,)), ((), ())), preferred_element_...]
    dot_general x6, matrix products: 16.2 us -> 37.9 us  [back_block(): jnp.einsum('hqk,khd->qhd', grad_scores, key_rows, preferred_element_type=...]
    dot_general x6, matrix products: 13.6 us -> 34.6 us  [back_block(): jnp.einsum('hqk,qhd->khd', grad_scores, query_part, preferred_element_typ...]
    all_to_all x0 -> x1, waiting for transfers between devices: none -> 18.7 us  [layer_body(): lax.all_to_all(by_row.reshape(qkv_blocks, seq_count, block_height, head_w...]
    dot_general x1, matrix products: 4.59 us -> 20.4 us  [layer_body(): jnp.dot(active_low, down_weights, preferred_element_type=jnp.float32)]
  transfers between devices with their start and end apart: 11 -> 13, of which waited for: 5 -> 5; matrix products, arithmetic and copies ran while one was open for 49% -> 58% of each run, Pallas kernels for 0% -> 0%
where the time goes in v3:
time: 963 us; the launch traced here: 951 us
  matrix products  340 us (35%)
  blocking collectives  186 us (19%)
  waiting for transfers between devices  169 us (18%)
  other arithmetic  108 us (11%)
  local copies, waits for them, and re-layouts  105 us (11%)
  starting transfers between devices  23.1 us (2%)
  between operations  17.8 us (2%)
    all_to_all x1, waiting for transfers between devices, layer_body(): lax.all_to_all(qkv_split, 'seq', split_axis=2, concat_axis=0, tiled=True)  78.4 us
    all_gather x1, blocking collectives, layer_body(): lax.all_gather(param_vector, ('fsdp', 'seq'), axis=0, tiled=True)  71.1 us
    psum x1, blocking collectives, layer_body(): lax.psum((squares, jnp.sum(valid_rows)), ('fsdp', 'seq'))  68.1 us
    dot_general x6, matrix products, back_block(): jnp.einsum('qhd,khd->hqk', grad_part, value_rows, preferred_element_type=...  48 us
    unnamed x2, blocking collectives  46.8 us
    convert_element_type x6, other arithmetic, back_block(): grad_scores = (probs * (grad_probs - row_inner)).astype(jnp.bfloat16)  41.7 us
    dot_general x3, matrix products, contract_rows(): lax.dot_general(left, right, (((0,), (0,)), ((), ())), preferred_element_...  39.7 us
    dot_general x6, matrix products, back_block(): jnp.einsum('hqk,qhd->khd', probs.astype(jnp.bfloat16), grad_part, preferr...  38 us
  transfers between devices with their start and end apart: 13, of which 5 were waited for; matrix products, arithmetic and copies ran while one was open for 58% of the time, Pallas kernels for 0%

profile of v3, /device:TPU:0, one launch (start us, length us, event | category | flops | bytes accessed | tf_op | source)
XLA Modules:
  0.0 951.1 jit_solution(9705258071995438147)
XLA Ops:
  9.3 71.1 %all-gather = bf16[32,1,384]{2,1,0:T(2,128)(2,1)S(1)} all-gather(bf16[1,1,384]{2,1,0:T(2,128)(2,1)S(1)} %reshape.303), channel_id=1, replica_groups=mesh['fsdp'=4,'seq'=8] {'fsdp','seq'}, dimensions={0}, use_global_device_ids=true | all-gather | bytes 25344 | tf_op jit(solution)/shard_map/all_gather | solution.py:77
  81.3 9.7 %all-gather.7.cloned.1.call-done = bf16[4096,1024]{1,0:T(8,128)(2,1)} async-done(((bf16[128,1024]{1,0:T(8,128)(2,1)}), bf16[4096,1024]{1,0:T(8,128)(2,1)}) %all-gather.7.cloned.1.call-update) | async-done | bytes 8388624 | tf_op jit(solution)/shard_map/all_gather | solution.py:75
  111.8 78.4 %all-to-all-done = bf16[384,3,8,2,64]{0,4,3,1,2:T(8,128)(2,1)S(1)} async-done(((bf16[384,3,8,2,64]{0,4,3,1,2:T(8,128)(2,1)}), bf16[384,3,8,2,64]{0,4,3,1,2:T(8,128)(2,1)S(1)}, u32[]{:S(2)}, u32[]{:S(2)}) %all-to-all-start) | async-done | bytes 2359328 | tf_op jit(solution)/shard_map/all_to_all | solution.py:106
  195.7 75.9 %while.27 = (s32[]{:T(128)}, bf16[6,512,2,64]{1,3,2,0:T(8,128)(2,1)S(1)}, f32[6,2,512]{2,1,0:T(2,128)S(1)}, s32[6,512]{1,0:T(8,128)S(1)}, s32[1,3072]{1,0:T(1,12...) while((s32[]{:T(128)}, ...), condition=%wide.region_3.4_spmd, body=%wide.region_0.3_spmd.sunk | while | flops 844626944 | bytes 49203844 | solution.py:125
  196.6 4.2 fusion.231
  209.3 4.2 fusion.231
  221.9 4.2 fusion.231
  234.6 4.2 fusion.231
  247.2 4.2 fusion.231
  259.9 4.2 fusion.231
  279.6 33.4 %all-to-all-done.1 = bf16[8,2,24576]{2,1,0:T(2,128)(2,1)S(1)} async-done(((bf16[8,2,24576]{2,1,0:T(2,128)(2,1)}), bf16[8,2,24576]{2,1,0:T(2,128)(2,1)S(1)}, u32[]{:S(2)}, u32[]{:S(2)}) %all-to-all-start.1) | async-done | bytes 786464 | tf_op jit(solution)/shard_map/all_to_all | solution.py:128
  321.8 10.2 %fusion.181 = f32[384,4096]{1,0:T(8,128)} fusion(bf16[384,1024]{1,0:T(8,128)(2,1)} %fusion.103, bf16[8192,1024]{1,0:T(8,128)(2,1)} %all-gather.9.cloned.1.call-done), kind=kOutput, calls=%fused_computation.266 | convolution fusion | flops 3221225472 | bytes 15466496 | tf_op jit(solution)/shard_map/dot_general | solution.py:62
  332.2 20.4 %fusion.94 = (f32[]{:T(128)}, f32[]{:T(128)}, f32[384]{0:T(512)S(1)}, f32[384,1024]{1,0:T(8,128)S(1)}) fusion(f32[384,1024]{1,0:T(8,128)S(1)} %copy-done.38, f32[384]{0:T(512)S(1)} %fusion.107, f32[1024]{0:T(1024)S(1)} %copy-done.32, f32[1024]{0:T(1024)S(1)} %copy-done.26, f32[1024]{0:T(1024)S(1)} %copy-done.23, f32[384]{0:T(512)S(1)} %add_rsqrt_fusion.1, ...), kind=kOutput, calls=%fused_computation.135 | convolution fusion | flops 3330145792 | bytes 19435016 | tf_op jit(solution)/shard_map/dot_general | solution.py:137
  357.0 9.8 %convert_reduce_fusion = (f32[4096]{0:T(1024)}, bf16[384,4096]{1,0:T(8,128)(2,1)S(1)}) fusion(f32[384,4096]{1,0:T(8,128)} %fusion.181, f32[4096]{0:T(1024)S(1)} %slice.108, bf16[384,1024]{1,0:T(8,128)(2,1)} %get-tuple-element.334, bf16[8192,1024]{1,0:T(8,128)(2,1)} %all-gather.9.cloned.1.call-done), kind=kOutput, calls=%fused_computation.72 | convolution fusion | flops 3241668608 | bytes 18644992 | tf_op jit(solution)/shard_map/dot_general | solution.py:62
  366.9 8.3 multiply_reduce_fusion.1
  385.3 4.2 all-to-all-start.2
  399.8 26.6 %all-to-all-done.2 = bf16[384,1,8,2,64]{0,4,3,1,2:T(8,128)(2,1)} async-done(((bf16[384,1,8,2,64]{0,4,3,1,2:T(8,128)(2,1)}), bf16[384,1,8,2,64]{0,4,3,1,2:T(8,128)(2,1)}, u32[]{:S(2)}, u32[]{:S(2)}) %all-to-all-start.2) | async-done | bytes 786464 | tf_op jit(solution)/shard_map/all_to_all | solution.py:203
  430.5 227.4 %while.28 = (s32[]{:T(128)}, f32[3072,2,64]{0,2,1:T(8,128)}, f32[3072,2,64]{0,2,1:T(8,128)}, bf16[6,512,2,64]{1,3,2,0:T(8,128)(2,1)}, bf16[6,512,2,64]{1,3,2,0:T...) while((s32[]{:T(128)}, f32[3072,2,64]{0,2,1:T(8,128)}, ...), condition=%wide.region_14.15_spmd.clone, body=%wide.region_12.14_spmd.clone.sunk | while | flops 2064055296 | bytes 229687664 | solution.py:243
  435.3 8.0 multiply_reduce_fusion.7
  443.3 6.9 multiply_convert_fusion.2
  450.3 5.4 fusion.244
  455.7 6.3 fusion.246
  462.0 5.8 fusion.245
  472.2 8.0 multiply_reduce_fusion.7
  480.2 7.0 multiply_convert_fusion.2
  487.2 6.0 fusion.244
  493.2 6.3 fusion.246
  499.5 6.4 fusion.245
  510.4 8.0 multiply_reduce_fusion.7
  518.4 6.9 multiply_convert_fusion.2
  525.4 5.8 fusion.244
  531.2 6.3 fusion.246
  537.5 6.4 fusion.245
  548.3 8.0 multiply_reduce_fusion.7
  556.3 6.9 multiply_convert_fusion.2
  563.3 5.8 fusion.244
  569.1 6.3 fusion.246
  575.4 6.4 fusion.245
  586.3 8.0 multiply_reduce_fusion.7
  594.2 6.9 multiply_convert_fusion.2
  601.2 5.8 fusion.244
  607.0 6.3 fusion.246
  613.4 6.4 fusion.245
  624.2 8.0 multiply_reduce_fusion.7
  632.2 7.0 multiply_convert_fusion.2
  639.2 5.8 fusion.244
  645.0 6.3 fusion.246
  651.3 6.4 fusion.245
  665.4 6.5 fusion.57
  675.0 7.2 all-to-all-start.4
  682.3 6.8 fusion.186
  691.3 9.2 fusion.189
  700.5 18.7 %all-to-all-done.4 = f32[3,8,128,128]{3,2,0,1:T(8,128)S(1)} async-done(((f32[3,8,128,128]{3,2,0,1:T(8,128)}), f32[3,8,128,128]{3,2,0,1:T(8,128)S(1)}, u32[]{:S(2)}, u32[]{:S(2)}) %all-to-all-start.4) | async-done | bytes 1572896 | tf_op jit(solution)/shard_map/all_to_all | solution.py:254
  725.1 16.5 %fusion.104 = f32[512,1024]{1,0:T(8,128)S(1)} fusion(bf16[3072,1024]{1,0:T(8,128)(2,1)} %all-gather.15.cloned.1.call-done, f32[3072,512]{1,0:T(8,128)} %fusion.189, bf16[3072,1024]{1,0:T(8,128)(2,1)} %all-gather.13.cloned.1.call-done, bf16[512,1024]{1,0:T(8,128)(2,1)} %bitcast.246, f32[512]{0:T(512)S(1)} %bitcast.257), kind=kOutput, calls=%fused_computation.157 | convolution fusion | flops 6459752448 | bytes 22022144 | tf_op jit(solution)/shard_map/dot_general | solution.py:56
  741.6 19.8 %fusion.75 = f32[512,1024]{1,0:T(8,128)S(1)} fusion(bf16[3072,1024]{1,0:T(8,128)(2,1)} %all-gather.13.cloned.1.call-done, f32[3072,512]{1,0:T(8,128)} %fusion.189, f32[512]{0:T(512)S(1)} %bitcast.258), kind=kOutput, calls=%fused_computation.107 | convolution fusion | flops 3325034496 | bytes 14682112 | tf_op jit(solution)/shard_map/dot_general | solution.py:56
  766.5 8.0 copy.129
  774.5 8.1 reshape.324
  791.9 68.1 %all-reduce.2 = (f32[4]{0:T(128)S(1)}, f32[]{:T(128)}) all-reduce(f32[4]{0:T(128)S(1)} %pad_maximum_fusion.4, f32[]{:T(128)} %fusion.108), channel_id=1, replica_groups=mesh['fsdp'=4,'seq'=8] {'fsdp','seq'}, use_global_device_ids=true, to_apply=%region_32.33 | all-reduce | flops 5 | bytes 40 | tf_op jit(solution)/shard_map/psum | solution.py:148
  861.2 5.2 reshape.325
  866.4 7.3 copy.145
  873.8 11.8 %copy.146 = bf16[8,384,3,1,2,64]{1,5,4,0,2,3:T(8,128)(2,1)} copy(bf16[8,384,3,1,2,64]{5,4,2,1,0,3:T(2,128)(2,1)} %bitcast.224) | data formatting | bytes 4718592 | tf_op jit(solution)/shard_map/all_to_all | solution.py:260
  886.6 10.7 %all-reduce = f32[12288]{0:T(1024)S(1)} all-reduce(f32[12288]{0:T(1024)S(1)} %constant_dynamic-update-slice_fusion), channel_id=5, replica_groups=mesh['fsdp'=4,'seq'=8] {'fsdp'}, use_global_device_ids=true, to_apply=%region_26.27.clone | all-reduce | flops 12288 | bytes 98304
  897.3 36.1 %all-reduce.1 = f32[3072]{0:T(1024)S(1)} all-reduce(f32[3072]{0:T(1024)S(1)} %dynamic-slice.1), channel_id=6, replica_groups=mesh['fsdp'=4,'seq'=8] {'seq'}, use_global_device_ids=true, to_apply=%region_27.28.clone | all-reduce | flops 3072 | bytes 24576
  934.0 7.7 bitcast_add_fusion
  (331 shorter events, 187.0 us)
Async XLA Ops:
  7.2 83.8 %all-gather.7.cloned.1.call-start = ((), (), s32[]{:S(2)}) async-start(), calls=%async_computation.8 | async-start | bytes 8650752 | tf_op jit(solution)/shard_map/all_gather | solution.py:75
  7.9 313.9 %all-gather.9.cloned.1.call-start = ((), (), s32[]{:S(2)}) async-start(), calls=%async_computation.9 | async-start | bytes 17301504 | tf_op jit(solution)/shard_map/all_gather | solution.py:76
  81.3 15.8 %copy-start.18 = (bf16[384,1024]{1,0:T(8,128)(2,1)S(1)}, bf16[384,1024]{1,0:T(8,128)(2,1)}, u32[]{:S(2)}) copy-start(bf16[384,1024]{1,0:T(8,128)(2,1)} %param.11) | copy-start | bytes 2359300
  104.0 7.1 copy-start.16
  105.8 84.4 %all-to-all-start = ((bf16[384,3,8,2,64]{0,4,3,1,2:T(8,128)(2,1)}), bf16[384,3,8,2,64]{0,4,3,1,2:T(8,128)(2,1)S(1)}, u32[]{:S(2)}, u32[]{:S(2)}) async-start(bf16[384,3,8,2,64]{0,4,3,1,2:T(8,128)(2,1)} %copy.115), calls=%async_computation | async-start | bytes 4718592 | tf_op jit(solution)/shard_map/all_to_all | solution.py:106
  109.8 555.5 %all-gather.11.cloned.1.call-start = ((), (), s32[]{:S(2)}) async-start(), calls=%async_computation.10 | async-start | bytes 7077888 | tf_op jit(solution)/shard_map/all_gather | solution.py:91
  271.6 44.6 %copy-start.19 = (bf16[384,1024]{1,0:T(8,128)(2,1)S(1)}, bf16[384,1024]{1,0:T(8,128)(2,1)}, u32[]{:S(2)}) copy-start(bf16[384,1024]{1,0:T(8,128)(2,1)} %param.11) | copy-start | bytes 2359300
  271.6 44.6 %copy-start.33 = (f32[1024]{0:T(1024)S(1)}, f32[1024]{0:T(1024)}, u32[]{:S(2)}) copy-start(f32[1024]{0:T(1024)} %get-tuple-element.367) | copy-start | bytes 12292
  274.6 38.4 %all-to-all-start.1 = ((bf16[8,2,24576]{2,1,0:T(2,128)(2,1)}), bf16[8,2,24576]{2,1,0:T(2,128)(2,1)S(1)}, u32[]{:S(2)}, u32[]{:S(2)}) async-start(bf16[8,2,24576]{2,1,0:T(2,128)(2,1)} %reshape.322), calls=%async_computation.1 | async-start | bytes 1572864 | tf_op jit(solution)/shard_map/all_to_all | solution.py:128
  278.2 413.1 %all-gather.15.cloned.1.call-start = ((), (), s32[]{:S(2)}) async-start(), calls=%async_computation.14 | async-start | bytes 7077888 | tf_op jit(solution)/shard_map/all_gather | solution.py:134
  279.0 78.1 %copy-start.21 = (f32[4096]{0:T(1024)}, f32[4096]{0:T(1024)S(1)}, u32[]{:S(2)}) copy-start(f32[4096]{0:T(1024)S(1)} %slice.108) | copy-start | bytes 49156
  321.5 399.3 %reduce-scatter.4.cloned.1.call-start = ((), (), s32[]{:S(2)}) async-start(), calls=%async_computation.11 | async-start | bytes 4718592 | tf_op jit(solution)/shard_map/reduce_scatter | solution.py:193
  321.8 10.2 %copy-start.32 = (f32[1024]{0:T(1024)S(1)}, f32[1024]{0:T(1024)}, u32[]{:S(2)}) copy-start(f32[1024]{0:T(1024)} %get-tuple-element.364) | copy-start | bytes 12292
  321.8 10.2 %copy-start.7 = (bf16[8192,1024]{1,0:T(8,128)(2,1)S(1)}, bf16[8192,1024]{1,0:T(8,128)(2,1)}, u32[]{:S(2)}) copy-start(bf16[8192,1024]{1,0:T(8,128)(2,1)} %all-gather.9.cloned.1.call-done) | copy-start | bytes 50331652
  321.8 10.3 %copy-start.38 = (f32[384,1024]{1,0:T(8,128)S(1)}, f32[384,1024]{1,0:T(8,128)}, u32[]{:S(2)}) copy-start(f32[384,1024]{1,0:T(8,128)} %get-tuple-element.370) | copy-start | bytes 4718596
  332.1 20.7 %copy-start.14 = (bf16[384,1024]{1,0:T(8,128)(2,1)S(1)}, bf16[384,1024]{1,0:T(8,128)(2,1)}, u32[]{:S(2)}) copy-start(bf16[384,1024]{1,0:T(8,128)(2,1)} %param.12) | copy-start | bytes 2359300
  332.1 20.7 %copy-start.24 = (f32[1024]{0:T(1024)S(1)}, f32[1024]{0:T(1024)}, u32[]{:S(2)}) copy-start(f32[1024]{0:T(1024)} %get-tuple-element.362) | copy-start | bytes 12292
  332.1 22.5 %copy-start.25 = (f32[1024]{0:T(1024)S(1)}, f32[1024]{0:T(1024)}, u32[]{:S(2)}) copy-start(f32[1024]{0:T(1024)} %get-tuple-element.363) | copy-start | bytes 12292
  357.0 9.8 %copy-start.15 = (bf16[384,1024]{1,0:T(8,128)(2,1)S(1)}, bf16[384,1024]{1,0:T(8,128)(2,1)}, u32[]{:S(2)}) copy-start(bf16[384,1024]{1,0:T(8,128)(2,1)} %param.12) | copy-start | bytes 2359300
  366.9 10.6 %copy-start.13 = (bf16[384,8,1,2,64]{0,4,3,1,2:T(8,128)(2,1)S(1)}, bf16[384,8,1,2,64]{0,4,3,1,2:T(8,128)(2,1)}, u32[]{:S(2)}) copy-start(bf16[384,8,1,2,64]{0,4,3,1,2:T(8,128)(2,1)} %copy-done.12) | copy-start | bytes 2359300
  380.8 8.7 copy-start.6
  385.3 41.1 %all-to-all-start.2 = ((bf16[384,1,8,2,64]{0,4,3,1,2:T(8,128)(2,1)}), bf16[384,1,8,2,64]{0,4,3,1,2:T(8,128)(2,1)}, u32[]{:S(2)}, u32[]{:S(2)}) async-start(bf16[384,1,8,2,64]{0,4,3,1,2:T(8,128)(2,1)} %bitcast.24), calls=%async_computation.2 | async-start | bytes 1572864 | tf_op jit(solution)/shard_map/all_to_all | solution.py:203
  389.5 335.6 %all-gather.13.cloned.1.call-start = ((), (), s32[]{:S(2)}) async-start(), calls=%async_computation.13 | async-start | bytes 7077888 | tf_op jit(solution)/shard_map/all_gather | solution.py:171
  432.8 10.6 %copy-start = (f32[2,512,3072]{2,1,0:T(8,128)}, f32[2,512,3072]{2,1,0:T(8,128)S(1)}, u32[]{:S(2)}) copy-start(f32[2,512,3072]{2,1,0:T(8,128)S(1)} %fusion.243) | copy-start | bytes 37748740 | tf_op jit(solution)/shard_map/while
  450.3 11.7 %copy-start.1 = (f32[2,512,3072]{2,1,0:T(8,128)S(1)}, f32[2,512,3072]{2,1,0:T(8,128)}, u32[]{:S(2)}) copy-start(f32[2,512,3072]{2,1,0:T(8,128)} %copy-done) | copy-start | bytes 37748740 | tf_op jit(solution)/shard_map/while
  455.7 6.3 copy-start.2
  461.9 5.9 copy-start.11
  469.7 10.5 %copy-start = (f32[2,512,3072]{2,1,0:T(8,128)}, f32[2,512,3072]{2,1,0:T(8,128)S(1)}, u32[]{:S(2)}) copy-start(f32[2,512,3072]{2,1,0:T(8,128)S(1)} %fusion.243) | copy-start | bytes 37748740 | tf_op jit(solution)/shard_map/while
  487.1 6.0 copy-start.4
  487.2 12.4 %copy-start.1 = (f32[2,512,3072]{2,1,0:T(8,128)S(1)}, f32[2,512,3072]{2,1,0:T(8,128)}, u32[]{:S(2)}) copy-start(f32[2,512,3072]{2,1,0:T(8,128)} %copy-done) | copy-start | bytes 37748740 | tf_op jit(solution)/shard_map/while
  493.2 6.3 copy-start.2
  499.5 6.4 copy-start.11
  507.8 10.6 %copy-start = (f32[2,512,3072]{2,1,0:T(8,128)}, f32[2,512,3072]{2,1,0:T(8,128)S(1)}, u32[]{:S(2)}) copy-start(f32[2,512,3072]{2,1,0:T(8,128)S(1)} %fusion.243) | copy-start | bytes 37748740 | tf_op jit(solution)/shard_map/while
  525.4 12.1 %copy-start.1 = (f32[2,512,3072]{2,1,0:T(8,128)S(1)}, f32[2,512,3072]{2,1,0:T(8,128)}, u32[]{:S(2)}) copy-start(f32[2,512,3072]{2,1,0:T(8,128)} %copy-done) | copy-start | bytes 37748740 | tf_op jit(solution)/shard_map/while
  531.1 6.3 copy-start.2
  537.5 6.4 copy-start.11
  545.8 10.6 %copy-start = (f32[2,512,3072]{2,1,0:T(8,128)}, f32[2,512,3072]{2,1,0:T(8,128)S(1)}, u32[]{:S(2)}) copy-start(f32[2,512,3072]{2,1,0:T(8,128)S(1)} %fusion.243) | copy-start | bytes 37748740 | tf_op jit(solution)/shard_map/while
  563.3 5.8 copy-start.4
  563.3 12.1 %copy-start.1 = (f32[2,512,3072]{2,1,0:T(8,128)S(1)}, f32[2,512,3072]{2,1,0:T(8,128)}, u32[]{:S(2)}) copy-start(f32[2,512,3072]{2,1,0:T(8,128)} %copy-done) | copy-start | bytes 37748740 | tf_op jit(solution)/shard_map/while
  569.1 6.3 copy-start.2
  575.4 6.4 copy-start.11
  583.7 10.5 %copy-start = (f32[2,512,3072]{2,1,0:T(8,128)}, f32[2,512,3072]{2,1,0:T(8,128)S(1)}, u32[]{:S(2)}) copy-start(f32[2,512,3072]{2,1,0:T(8,128)S(1)} %fusion.243) | copy-start | bytes 37748740 | tf_op jit(solution)/shard_map/while
  601.2 5.8 copy-start.4
  601.2 12.2 %copy-start.1 = (f32[2,512,3072]{2,1,0:T(8,128)S(1)}, f32[2,512,3072]{2,1,0:T(8,128)}, u32[]{:S(2)}) copy-start(f32[2,512,3072]{2,1,0:T(8,128)} %copy-done) | copy-start | bytes 37748740 | tf_op jit(solution)/shard_map/while
  607.0 6.3 copy-start.2
  613.4 6.4 copy-start.11
  621.7 10.5 %copy-start = (f32[2,512,3072]{2,1,0:T(8,128)}, f32[2,512,3072]{2,1,0:T(8,128)S(1)}, u32[]{:S(2)}) copy-start(f32[2,512,3072]{2,1,0:T(8,128)S(1)} %fusion.243) | copy-start | bytes 37748740 | tf_op jit(solution)/shard_map/while
  639.2 12.1 %copy-start.1 = (f32[2,512,3072]{2,1,0:T(8,128)S(1)}, f32[2,512,3072]{2,1,0:T(8,128)}, u32[]{:S(2)}) copy-start(f32[2,512,3072]{2,1,0:T(8,128)} %copy-done) | copy-start | bytes 37748740 | tf_op jit(solution)/shard_map/while
  645.0 6.3 copy-start.2
  651.3 6.4 copy-start.11
  671.9 10.4 %copy-start.22 = (f32[4096]{0:T(1024)S(1)}, f32[4096]{0:T(1024)}, u32[]{:S(2)}) copy-start(f32[4096]{0:T(1024)} %copy-done.21) | copy-start | bytes 49156
  675.0 44.1 %all-to-all-start.4 = ((f32[3,8,128,128]{3,2,0,1:T(8,128)}), f32[3,8,128,128]{3,2,0,1:T(8,128)S(1)}, u32[]{:S(2)}, u32[]{:S(2)}) async-start(f32[3,8,128,128]{3,2,0,1:T(8,128)} %copy.135), calls=%async_computation.4 | async-start | bytes 3145728 | tf_op jit(solution)/shard_map/all_to_all | solution.py:254
  682.2 259.5 %reduce-scatter.6.cloned.1.call-start = ((), (), s32[]{:S(2)}) async-start(), calls=%async_computation.12 | async-start | bytes 2621440 | tf_op jit(solution)/shard_map/reduce_scatter | solution.py:52
  725.0 218.8 %reduce-scatter.8.cloned.1.call-start = ((), (), s32[]{:S(2)}) async-start(), calls=%async_computation.15 | async-start | bytes 5242880 | tf_op jit(solution)/shard_map/reduce_scatter | solution.py:185
  774.5 11.7 %copy-start.37 = (u32[32]{0:T(128)S(1)}, u32[32]{0:T(128)}, u32[]{:S(2)}) copy-start(u32[32]{0:T(128)} %constant.49) | copy-start | bytes 388
  774.5 12.4 %copy-start.36 = (u32[32]{0:T(128)S(1)}, u32[32]{0:T(128)}, u32[]{:S(2)}) copy-start(u32[32]{0:T(128)} %constant.53) | copy-start | bytes 388
  782.6 78.6 %all-to-all-start.3 = ((bf16[8,2,73728]{2,1,0:T(2,128)(2,1)}), bf16[8,2,73728]{2,1,0:T(2,128)(2,1)S(1)}, u32[]{:S(2)}, u32[]{:S(2)}) async-start(bf16[8,2,73728]{2,1,0:T(2,128)(2,1)} %reshape.324), calls=%async_computation.3 | async-start | bytes 4718592 | tf_op jit(solution)/shard_map/all_to_all | solution.py:260
  873.7 12.7 %copy-start.30 = (f32[1024]{0:T(1024)S(1)}, f32[1024]{0:T(1024)}, u32[]{:S(2)}) copy-start(f32[1024]{0:T(1024)} %get-tuple-element.335) | copy-start | bytes 12292
  873.7 12.7 %copy-start.35 = (f32[1024]{0:T(1024)S(1)}, f32[1024]{0:T(1024)}, u32[]{:S(2)}) copy-start(f32[1024]{0:T(1024)} %get-tuple-element.281) | copy-start | bytes 12292
  873.7 12.7 %copy-start.34 = (f32[1024]{0:T(1024)S(1)}, f32[1024]{0:T(1024)}, u32[]{:S(2)}) copy-start(f32[1024]{0:T(1024)} %get-tuple-element.287) | copy-start | bytes 12292
  873.7 12.8 %copy-start.29 = (f32[1024]{0:T(1024)S(1)}, f32[1024]{0:T(1024)}, u32[]{:S(2)}) copy-start(f32[1024]{0:T(1024)} %get-tuple-element.333) | copy-start | bytes 12292
  873.8 12.8 %copy-start.28 = (f32[1024]{0:T(1024)S(1)}, f32[1024]{0:T(1024)}, u32[]{:S(2)}) copy-start(f32[1024]{0:T(1024)} %get-tuple-element.283) | copy-start | bytes 12292
  873.8 12.8 %copy-start.27 = (f32[1024]{0:T(1024)S(1)}, f32[1024]{0:T(1024)}, u32[]{:S(2)}) copy-start(f32[1024]{0:T(1024)} %get-tuple-element.290) | copy-start | bytes 12292
  873.8 12.8 %copy-start.31 = (f32[4096]{0:T(1024)S(1)}, f32[4096]{0:T(1024)}, u32[]{:S(2)}) copy-start(f32[4096]{0:T(1024)} %get-tuple-element.372) | copy-start | bytes 49156
  (28 other events, 82.3 us)
Sparse Core Ops, SparseCore 0:
  11.0 79.9 all-gather.6
  94.0 151.3 all-gather.8
  247.6 104.3 all-gather.10
  354.0 106.9 all-gather.14
  464.5 86.6 reduce-scatter.3
  553.3 98.3 all-gather.12
  725.1 29.5 reduce-scatter.5
  764.0 42.7 reduce-scatter.7

commit v4 on v3

--- a/solution.py
+++ b/solution.py
@@ -41,11 +41,6 @@
     )
     same_doc = query_doc[:, None] == key_doc[None, :]
     return jnp.where(same_doc[None], scores, -1e30)
-
-
-def scatter_sum(values):
-    partial = lax.psum_scatter(values, "fsdp", scatter_dimension=0, tiled=True)
-    return lax.psum_scatter(partial, "seq", scatter_dimension=0, tiled=True)
 
 
 def attn_sum(values):
@@ -146,7 +141,9 @@
         ]
     )
     square_sums, valid_total = lax.psum((squares, jnp.sum(valid_rows)), ("fsdp", "seq"))
-    rms_values = jnp.sqrt(square_sums / (valid_total * model_width))
+    square_sums, valid_total, cotangent = lax.optimization_barrier(
+        (square_sums, valid_total, cotangent)
+    )
     grad_out = cotangent.astype(jnp.float32)
     grad_resid_two, grad_gain_two, grad_shift_two = norm_backward(
         grad_out, scaled_two, inverse_two, gain_two
@@ -250,23 +247,15 @@
     )
     qkv_blocks = 3 * out_blocks
     head_width = local_heads * head_size
-    by_row = jnp.transpose(head_weight_grads.reshape(model_width, 3, head_width), (1, 0, 2))
-    row_blocks = lax.all_to_all(
-        by_row.reshape(qkv_blocks, seq_count, block_height, head_width),
-        "seq", split_axis=1, concat_axis=1, tiled=True,
-    )
-    qkv_rows = jnp.transpose(row_blocks, (0, 2, 1, 3)).reshape(qkv_blocks, block_height, model_width)
-    head_grads = head_grads[:, :, None]
-    token_grads = lax.all_to_all(head_grads, "seq", split_axis=0, concat_axis=2, tiled=True)
-    grad_qkv = token_grads.reshape(tokens, 3, model_width)
-    input_grad = grad_resid_one + jnp.einsum(
-        "tie,ide->td", grad_qkv, qkv_weights, preferred_element_type=jnp.float32
-    )
-    grad_bias_qkv = jnp.sum(grad_qkv.astype(jnp.float32), axis=0)
+    head_bias_sums = jnp.sum(head_grads.astype(jnp.float32), axis=0).reshape(3, head_width)
+    bias_qv = lax.dynamic_update_slice(
+        jnp.zeros((2, model_width), jnp.float32),
+        head_bias_sums[::2],
+        (0, seq_index * head_width),
+    )
     grad_vector = jnp.concatenate(
         [
-            grad_bias_qkv[0],
-            grad_bias_qkv[2],
+            bias_qv.reshape(-1),
             grad_bias_o,
             grad_gain_one,
             grad_shift_one,
@@ -276,12 +265,34 @@
             grad_bias_up,
         ]
     )
+    slot = grad_vector.shape[0] // (fsdp_count * seq_count)
+    vector_part = jnp.transpose(grad_vector.reshape(fsdp_count, seq_count, slot), (1, 0, 2))
+    by_row = jnp.transpose(head_weight_grads.reshape(model_width, 3, head_width), (1, 0, 2))
+    row_part = jnp.transpose(
+        by_row.reshape(qkv_blocks, seq_count, block_height, head_width), (1, 0, 2, 3)
+    )
+    row_size = qkv_blocks * block_height * head_width
+    exchanged = lax.all_to_all(
+        jnp.concatenate(
+            [row_part.reshape(seq_count, -1), vector_part.reshape(seq_count, -1)], axis=1
+        ),
+        "seq", split_axis=0, concat_axis=0, tiled=True,
+    )
+    row_blocks = exchanged[:, :row_size].reshape(seq_count, qkv_blocks, block_height, head_width)
+    qkv_rows = jnp.transpose(row_blocks, (1, 2, 0, 3)).reshape(qkv_blocks, block_height, model_width)
+    vector_rows = jnp.sum(exchanged[:, row_size:].reshape(seq_count, fsdp_count, slot), axis=0)
+    vector_rows = jnp.pad(vector_rows, ((0, 0), (0, model_width - slot)))[:, None]
+    head_grads = head_grads[:, :, None]
+    token_grads = lax.all_to_all(head_grads, "seq", split_axis=0, concat_axis=2, tiled=True)
+    grad_qkv = token_grads.reshape(tokens, 3, model_width)
+    input_grad = grad_resid_one + jnp.einsum(
+        "tie,ide->td", grad_qkv, qkv_weights, preferred_element_type=jnp.float32
+    )
     grad_attn_rows = jnp.concatenate([qkv_rows, out_rows], axis=0)
-    attn_shard, mlp_shard, vector_shard = (
-        attn_sum(grad_attn_rows),
-        mlp_shard,
-        scatter_sum(grad_vector),
-    )
+    summed = attn_sum(jnp.concatenate([grad_attn_rows, vector_rows], axis=1))
+    attn_shard = summed[:block_height]
+    vector_shard = summed[block_height, :slot]
+    rms_values = jnp.sqrt(square_sums / (valid_total * model_width))
     return (
         layer_values.astype(jnp.bfloat16),
         input_grad,

time: 963 us -> 921 us (0.956)
  blocking collectives: 186 us -> 112 us
  waiting for transfers between devices: 169 us -> 219 us
  matrix products: 340 us -> 320 us
    all_to_all x1, waiting for transfers between devices: 0.01 us -> 52.7 us  [layer_body(): lax.all_to_all(head_grads, 'seq', split_axis=0, concat_axis=2, tiled=True)]
    unnamed x2 -> x0, blocking collectives: 46.8 us -> none
    psum x1, blocking collectives: 68.1 us -> 41.3 us  [layer_body(): lax.psum((squares, jnp.sum(valid_rows)), ('fsdp', 'seq'))]
    dot_general x6, matrix products: 37.9 us -> 16.2 us  [back_block(): jnp.einsum('hqk,khd->qhd', grad_scores, key_rows, preferred_element_type=...]
    while x96 -> x108, local copies, waits for them, and re-layouts: 0.2 us -> 10.5 us
    unnamed x83 -> x77, local copies, waits for them, and re-layouts: 27.7 us -> 24.5 us
  transfers between devices with their start and end apart: 13 -> 13, of which waited for: 5 -> 6; matrix products, arithmetic and copies ran while one was open for 58% -> 58% of each run, Pallas kernels for 0% -> 0%
where the time goes in v4:
time: 921 us; the launch traced here: 911 us
  matrix products  320 us (35%)
  waiting for transfers between devices  219 us (24%)
  other arithmetic  113 us (12%)
  blocking collectives  112 us (12%)
  local copies, waits for them, and re-layouts  107 us (12%)
  starting transfers between devices  21.7 us (2%)
  between operations  16.6 us (2%)
    all_to_all x1, waiting for transfers between devices, layer_body(): lax.all_to_all(qkv_split, 'seq', split_axis=2, concat_axis=0, tiled=True)  78.4 us
    all_gather x1, blocking collectives, layer_body(): lax.all_gather(param_vector, ('fsdp', 'seq'), axis=0, tiled=True)  71.1 us
    all_to_all x1, waiting for transfers between devices, layer_body(): lax.all_to_all(head_grads, 'seq', split_axis=0, concat_axis=2, tiled=True)  52.7 us
    dot_general x6, matrix products, back_block(): jnp.einsum('qhd,khd->hqk', grad_part, value_rows, preferred_element_type=...  47.9 us
    dot_general x6, matrix products, back_block(): jnp.einsum('hqk,qhd->khd', probs.astype(jnp.bfloat16), grad_part, preferr...  42.1 us
    convert_element_type x6, other arithmetic, back_block(): grad_scores = (probs * (grad_probs - row_inner)).astype(jnp.bfloat16)  41.6 us
    psum x1, blocking collectives, layer_body(): lax.psum((squares, jnp.sum(valid_rows)), ('fsdp', 'seq'))  41.3 us
    dot_general x3, matrix products, contract_rows(): lax.dot_general(left, right, (((0,), (0,)), ((), ())), preferred_element_...  39.7 us
  transfers between devices with their start and end apart: 13, of which 6 were waited for; matrix products, arithmetic and copies ran while one was open for 58% of the time, Pallas kernels for 0%

profile of v4, /device:TPU:0, one launch (start us, length us, event | category | flops | bytes accessed | tf_op | source)
XLA Modules:
  0.0 910.9 jit_solution(10722524201809426979)
XLA Ops:
  9.3 71.1 %all-gather = bf16[32,1,384]{2,1,0:T(2,128)(2,1)S(1)} all-gather(bf16[1,1,384]{2,1,0:T(2,128)(2,1)S(1)} %reshape.325), channel_id=1, replica_groups=mesh['fsdp'=4,'seq'=8] {'fsdp','seq'}, dimensions={0}, use_global_device_ids=true | all-gather | bytes 25344 | tf_op jit(solution)/shard_map/all_gather | solution.py:72
  81.3 9.7 %all-gather.7.cloned.1.call-done = bf16[4096,1024]{1,0:T(8,128)(2,1)} async-done(((bf16[128,1024]{1,0:T(8,128)(2,1)}), bf16[4096,1024]{1,0:T(8,128)(2,1)}) %all-gather.7.cloned.1.call-update) | async-done | bytes 8388624 | tf_op jit(solution)/shard_map/all_gather | solution.py:70
  97.0 3.9 add_convert_fusion
  105.8 4.0 all-to-all-start
  111.8 78.4 %all-to-all-done = bf16[384,3,8,2,64]{0,4,3,1,2:T(8,128)(2,1)S(1)} async-done(((bf16[384,3,8,2,64]{0,4,3,1,2:T(8,128)(2,1)}), bf16[384,3,8,2,64]{0,4,3,1,2:T(8,128)(2,1)S(1)}, u32[]{:S(2)}, u32[]{:S(2)}) %all-to-all-start) | async-done | bytes 2359328 | tf_op jit(solution)/shard_map/all_to_all | solution.py:101
  195.7 75.9 %while.27 = (s32[]{:T(128)}, bf16[6,512,2,64]{1,3,2,0:T(8,128)(2,1)S(1)}, f32[6,2,512]{2,1,0:T(2,128)S(1)}, s32[6,512]{1,0:T(8,128)S(1)}, s32[1,3072]{1,0:T(1,12...) while((s32[]{:T(128)}, ...), condition=%wide.region_3.4_spmd, body=%wide.region_0.3_spmd.sunk | while | flops 844626944 | bytes 49203344 | solution.py:120
  196.6 4.2 fusion.225
  204.5 3.8 fusion.227
  209.3 4.2 fusion.225
  217.1 3.8 fusion.227
  221.9 4.2 fusion.225
  229.8 3.8 fusion.227
  234.6 4.2 fusion.225
  242.4 3.8 fusion.227
  247.2 4.2 fusion.225
  255.1 3.8 fusion.227
  259.9 4.2 fusion.225
  267.7 3.8 fusion.227
  279.1 33.8 %all-to-all-done.1 = bf16[8,2,24576]{2,1,0:T(2,128)(2,1)S(1)} async-done(((bf16[8,2,24576]{2,1,0:T(2,128)(2,1)}), bf16[8,2,24576]{2,1,0:T(2,128)(2,1)S(1)}, u32[]{:S(2)}, u32[]{:S(2)}) %all-to-all-start.1) | async-done | bytes 786464 | tf_op jit(solution)/shard_map/all_to_all | solution.py:123
  322.7 9.9 %fusion.176 = f32[384,4096]{1,0:T(8,128)} fusion(bf16[384,1024]{1,0:T(8,128)(2,1)} %fusion.98, bf16[8192,1024]{1,0:T(8,128)(2,1)} %all-gather.9.cloned.1.call-done), kind=kOutput, calls=%fused_computation.268 | convolution fusion | flops 3221225472 | bytes 15466496 | tf_op jit(solution)/shard_map/dot_general | solution.py:57
  332.6 19.5 %fusion.179 = (f32[384]{0:T(512)S(1)}, f32[384,1024]{1,0:T(8,128)S(1)}, f32[384,1024]{1,0:T(8,128)S(1)}) fusion(f32[1024]{0:T(1024)S(1)} %copy-done.26, f32[1024]{0:T(1024)S(1)} %copy-done.27, f32[1024]{0:T(1024)S(1)} %copy-done.23, f32[384]{0:T(512)S(1)} %add_rsqrt_fusion.1, f32[384,1024]{1,0:T(8,128)S(1)} %get-tuple-element.292, ...), kind=kOutput, calls=%fused_computation.270 | convolution fusion | flops 3327786496 | bytes 19432960 | tf_op jit(solution)/shard_map/dot_general | solution.py:132
  356.1 41.3 %all-reduce.1 = (f32[4]{0:T(128)}, f32[]{:T(128)}) all-reduce(f32[4]{0:T(128)S(1)} %pad_maximum_fusion.6, f32[]{:T(128)} %fusion.103), channel_id=1, replica_groups=mesh['fsdp'=4,'seq'=8] {'fsdp','seq'}, use_global_device_ids=true, to_apply=%region_12.13 | all-reduce | flops 5 | bytes 40 | tf_op jit(solution)/shard_map/psum | solution.py:143
  403.5 9.4 %convert_reduce_fusion = (f32[4096]{0:T(1024)}, bf16[384,4096]{1,0:T(8,128)(2,1)S(1)}) fusion(f32[384,4096]{1,0:T(8,128)} %fusion.176, f32[4096]{0:T(1024)S(1)} %slice.122, bf16[384,1024]{1,0:T(8,128)(2,1)} %get-tuple-element.286, bf16[8192,1024]{1,0:T(8,128)(2,1)} %all-gather.9.cloned.1.call-done), kind=kOutput, calls=%fused_computation.85 | convolution fusion | flops 3241668608 | bytes 18644992 | tf_op jit(solution)/shard_map/dot_general | solution.py:57
  412.9 8.1 multiply_reduce_fusion.1
  431.1 5.8 all-to-all-start.2
  447.2 22.0 %all-to-all-done.2 = bf16[384,1,8,2,64]{0,4,3,1,2:T(8,128)(2,1)} async-done(((bf16[384,1,8,2,64]{0,4,3,1,2:T(8,128)(2,1)}), bf16[384,1,8,2,64]{0,4,3,1,2:T(8,128)(2,1)}, u32[]{:S(2)}, u32[]{:S(2)}) %all-to-all-start.2) | async-done | bytes 786464 | tf_op jit(solution)/shard_map/all_to_all | solution.py:200
  473.3 220.7 %while.28 = (s32[]{:T(128)}, f32[3072,2,64]{0,2,1:T(8,128)}, f32[3072,2,64]{0,2,1:T(8,128)}, bf16[6,512,2,64]{1,3,2,0:T(8,128)(2,1)}, bf16[6,512,2,64]{1,3,2,0:T...) while((s32[]{:T(128)}, f32[3072,2,64]{0,2,1:T(8,128)}, ...), condition=%wide.region_21.22_spmd.clone, body=%wide.region_19.21_spmd.clone.sunk | while | flops 2064055296 | bytes 242268560 | solution.py:240
  478.1 8.0 multiply_reduce_fusion.7
  486.1 6.9 multiply_convert_fusion.2
  493.0 5.6 fusion.238
  500.5 6.6 fusion.239
  514.2 8.0 multiply_reduce_fusion.7
  522.2 6.9 multiply_convert_fusion.2
  529.1 5.8 fusion.238
  536.6 7.4 fusion.239
  551.2 8.0 multiply_reduce_fusion.7
  559.2 6.9 multiply_convert_fusion.2
  566.1 6.4 fusion.238
  574.3 7.1 fusion.239
  588.5 8.0 multiply_reduce_fusion.7
  596.5 6.9 multiply_convert_fusion.2
  603.4 5.8 fusion.238
  610.9 7.0 fusion.239
  625.1 8.0 multiply_reduce_fusion.7
  633.1 6.9 multiply_convert_fusion.2
  640.0 5.8 fusion.238
  647.5 7.0 fusion.239
  661.7 8.0 multiply_reduce_fusion.7
  669.7 6.9 multiply_convert_fusion.2
  676.6 5.8 fusion.238
  684.1 7.0 fusion.239
  701.2 6.5 fusion.57
  717.3 6.8 fusion.181
  726.3 9.2 %fusion.183 = f32[3072,512]{1,0:T(8,128)} fusion(bf16[3072,1024]{1,0:T(8,128)(2,1)} %all-gather.15.cloned.1.call-done, bf16[512,1024]{1,0:T(8,128)(2,1)} %bitcast.271), kind=kOutput, calls=%fused_computation.274 | convolution fusion | flops 3221225472 | bytes 13631488 | tf_op jit(solution)/shard_map/dot_general | solution.py:57
  735.5 19.9 %all-to-all-done.4 = f32[8,1,50688]{2,1,0:T(1,128)S(1)} async-done(((f32[8,1,50688]{2,1,0:T(1,128)}), f32[8,1,50688]{2,1,0:T(1,128)S(1)}, u32[]{:S(2)}, u32[]{:S(2)}) %all-to-all-start.4) | async-done | bytes 1622048 | tf_op jit(solution)/shard_map/all_to_all | solution.py:275
  760.8 16.5 %fusion.99 = f32[512,1024]{1,0:T(8,128)S(1)} fusion(bf16[3072,1024]{1,0:T(8,128)(2,1)} %all-gather.15.cloned.1.call-done, f32[3072,512]{1,0:T(8,128)} %fusion.183, bf16[3072,1024]{1,0:T(8,128)(2,1)} %all-gather.13.cloned.1.call-done, bf16[512,1024]{1,0:T(8,128)(2,1)} %bitcast.270, f32[512]{0:T(512)S(1)} %bitcast.283), kind=kOutput, calls=%fused_computation.156 | convolution fusion | flops 6459752448 | bytes 22022144 | tf_op jit(solution)/shard_map/dot_general | solution.py:51
  777.3 19.9 %fusion.75 = f32[512,1024]{1,0:T(8,128)S(1)} fusion(bf16[3072,1024]{1,0:T(8,128)(2,1)} %all-gather.13.cloned.1.call-done, f32[3072,512]{1,0:T(8,128)} %fusion.183, f32[512]{0:T(512)S(1)} %bitcast.284), kind=kOutput, calls=%fused_computation.107 | convolution fusion | flops 3325034496 | bytes 14682112 | tf_op jit(solution)/shard_map/dot_general | solution.py:51
  802.2 8.0 copy.81
  810.2 7.9 reshape.345
  818.1 3.9 all-to-all-start.3
  823.2 52.7 %all-to-all-done.3 = bf16[8,2,73728]{2,1,0:T(2,128)(2,1)S(1)} async-done(((bf16[8,2,73728]{2,1,0:T(2,128)(2,1)}), bf16[8,2,73728]{2,1,0:T(2,128)(2,1)S(1)}, u32[]{:S(2)}, u32[]{:S(2)}) %all-to-all-start.3) | async-done | bytes 2359328 | tf_op jit(solution)/shard_map/all_to_all | solution.py:286
  875.9 5.3 reshape.346
  881.1 11.9 %copy.94 = bf16[8,384,3,1,2,64]{1,5,4,0,2,3:T(8,128)(2,1)} copy(bf16[8,384,3,1,2,64]{5,4,2,1,0,3:T(2,128)(2,1)} %bitcast.246) | data formatting | bytes 4718592 | tf_op jit(solution)/shard_map/all_to_all | solution.py:286
  893.0 7.3 bitcast_add_fusion
  (348 shorter events, 185.2 us)
Async XLA Ops:
  7.2 83.8 %all-gather.7.cloned.1.call-start = ((), (), s32[]{:S(2)}) async-start(), calls=%async_computation.8 | async-start | bytes 8650752 | tf_op jit(solution)/shard_map/all_gather | solution.py:70
  7.9 314.8 %all-gather.9.cloned.1.call-start = ((), (), s32[]{:S(2)}) async-start(), calls=%async_computation.9 | async-start | bytes 17301504 | tf_op jit(solution)/shard_map/all_gather | solution.py:71
  81.3 15.8 %copy-start.18 = (bf16[384,1024]{1,0:T(8,128)(2,1)S(1)}, bf16[384,1024]{1,0:T(8,128)(2,1)}, u32[]{:S(2)}) copy-start(bf16[384,1024]{1,0:T(8,128)(2,1)} %param.11) | copy-start | bytes 2359300
  104.0 7.1 copy-start.16
  105.8 84.4 %all-to-all-start = ((bf16[384,3,8,2,64]{0,4,3,1,2:T(8,128)(2,1)}), bf16[384,3,8,2,64]{0,4,3,1,2:T(8,128)(2,1)S(1)}, u32[]{:S(2)}, u32[]{:S(2)}) async-start(bf16[384,3,8,2,64]{0,4,3,1,2:T(8,128)(2,1)} %copy.67), calls=%async_computation | async-start | bytes 4718592 | tf_op jit(solution)/shard_map/all_to_all | solution.py:101
  109.8 591.4 %all-gather.11.cloned.1.call-start = ((), (), s32[]{:S(2)}) async-start(), calls=%async_computation.10 | async-start | bytes 7077888 | tf_op jit(solution)/shard_map/all_gather | solution.py:86
  271.6 44.5 %copy-start.19 = (bf16[384,1024]{1,0:T(8,128)(2,1)S(1)}, bf16[384,1024]{1,0:T(8,128)(2,1)}, u32[]{:S(2)}) copy-start(bf16[384,1024]{1,0:T(8,128)(2,1)} %param.11) | copy-start | bytes 2359300
  271.6 44.4 %copy-start.33 = (f32[1024]{0:T(1024)S(1)}, f32[1024]{0:T(1024)}, u32[]{:S(2)}) copy-start(f32[1024]{0:T(1024)} %get-tuple-element.315) | copy-start | bytes 12292
  274.6 38.3 %all-to-all-start.1 = ((bf16[8,2,24576]{2,1,0:T(2,128)(2,1)}), bf16[8,2,24576]{2,1,0:T(2,128)(2,1)S(1)}, u32[]{:S(2)}, u32[]{:S(2)}) async-start(bf16[8,2,24576]{2,1,0:T(2,128)(2,1)} %reshape.343), calls=%async_computation.1 | async-start | bytes 1572864 | tf_op jit(solution)/shard_map/all_to_all | solution.py:123
  278.2 448.1 %all-gather.15.cloned.1.call-start = ((), (), s32[]{:S(2)}) async-start(), calls=%async_computation.14 | async-start | bytes 7077888 | tf_op jit(solution)/shard_map/all_gather | solution.py:129
  321.3 435.8 %reduce-scatter.4.cloned.1.call-start = ((), (), s32[]{:S(2)}) async-start(), calls=%async_computation.11 | async-start | bytes 4718592 | tf_op jit(solution)/shard_map/reduce_scatter | solution.py:190
  322.1 81.4 %copy-start.21 = (f32[4096]{0:T(1024)}, f32[4096]{0:T(1024)S(1)}, u32[]{:S(2)}) copy-start(f32[4096]{0:T(1024)S(1)} %slice.122) | copy-start | bytes 49156
  322.7 9.9 %copy-start.26 = (f32[1024]{0:T(1024)S(1)}, f32[1024]{0:T(1024)}, u32[]{:S(2)}) copy-start(f32[1024]{0:T(1024)} %get-tuple-element.312) | copy-start | bytes 12292
  322.7 9.9 %copy-start.6 = (bf16[8192,1024]{1,0:T(8,128)(2,1)S(1)}, bf16[8192,1024]{1,0:T(8,128)(2,1)}, u32[]{:S(2)}) copy-start(bf16[8192,1024]{1,0:T(8,128)(2,1)} %all-gather.9.cloned.1.call-done) | copy-start | bytes 50331652
  332.6 64.8 %copy-start.24 = (f32[1024]{0:T(1024)S(1)}, f32[1024]{0:T(1024)}, u32[]{:S(2)}) copy-start(f32[1024]{0:T(1024)} %get-tuple-element.310) | copy-start | bytes 12292
  332.6 67.3 %copy-start.25 = (f32[1024]{0:T(1024)S(1)}, f32[1024]{0:T(1024)}, u32[]{:S(2)}) copy-start(f32[1024]{0:T(1024)} %get-tuple-element.311) | copy-start | bytes 12292
  403.5 9.4 %copy-start.15 = (bf16[384,1024]{1,0:T(8,128)(2,1)S(1)}, bf16[384,1024]{1,0:T(8,128)(2,1)}, u32[]{:S(2)}) copy-start(bf16[384,1024]{1,0:T(8,128)(2,1)} %param.12) | copy-start | bytes 2359300
  412.9 10.4 %copy-start.13 = (bf16[384,8,1,2,64]{0,4,3,1,2:T(8,128)(2,1)S(1)}, bf16[384,8,1,2,64]{0,4,3,1,2:T(8,128)(2,1)}, u32[]{:S(2)}) copy-start(bf16[384,8,1,2,64]{0,4,3,1,2:T(8,128)(2,1)} %copy-done.12) | copy-start | bytes 2359300
  426.7 10.3 %copy-start.5 = (bf16[384,3,8,2,64]{0,4,3,1,2:T(8,128)(2,1)S(1)}, bf16[384,3,8,2,64]{0,4,3,1,2:T(8,128)(2,1)}, u32[]{:S(2)}) copy-start(bf16[384,3,8,2,64]{0,4,3,1,2:T(8,128)(2,1)} %copy-done.4) | copy-start | bytes 7077892
  431.1 38.0 %all-to-all-start.2 = ((bf16[384,1,8,2,64]{0,4,3,1,2:T(8,128)(2,1)}), bf16[384,1,8,2,64]{0,4,3,1,2:T(8,128)(2,1)}, u32[]{:S(2)}, u32[]{:S(2)}) async-start(bf16[384,1,8,2,64]{0,4,3,1,2:T(8,128)(2,1)} %bitcast.29), calls=%async_computation.2 | async-start | bytes 1572864 | tf_op jit(solution)/shard_map/all_to_all | solution.py:200
  436.9 323.8 %all-gather.13.cloned.1.call-start = ((), (), s32[]{:S(2)}) async-start(), calls=%async_computation.13 | async-start | bytes 7077888 | tf_op jit(solution)/shard_map/all_gather | solution.py:168
  475.5 10.5 %copy-start = (f32[2,512,3072]{2,1,0:T(8,128)}, f32[2,512,3072]{2,1,0:T(8,128)S(1)}, u32[]{:S(2)}) copy-start(f32[2,512,3072]{2,1,0:T(8,128)S(1)} %fusion.237) | copy-start | bytes 37748740 | tf_op jit(solution)/shard_map/while
  493.0 7.5 copy-start.1
  493.0 14.0 %slice-start = ((s8[6291456]{0:T(1024)(128)(4,1)}), s8[4194304]{0:T(1024)(128)(4,1)S(1)}, s32[]{:S(2)}) async-start(s8[6291456]{0:T(1024)(128)(4,1)} %bitcast.242), calls=%async_computation.16 | async-start | bytes 8388608 | tf_op jit(solution)/shard_map/while
  500.5 6.6 copy-start.3
  511.7 10.5 %copy-start = (f32[2,512,3072]{2,1,0:T(8,128)}, f32[2,512,3072]{2,1,0:T(8,128)S(1)}, u32[]{:S(2)}) copy-start(f32[2,512,3072]{2,1,0:T(8,128)S(1)} %fusion.237) | copy-start | bytes 37748740 | tf_op jit(solution)/shard_map/while
  529.1 7.5 copy-start.1
  529.1 14.9 %slice-start = ((s8[6291456]{0:T(1024)(128)(4,1)}), s8[4194304]{0:T(1024)(128)(4,1)S(1)}, s32[]{:S(2)}) async-start(s8[6291456]{0:T(1024)(128)(4,1)} %bitcast.242), calls=%async_computation.16 | async-start | bytes 8388608 | tf_op jit(solution)/shard_map/while
  536.6 7.4 slice-start.1
  536.6 7.4 copy-start.3
  548.6 10.6 %copy-start = (f32[2,512,3072]{2,1,0:T(8,128)}, f32[2,512,3072]{2,1,0:T(8,128)S(1)}, u32[]{:S(2)}) copy-start(f32[2,512,3072]{2,1,0:T(8,128)S(1)} %fusion.237) | copy-start | bytes 37748740 | tf_op jit(solution)/shard_map/while
  566.1 8.1 copy-start.1
  566.1 15.2 %slice-start = ((s8[6291456]{0:T(1024)(128)(4,1)}), s8[4194304]{0:T(1024)(128)(4,1)S(1)}, s32[]{:S(2)}) async-start(s8[6291456]{0:T(1024)(128)(4,1)} %bitcast.242), calls=%async_computation.16 | async-start | bytes 8388608 | tf_op jit(solution)/shard_map/while
  574.3 7.1 slice-start.1
  574.3 7.1 copy-start.3
  585.9 10.6 %copy-start = (f32[2,512,3072]{2,1,0:T(8,128)}, f32[2,512,3072]{2,1,0:T(8,128)S(1)}, u32[]{:S(2)}) copy-start(f32[2,512,3072]{2,1,0:T(8,128)S(1)} %fusion.237) | copy-start | bytes 37748740 | tf_op jit(solution)/shard_map/while
  603.4 7.5 copy-start.1
  603.4 14.5 %slice-start = ((s8[6291456]{0:T(1024)(128)(4,1)}), s8[4194304]{0:T(1024)(128)(4,1)S(1)}, s32[]{:S(2)}) async-start(s8[6291456]{0:T(1024)(128)(4,1)} %bitcast.242), calls=%async_computation.16 | async-start | bytes 8388608 | tf_op jit(solution)/shard_map/while
  610.9 7.1 slice-start.1
  610.9 7.1 copy-start.3
  622.6 10.5 %copy-start = (f32[2,512,3072]{2,1,0:T(8,128)}, f32[2,512,3072]{2,1,0:T(8,128)S(1)}, u32[]{:S(2)}) copy-start(f32[2,512,3072]{2,1,0:T(8,128)S(1)} %fusion.237) | copy-start | bytes 37748740 | tf_op jit(solution)/shard_map/while
  640.0 7.5 copy-start.1
  640.0 14.5 %slice-start = ((s8[6291456]{0:T(1024)(128)(4,1)}), s8[4194304]{0:T(1024)(128)(4,1)S(1)}, s32[]{:S(2)}) async-start(s8[6291456]{0:T(1024)(128)(4,1)} %bitcast.242), calls=%async_computation.16 | async-start | bytes 8388608 | tf_op jit(solution)/shard_map/while
  647.5 7.0 slice-start.1
  647.5 7.0 copy-start.3
  659.1 10.5 %copy-start = (f32[2,512,3072]{2,1,0:T(8,128)}, f32[2,512,3072]{2,1,0:T(8,128)S(1)}, u32[]{:S(2)}) copy-start(f32[2,512,3072]{2,1,0:T(8,128)S(1)} %fusion.237) | copy-start | bytes 37748740 | tf_op jit(solution)/shard_map/while
  676.6 7.5 copy-start.1
  676.6 14.5 %slice-start = ((s8[6291456]{0:T(1024)(128)(4,1)}), s8[4194304]{0:T(1024)(128)(4,1)S(1)}, s32[]{:S(2)}) async-start(s8[6291456]{0:T(1024)(128)(4,1)} %bitcast.242), calls=%async_computation.16 | async-start | bytes 8388608 | tf_op jit(solution)/shard_map/while
  684.1 7.0 slice-start.1
  684.1 7.0 copy-start.3
  694.0 7.1 copy-start.31
  694.0 7.1 copy-start.35
  694.0 7.1 copy-start.34
  694.0 7.1 copy-start.30
  694.0 7.1 copy-start.29
  694.0 7.1 copy-start.28
  694.0 7.1 copy-start.32
  709.8 7.5 copy-start.22
  713.7 41.8 %all-to-all-start.4 = ((f32[8,1,50688]{2,1,0:T(1,128)}), f32[8,1,50688]{2,1,0:T(1,128)S(1)}, u32[]{:S(2)}, u32[]{:S(2)}) async-start(f32[8,1,50688]{2,1,0:T(1,128)} %copy.88), calls=%async_computation.4 | async-start | bytes 3244032 | tf_op jit(solution)/shard_map/all_to_all | solution.py:275
  717.3 183.1 %reduce-scatter.6.cloned.1.call-start = ((), (), s32[]{:S(2)}) async-start(), calls=%async_computation.12 | async-start | bytes 2785280 | tf_op jit(solution)/shard_map/reduce_scatter | solution.py:47
  760.5 143.1 %reduce-scatter.8.cloned.1.call-start = ((), (), s32[]{:S(2)}) async-start(), calls=%async_computation.15 | async-start | bytes 5242880 | tf_op jit(solution)/shard_map/reduce_scatter | solution.py:182
  810.2 12.5 %copy-start.36 = (f32[4]{0:T(128)S(1)}, f32[4]{0:T(128)}, u32[]{:S(2)}) copy-start(f32[4]{0:T(128)} %get-tuple-element.117) | copy-start | bytes 52
  818.1 57.7 %all-to-all-start.3 = ((bf16[8,2,73728]{2,1,0:T(2,128)(2,1)}), bf16[8,2,73728]{2,1,0:T(2,128)(2,1)S(1)}, u32[]{:S(2)}, u32[]{:S(2)}) async-start(bf16[8,2,73728]{2,1,0:T(2,128)(2,1)} %reshape.345), calls=%async_computation.3 | async-start | bytes 4718592 | tf_op jit(solution)/shard_map/all_to_all | solution.py:286
  881.1 11.9 %copy-start.9 = (f32[384,1024]{1,0:T(8,128)S(1)}, f32[384,1024]{1,0:T(8,128)}, u32[]{:S(2)}) copy-start(f32[384,1024]{1,0:T(8,128)} %copy-done.8) | copy-start | bytes 4718596
  (33 other events, 93.0 us)
Sparse Core Ops, SparseCore 0:
  11.0 79.9 all-gather.6
  94.0 151.3 all-gather.8
  247.6 104.2 all-gather.10
  354.0 114.0 all-gather.14
  471.6 86.1 reduce-scatter.3
  559.9 98.3 all-gather.12
  760.6 30.9 reduce-scatter.5
  799.7 43.3 reduce-scatter.7

commit v5 on v4

--- a/solution.py
+++ b/solution.py
@@ -1,10 +1,165 @@
+import functools
 import jax
 import jax.numpy as jnp
 from jax import lax
 from jax.sharding import PartitionSpec as P
 
+from jax.experimental import pallas as pl
+from jax.experimental.pallas import tpu as pltpu
+
 
 H = 16
+
+BLOCK = 256
+NEG = -1e30
+
+
+def key_ranges(segment_doc, block):
+    firsts = segment_doc[::block]
+    lasts = segment_doc[block - 1 :: block]
+    starts = jnp.sum(segment_doc[None, :] < firsts[:, None], axis=1).astype(jnp.int32)
+    ends = jnp.sum(segment_doc[None, :] <= lasts[:, None], axis=1).astype(jnp.int32)
+    return starts // block, (ends + block - 1) // block
+
+
+def _scores(q, k, doc_q, doc_k, scale):
+    s = lax.dot_general(q, k, (((1,), (1,)), ((), ())), preferred_element_type=jnp.float32) * scale
+    return jnp.where(doc_q == doc_k, s, NEG)
+
+
+def _fwd_kernel(lo_ref, hi_ref, q_ref, k_ref, v_ref, dq_ref, dk_ref, out_ref, lse_ref, *, scale, block):
+    i = pl.program_id(1)
+    lo = lo_ref[i]
+    hi = hi_ref[i]
+    q = q_ref[...]
+    doc_q = dq_ref[...]
+
+    def pass_one(kb, carry):
+        m, l = carry
+        start = pl.multiple_of(kb * block, block)
+        s = _scores(q, k_ref[pl.ds(start, block), :], doc_q, dk_ref[:, pl.ds(start, block)], scale)
+        m_new = jnp.maximum(m, jnp.max(s, axis=1, keepdims=True))
+        l = l * jnp.exp(m - m_new) + jnp.sum(jnp.exp(s - m_new), axis=1, keepdims=True)
+        return m_new, l
+
+    rows = q.shape[0]
+    m, l = lax.fori_loop(
+        lo, hi, pass_one,
+        (jnp.full((rows, 1), NEG, jnp.float32), jnp.zeros((rows, 1), jnp.float32)),
+    )
+
+    def pass_two(kb, acc):
+        start = pl.multiple_of(kb * block, block)
+        s = _scores(q, k_ref[pl.ds(start, block), :], doc_q, dk_ref[:, pl.ds(start, block)], scale)
+        p = (jnp.exp(s - m) / l).astype(jnp.bfloat16)
+        return acc + jnp.dot(p, v_ref[pl.ds(start, block), :], preferred_element_type=jnp.float32)
+
+    acc = lax.fori_loop(lo, hi, pass_two, jnp.zeros(out_ref.shape, jnp.float32))
+    out_ref[...] = acc.astype(out_ref.dtype)
+    lse_ref[...] = m + jnp.log(l)
+
+
+def attn_forward(q, k, v, segment_doc, scale, block=BLOCK):
+    heads, seg_len, d = q.shape
+    lo, hi = key_ranges(segment_doc, block)
+    doc_col = segment_doc.reshape(seg_len, 1)
+    doc_row = segment_doc.reshape(1, seg_len)
+    grid = (heads, seg_len // block)
+    spec_q = pl.BlockSpec((None, block, d), lambda h, i, lo, hi: (h, i, 0))
+    spec_kv = pl.BlockSpec((None, seg_len, d), lambda h, i, lo, hi: (h, 0, 0))
+    spec_dq = pl.BlockSpec((block, 1), lambda h, i, lo, hi: (i, 0))
+    spec_dk = pl.BlockSpec((1, seg_len), lambda h, i, lo, hi: (0, 0))
+    spec_lse = pl.BlockSpec((None, block, 1), lambda h, i, lo, hi: (h, i, 0))
+    return pl.pallas_call(
+        functools.partial(_fwd_kernel, scale=scale, block=block),
+        grid_spec=pltpu.PrefetchScalarGridSpec(
+            num_scalar_prefetch=2,
+            grid=grid,
+            in_specs=[spec_q, spec_kv, spec_kv, spec_dq, spec_dk],
+            out_specs=[spec_q, spec_lse],
+        ),
+        out_shape=[
+            jax.ShapeDtypeStruct((heads, seg_len, d), jnp.bfloat16),
+            jax.ShapeDtypeStruct((heads, seg_len, 1), jnp.float32),
+        ],
+        compiler_params=pltpu.CompilerParams(dimension_semantics=("arbitrary", "arbitrary")),
+    )(lo, hi, q, k, v, doc_col, doc_row)
+
+
+def _bwd_kernel(lo_ref, hi_ref, q_ref, k_ref, v_ref, da_ref, lse_ref, dq_ref, dk_ref,
+                gq_ref, gk_ref, gv_ref, *, scale, block):
+    i = pl.program_id(1)
+    lo = lo_ref[i]
+    hi = hi_ref[i]
+
+    @pl.when(i == 0)
+    def _():
+        gk_ref[...] = jnp.zeros(gk_ref.shape, gk_ref.dtype)
+        gv_ref[...] = jnp.zeros(gv_ref.shape, gv_ref.dtype)
+
+    q = q_ref[...]
+    da = da_ref[...]
+    lse = lse_ref[...]
+    doc_q = dq_ref[...]
+
+    def probs(start):
+        s = _scores(q, k_ref[pl.ds(start, block), :], doc_q, dk_ref[:, pl.ds(start, block)], scale)
+        p = jnp.exp(s - lse)
+        dp = lax.dot_general(da, v_ref[pl.ds(start, block), :], (((1,), (1,)), ((), ())),
+                             preferred_element_type=jnp.float32)
+        return p, dp
+
+    def pass_one(kb, delta):
+        start = pl.multiple_of(kb * block, block)
+        p, dp = probs(start)
+        return delta + jnp.sum(dp * p, axis=1, keepdims=True)
+
+    rows = q.shape[0]
+    delta = lax.fori_loop(lo, hi, pass_one, jnp.zeros((rows, 1), jnp.float32))
+
+    def pass_two(kb, gq):
+        start = pl.multiple_of(kb * block, block)
+        p, dp = probs(start)
+        ds = (p * (dp - delta)).astype(jnp.bfloat16)
+        pb = p.astype(jnp.bfloat16)
+        k_blk = k_ref[pl.ds(start, block), :]
+        gq = gq + jnp.dot(ds, k_blk, preferred_element_type=jnp.float32)
+        gk_ref[pl.ds(start, block), :] += lax.dot_general(
+            ds, q, (((0,), (0,)), ((), ())), preferred_element_type=jnp.float32)
+        gv_ref[pl.ds(start, block), :] += lax.dot_general(
+            pb, da, (((0,), (0,)), ((), ())), preferred_element_type=jnp.float32)
+        return gq
+
+    gq = lax.fori_loop(lo, hi, pass_two, jnp.zeros(gq_ref.shape, jnp.float32))
+    gq_ref[...] = gq * scale
+
+    @pl.when(i == pl.num_programs(1) - 1)
+    def _():
+        gk_ref[...] = gk_ref[...] * scale
+
+
+def attn_backward(q, k, v, da, lse, segment_doc, scale, block=BLOCK):
+    heads, seg_len, d = q.shape
+    lo, hi = key_ranges(segment_doc, block)
+    doc_col = segment_doc.reshape(seg_len, 1)
+    doc_row = segment_doc.reshape(1, seg_len)
+    grid = (heads, seg_len // block)
+    spec_q = pl.BlockSpec((None, block, d), lambda h, i, lo, hi: (h, i, 0))
+    spec_kv = pl.BlockSpec((None, seg_len, d), lambda h, i, lo, hi: (h, 0, 0))
+    spec_dq = pl.BlockSpec((block, 1), lambda h, i, lo, hi: (i, 0))
+    spec_dk = pl.BlockSpec((1, seg_len), lambda h, i, lo, hi: (0, 0))
+    spec_lse = pl.BlockSpec((None, block, 1), lambda h, i, lo, hi: (h, i, 0))
+    return pl.pallas_call(
+        functools.partial(_bwd_kernel, scale=scale, block=block),
+        grid_spec=pltpu.PrefetchScalarGridSpec(
+            num_scalar_prefetch=2,
+            grid=grid,
+            in_specs=[spec_q, spec_kv, spec_kv, spec_q, spec_lse, spec_dq, spec_dk],
+            out_specs=[spec_q, spec_kv, spec_kv],
+        ),
+        out_shape=[jax.ShapeDtypeStruct((heads, seg_len, d), jnp.float32)] * 3,
+        compiler_params=pltpu.CompilerParams(dimension_semantics=("arbitrary", "arbitrary")),
+    )(lo, hi, q, k, v, da, lse, doc_col, doc_row)
 
 
 EPSILON = 1e-05
@@ -32,15 +187,6 @@
     return 0.5 * (1.0 + lax.erf(entries * ROOT_HALF)) + entries * INV_ROOT_TWO_PI * jnp.exp(
         -0.5 * entries * entries
     )
-
-
-def attend_block(queries, key_rows, query_doc, key_doc, score_scale):
-    scores = (
-        jnp.einsum("qhd,khd->hqk", queries, key_rows, preferred_element_type=jnp.float32)
-        * score_scale
-    )
-    same_doc = query_doc[:, None] == key_doc[None, :]
-    return jnp.where(same_doc[None], scores, -1e30)
 
 
 def attn_sum(values):
@@ -86,9 +232,6 @@
     segment_in = lax.all_gather(layer_in, "seq", axis=0, tiled=True)
     segment_doc = doc_ids[0]
     seg_len = segment_doc.shape[0]
-    block_rows = min(512, seg_len)
-    block_count = seg_len // block_rows
-    doc_blocks = segment_doc.reshape(block_count, block_rows)
     positions = seq_index * tokens + lax.iota(jnp.int32, tokens)
     valid_rows = (positions < valid_len[0]).astype(jnp.float32)[:, None]
     zero_row = jnp.zeros((1, model_width), jnp.float32)
@@ -103,23 +246,10 @@
     attend_key_rows = head_piece[:, 1, 0]
     attend_value_rows = head_piece[:, 2, 0]
     head_count = queries.shape[1]
-    query_blocks = queries.reshape(block_count, block_rows, head_count, head_size)
-
-    def one_block(block_pair):
-        query_part, doc_part = block_pair
-        scores = attend_block(query_part, attend_key_rows, doc_part, segment_doc, score_scale)
-        top_score = jnp.max(scores, axis=-1, keepdims=True)
-        exponent = jnp.exp(scores - top_score)
-        row_total = jnp.sum(exponent, axis=-1, keepdims=True)
-        weights_low = (exponent / row_total).astype(jnp.bfloat16)
-        mixed_part = jnp.einsum(
-            "hqk,khd->qhd", weights_low, attend_value_rows, preferred_element_type=jnp.float32
-        )
-        return (mixed_part, (top_score + jnp.log(row_total))[..., 0])
-
-    mixed_rows, log_total = lax.map(one_block, (query_blocks, doc_blocks))
-    mixed_rows = mixed_rows.reshape(seg_len, 1, head_count, head_size).astype(jnp.bfloat16)
-    log_total = jnp.transpose(log_total, (0, 2, 1)).reshape(seg_len, 1, head_count)
+    by_head = lambda rows: jnp.transpose(rows, (1, 0, 2))
+    head_q, head_k, head_v = by_head(queries), by_head(attend_key_rows), by_head(attend_value_rows)
+    head_mixed, log_total = attn_forward(head_q, head_k, head_v, segment_doc, score_scale)
+    mixed_rows = jnp.transpose(head_mixed, (1, 0, 2)).reshape(seg_len, 1, head_count, head_size)
     token_mixed = lax.all_to_all(mixed_rows, "seq", split_axis=0, concat_axis=1, tiled=True)
     attn_mixed = token_mixed.reshape(tokens, model_width)
     branch = jnp.dot(attn_mixed, out_weights, preferred_element_type=jnp.float32) + bias_o
@@ -198,50 +328,14 @@
     grad_mixed_low = contract_cols(grad_branch_low, out_weights).astype(jnp.bfloat16)
     grad_split = grad_mixed_low.reshape(tokens, 1, seq_count, local_heads, head_size)
     grad_heads = lax.all_to_all(grad_split, "seq", split_axis=2, concat_axis=0, tiled=True)
-    head_inputs = head_piece[:, :, 0]
-    head_grad = grad_heads[:, 0, 0]
-    queries = head_inputs[:, 0]
-    key_rows = head_inputs[:, 1]
-    value_rows = head_inputs[:, 2]
-    query_blocks = queries.reshape(block_count, block_rows, local_heads, head_size)
-    grad_blocks = head_grad.reshape(block_count, block_rows, local_heads, head_size)
-    log_blocks = log_total.reshape(block_count, block_rows, local_heads)
-
-    def back_block(running, block_inputs):
-        grad_keys, grad_values = running
-        query_part, grad_part, log_part, doc_part = block_inputs
-        scores = attend_block(query_part, key_rows, doc_part, segment_doc, score_scale)
-        probs = jnp.exp(scores - jnp.transpose(log_part)[:, :, None])
-        grad_probs = jnp.einsum(
-            "qhd,khd->hqk", grad_part, value_rows, preferred_element_type=jnp.float32
-        )
-        row_inner = jnp.sum(grad_probs * probs, axis=-1, keepdims=True)
-        grad_scores = (probs * (grad_probs - row_inner)).astype(jnp.bfloat16)
-        grad_query = (
-            jnp.einsum("hqk,khd->qhd", grad_scores, key_rows, preferred_element_type=jnp.float32)
-            * score_scale
-        )
-        grad_keys = (
-            grad_keys
-            + jnp.einsum(
-                "hqk,qhd->khd", grad_scores, query_part, preferred_element_type=jnp.float32
-            )
-            * score_scale
-        )
-        grad_values = grad_values + jnp.einsum(
-            "hqk,qhd->khd",
-            probs.astype(jnp.bfloat16),
-            grad_part,
-            preferred_element_type=jnp.float32,
-        )
-        return ((grad_keys, grad_values), grad_query)
-
-    zeros_head = jnp.zeros((seg_len, local_heads, head_size), jnp.float32)
-    (grad_keys, grad_values), grad_queries = lax.scan(
-        back_block, (zeros_head, zeros_head), (query_blocks, grad_blocks, log_blocks, doc_blocks)
-    )
-    grad_queries = grad_queries.reshape(seg_len, local_heads, head_size)
-    head_grads = jnp.stack([grad_queries, grad_keys, grad_values], axis=1).astype(jnp.bfloat16)
+    head_grad = by_head(grad_heads[:, 0, 0])
+
+    grad_queries, grad_keys, grad_values = attn_backward(
+        head_q, head_k, head_v, head_grad, log_total, segment_doc, score_scale
+    )
+    head_grads = jnp.transpose(
+        jnp.stack([grad_queries, grad_keys, grad_values], axis=0), (2, 0, 1, 3)
+    ).astype(jnp.bfloat16)
     head_weight_grads = jnp.einsum(
         "td,tihe->dihe", segment_in, head_grads, preferred_element_type=jnp.float32
     )

time: 921 us -> 884 us (0.960)
  matrix products: 320 us -> 119 us
  Pallas kernels: 0 us -> 171 us
  other arithmetic: 113 us -> 28.5 us
  waiting for transfers between devices: 219 us -> 274 us
  local copies, waits for them, and re-layouts: 107 us -> 129 us
    dot_general x42 -> x0, matrix products: 200 us -> none  [the longest x6 47.9 us: back_block(): jnp.einsum('qhd,khd->hqk', grad_part, value_rows, preferred_element_type=...]
    pallas_call x0 -> x2, Pallas kernels: none -> 171 us  [the longest x1 92.2 us: attn_backward(): pl.pallas_call(functools.partial(_bwd_kernel, scale=scale, block=block),...]
    broadcast_in_dim x0 -> x1, local copies, waits for them, and re-layouts: none -> 42.4 us  [layer_body(): head_grads = head_grads[:, :, None]]
    convert_element_type x6 -> x0, other arithmetic: 41.6 us -> none  [back_block(): grad_scores = (probs * (grad_probs - row_inner)).astype(jnp.bfloat16)]
    all_to_all x1, waiting for transfers between devices: 19.9 us -> 46.7 us  [layer_body(): lax.all_to_all(jnp.concatenate([row_part.reshape(seq_count, -1), vector_p...]
    reduce_sum x6 -> x1, other arithmetic: 21.9 us -> 0.23 us  [key_ranges(): jnp.sum(segment_doc[None, :] <= lasts[:, None], axis=1).astype(jnp.int32)]
    eq x12 -> x0, other arithmetic: 20.6 us -> none  [attend_block(): same_doc = query_doc[:, None] == key_doc[None, :]]
    all_gather x1, waiting for transfers between devices: 0.02 us -> 17.1 us  [layer_body(): grad_mlp_seg = lax.all_gather(grad_mlp_low, 'seq', axis=0, tiled=True)]
  transfers between devices with their start and end apart: 13 -> 13, of which waited for: 6 -> 7; matrix products, arithmetic and copies ran while one was open for 58% -> 31% of each run, Pallas kernels for 0% -> 19%
where the time goes in v5:
time: 884 us; the launch traced here: 875 us
  waiting for transfers between devices  274 us (31%)
  Pallas kernels  171 us (19%)
  local copies, waits for them, and re-layouts  129 us (15%)
  matrix products  119 us (13%)
  blocking collectives  116 us (13%)
  other arithmetic  28.5 us (3%)
  starting transfers between devices  22.3 us (3%)
  between operations  16.1 us (2%)
    pallas_call x1, Pallas kernels, attn_backward(): pl.pallas_call(functools.partial(_bwd_kernel, scale=scale, block=block),...  92.2 us
    pallas_call x1, Pallas kernels, attn_forward(): pl.pallas_call(functools.partial(_fwd_kernel, scale=scale, block=block),...  78.4 us
    all_to_all x1, waiting for transfers between devices, layer_body(): lax.all_to_all(qkv_split, 'seq', split_axis=2, concat_axis=0, tiled=True)  77.7 us
    all_gather x1, blocking collectives, layer_body(): lax.all_gather(param_vector, ('fsdp', 'seq'), axis=0, tiled=True)  71.1 us
    all_to_all x1, waiting for transfers between devices, layer_body(): lax.all_to_all(head_grads, 'seq', split_axis=0, concat_axis=2, tiled=True)  54.3 us
    all_to_all x1, waiting for transfers between devices, layer_body(): lax.all_to_all(jnp.concatenate([row_part.reshape(seq_count, -1), vector_p...  46.7 us
    psum x1, blocking collectives, layer_body(): lax.psum((squares, jnp.sum(valid_rows)), ('fsdp', 'seq'))  44.8 us
    broadcast_in_dim x1, local copies, waits for them, and re-layouts, layer_body(): head_grads = head_grads[:, :, None]  42.4 us
  transfers between devices with their start and end apart: 13, of which 7 were waited for; matrix products, arithmetic and copies ran while one was open for 31% of the time, Pallas kernels for 19%

profile of v5, /device:TPU:0, one launch (start us, length us, event | category | flops | bytes accessed | tf_op | source)
XLA Modules:
  0.0 875.3 jit_solution(12887094516969747404)
XLA Ops:
  10.1 71.1 %all-gather = bf16[32,1,384]{2,1,0:T(2,128)(2,1)S(1)} all-gather(bf16[1,1,384]{2,1,0:T(2,128)(2,1)S(1)} %reshape.181), channel_id=1, replica_groups=mesh['fsdp'=4,'seq'=8] {'fsdp','seq'}, dimensions={0}, use_global_device_ids=true | all-gather | bytes 25344 | tf_op jit(solution)/shard_map/all_gather | solution.py:218
  81.4 9.5 %all-gather.7.cloned.1.call-done = bf16[4096,1024]{1,0:T(8,128)(2,1)} async-done(((bf16[128,1024]{1,0:T(8,128)(2,1)}), bf16[4096,1024]{1,0:T(8,128)(2,1)}) %all-gather.7.cloned.1.call-update) | async-done | bytes 8388624 | tf_op jit(solution)/shard_map/all_gather | solution.py:216
  90.9 3.5 slice.109
  94.4 2.7 copy-done.2
  97.1 3.9 add_convert_fusion
  101.0 3.0 copy.73
  104.0 1.7 copy.74
  105.7 4.1 all-to-all-start
  110.0 1.7 copy.76.dq_ref
  112.4 77.7 %all-to-all-done = bf16[384,3,8,2,64]{0,4,3,1,2:T(8,128)(2,1)S(1)} async-done(((bf16[384,3,8,2,64]{0,4,3,1,2:T(8,128)(2,1)}), bf16[384,3,8,2,64]{0,4,3,1,2:T(8,128)(2,1)S(1)}, u32[]{:S(2)}, u32[]{:S(2)}) %all-to-all-start) | async-done | bytes 2359328 | tf_op jit(solution)/shard_map/all_to_all | solution.py:244
  190.2 4.0 copy.75
  194.1 5.3 slice_bitcast_fusion
  199.5 78.4 %shard_map.118 = (bf16[2,3072,64]{2,1,0:T(8,128)(2,1)}, f32[2,3072,1]{2,1,0:T(8,128)}) custom-call(s32[12]{0:T(128)} %get-tuple-element.68.lo_ref, s32[12]{0:T(128)} %get-tuple-element.67.hi_ref, bf16[2,3072,64]{2,1,0:T(8,128)(2,1)} %get-tuple-element.52.q_ref, bf16[2,3072,64]{2,1,0:T(8,128)(2,1)} %get-tuple-element.51.k_ref, ...), custom_call_target="tpu_custom_call" | custom-call | tf_op jit(solution)/shard_map/pallas_call | solution.py:73
  277.9 3.9 copy.77
  281.8 1.9 reshape.190
  283.7 3.8 all-to-all-start.1
  288.8 40.3 %all-to-all-done.1 = bf16[8,2,24576]{2,1,0:T(2,128)(2,1)S(1)} async-done(((bf16[8,2,24576]{2,1,0:T(2,128)(2,1)}), bf16[8,2,24576]{2,1,0:T(2,128)(2,1)S(1)}, u32[]{:S(2)}, u32[]{:S(2)}) %all-to-all-start.1) | async-done | bytes 786464 | tf_op jit(solution)/shard_map/all_to_all | solution.py:253
  332.2 2.7 fusion.140
  334.9 1.3 fusion.47
  336.3 1.3 fusion.58
  337.8 9.8 %fusion.136 = f32[384,4096]{1,0:T(8,128)} fusion(bf16[384,1024]{1,0:T(8,128)(2,1)} %fusion.58, bf16[8192,1024]{1,0:T(8,128)(2,1)} %all-gather.9.cloned.1.call-done), kind=kOutput, calls=%fused_computation.226 | convolution fusion | flops 3221225472 | bytes 15466496 | tf_op jit(solution)/shard_map/dot_general | solution.py:203
  347.7 19.2 %fusion.139 = (f32[384]{0:T(512)S(1)}, f32[384,1024]{1,0:T(8,128)S(1)}, f32[384,1024]{1,0:T(8,128)S(1)}) fusion(f32[1024]{0:T(1024)S(1)} %get-tuple-element.56, f32[1024]{0:T(1024)S(1)} %get-tuple-element.57, f32[1024]{0:T(1024)S(1)} %get-tuple-element.58, f32[384]{0:T(512)S(1)} %add_rsqrt_fusion.1, f32[384,1024]{1,0:T(8,128)S(1)} %get-tuple-element.47, ...), kind=kOutput, calls=%fused_computation.228 | convolution fusion | flops 3327786496 | bytes 19432960 | tf_op jit(solution)/shard_map/dot_general | solution.py:262
  366.9 1.4 fusion.49
  368.3 2.6 pad_maximum_fusion.4
  370.9 44.8 %all-reduce.1 = (f32[4]{0:T(128)}, f32[]{:T(128)}) all-reduce(f32[4]{0:T(128)S(1)} %pad_maximum_fusion.4, f32[]{:T(128)} %fusion.63), channel_id=1, replica_groups=mesh['fsdp'=4,'seq'=8] {'fsdp','seq'}, use_global_device_ids=true, to_apply=%region_10.11 | all-reduce | flops 5 | bytes 40 | tf_op jit(solution)/shard_map/psum | solution.py:273
  415.7 1.9 fusion.51
  417.6 3.0 convert_reduce_fusion.3
  420.6 8.8 %convert_reduce_fusion.1 = (f32[4096]{0:T(1024)S(1)}, bf16[384,4096]{1,0:T(8,128)(2,1)S(1)}) fusion(f32[384,4096]{1,0:T(8,128)} %fusion.136, f32[4096]{0:T(1024)S(1)} %slice.120, bf16[384,1024]{1,0:T(8,128)(2,1)} %get-tuple-element.41, bf16[8192,1024]{1,0:T(8,128)(2,1)} %all-gather.9.cloned.1.call-done), kind=kOutput, calls=%fused_computation.36 | convolution fusion | flops 3241668608 | bytes 18644992 | tf_op jit(solution)/shard_map/dot_general | solution.py:203
  429.4 7.5 multiply_reduce_fusion
  437.5 3.4 convolution_bitcast_fusion
  440.9 2.7 fusion.55
  444.7 5.7 all-to-all-start.2
  451.0 25.6 %all-to-all-done.2 = bf16[384,1,8,2,64]{0,4,3,1,2:T(8,128)(2,1)S(1)} async-done(((bf16[384,1,8,2,64]{0,4,3,1,2:T(8,128)(2,1)}), bf16[384,1,8,2,64]{0,4,3,1,2:T(8,128)(2,1)S(1)}, u32[]{:S(2)}, u32[]{:S(2)}) %all-to-all-start.2) | async-done | bytes 786464 | tf_op jit(solution)/shard_map/all_to_all | solution.py:330
  476.6 1.5 copy.82
  478.1 92.2 %shard_map.119 = (f32[2,3072,64]{2,1,0:T(8,128)}, f32[2,3072,64]{2,1,0:T(8,128)}, f32[2,3072,64]{2,1,0:T(8,128)}) custom-call(s32[12]{0:T(128)} %get-tuple-element.68.lo_ref, s32[12]{0:T(128)} %get-tuple-element.67.hi_ref, bf16[2,3072,64]{2,1,0:T(8,128)(2,1)} %get-tuple-element.52.q_ref, bf16[2,3072,64]{2,1,0:T(8,128)(2,1)} %get-tuple-element.51.k_ref, ...), custom_call_target="tpu_custom_call" | custom-call | tf_op jit(solution)/shard_map/pallas_call | solution.py:152
  570.4 2.5 convert_bitcast_fusion
  572.8 2.1 convert_bitcast_fusion.1
  576.3 1.3 convert_reduce_fusion
  577.8 7.1 fusion.16
  584.9 3.0 copy.89
  588.0 1.5 copy.90
  590.5 2.8 copy.91
  593.4 4.3 all-to-all-start.4
  597.7 6.8 fusion.141
  606.7 9.2 %fusion.143 = f32[3072,512]{1,0:T(8,128)} fusion(bf16[3072,1024]{1,0:T(8,128)(2,1)} %all-gather.15.cloned.1.call-done, bf16[512,1024]{1,0:T(8,128)(2,1)} %bitcast.169), kind=kOutput, calls=%fused_computation.233 | convolution fusion | flops 3221225472 | bytes 13631488 | tf_op jit(solution)/shard_map/dot_general | solution.py:203
  615.9 46.7 %all-to-all-done.4 = f32[8,1,50688]{2,1,0:T(1,128)} async-done(((f32[8,1,50688]{2,1,0:T(1,128)}), f32[8,1,50688]{2,1,0:T(1,128)}, u32[]{:S(2)}, u32[]{:S(2)}) %all-to-all-start.4) | async-done | bytes 1622048 | tf_op jit(solution)/shard_map/all_to_all | solution.py:369
  662.6 1.5 copy.105
  664.1 1.2 slice.125
  665.5 2.5 reshape.173
  668.0 3.4 pad_maximum_fusion.2
  671.6 17.1 %all-gather.13.cloned.1.call-done = bf16[3072,1024]{1,0:T(8,128)(2,1)} async-done(((bf16[384,1024]{1,0:T(8,128)(2,1)}), bf16[3072,1024]{1,0:T(8,128)(2,1)}) %all-gather.13.cloned.1.call-update) | async-done | bytes 6291472 | tf_op jit(solution)/shard_map/all_gather | solution.py:298
  688.7 17.0 %fusion.59 = f32[512,1024]{1,0:T(8,128)} fusion(bf16[3072,1024]{1,0:T(8,128)(2,1)} %all-gather.15.cloned.1.call-done, f32[3072,512]{1,0:T(8,128)} %fusion.143, bf16[3072,1024]{1,0:T(8,128)(2,1)} %all-gather.13.cloned.1.call-done, bf16[512,1024]{1,0:T(8,128)(2,1)} %bitcast.168, f32[512]{0:T(512)S(1)} %bitcast.182), kind=kOutput, calls=%fused_computation.112 | convolution fusion | flops 6459752448 | bytes 22022144 | tf_op jit(solution)/shard_map/dot_general | solution.py:197
  705.7 20.6 %fusion.35 = f32[512,1024]{1,0:T(8,128)S(1)} fusion(bf16[3072,1024]{1,0:T(8,128)(2,1)} %all-gather.13.cloned.1.call-done, f32[3072,512]{1,0:T(8,128)} %fusion.143, f32[512]{0:T(512)S(1)} %bitcast.183), kind=kOutput, calls=%fused_computation.59 | convolution fusion | flops 3325034496 | bytes 14682112 | tf_op jit(solution)/shard_map/dot_general | solution.py:197
  726.3 2.5 pad_maximum_fusion.1
  728.9 2.3 fusion.131
  731.2 42.4 %copy.107 = bf16[3072,3,1,2,64]{4,3,1,2,0:T(2,128)(2,1)} copy(bf16[3072,3,1,2,64]{4,0,3,1,2:T(8,128)(2,1)S(1)} %fusion.131) | data formatting | bytes 4718592 | tf_op jit(solution)/shard_map/broadcast_in_dim | solution.py:379
  773.6 8.0 reshape.192
  781.6 3.6 all-to-all-start.3
  786.4 54.3 %all-to-all-done.3 = bf16[8,2,73728]{2,1,0:T(2,128)(2,1)S(1)} async-done(((bf16[8,2,73728]{2,1,0:T(2,128)(2,1)}), bf16[8,2,73728]{2,1,0:T(2,128)(2,1)S(1)}, u32[]{:S(2)}, u32[]{:S(2)}) %all-to-all-start.3) | async-done | bytes 2359328 | tf_op jit(solution)/shard_map/all_to_all | solution.py:380
  840.7 5.3 reshape.193
  845.9 11.9 %copy.97 = bf16[8,384,3,1,2,64]{1,5,4,0,2,3:T(8,128)(2,1)} copy(bf16[8,384,3,1,2,64]{5,4,2,1,0,3:T(2,128)(2,1)} %bitcast.144) | data formatting | bytes 4718592 | tf_op jit(solution)/shard_map/all_to_all | solution.py:380
  857.8 7.3 bitcast_add_fusion
  865.1 1.3 slice_reduce_fusion.1
  866.4 1.9 slice_bitcast_fusion.3
  (97 shorter events, 15.9 us)
Async XLA Ops:
  7.2 83.7 %all-gather.7.cloned.1.call-start = ((), (), s32[]{:S(2)}) async-start(), calls=%async_computation.8 | async-start | bytes 8650752 | tf_op jit(solution)/shard_map/all_gather | solution.py:216
  7.9 329.9 %all-gather.9.cloned.1.call-start = ((), (), s32[]{:S(2)}) async-start(), calls=%async_computation.9 | async-start | bytes 17301504 | tf_op jit(solution)/shard_map/all_gather | solution.py:217
  8.6 569.2 %all-gather.11.cloned.1.call-start = ((), (), s32[]{:S(2)}) async-start(), calls=%async_computation.10 | async-start | bytes 7077888 | tf_op jit(solution)/shard_map/all_gather | solution.py:232
  81.4 15.7 %copy-start.10 = (bf16[384,1024]{1,0:T(8,128)(2,1)S(1)}, bf16[384,1024]{1,0:T(8,128)(2,1)}, u32[]{:S(2)}) copy-start(bf16[384,1024]{1,0:T(8,128)(2,1)} %param.7) | copy-start | bytes 2359300
  94.4 2.7 copy-start.2
  101.0 8.8 %copy-start.11 = (s32[1,3072]{1,0:T(1,128)S(1)}, s32[1,3072]{1,0:T(1,128)}, u32[]{:S(2)}) copy-start(s32[1,3072]{1,0:T(1,128)} %dk_ref.3) | copy-start | bytes 36868
  105.7 84.5 %all-to-all-start = ((bf16[384,3,8,2,64]{0,4,3,1,2:T(8,128)(2,1)}), bf16[384,3,8,2,64]{0,4,3,1,2:T(8,128)(2,1)S(1)}, u32[]{:S(2)}, u32[]{:S(2)}) async-start(bf16[384,3,8,2,64]{0,4,3,1,2:T(8,128)(2,1)} %copy.74), calls=%async_computation | async-start | bytes 4718592 | tf_op jit(solution)/shard_map/all_to_all | solution.py:244
  283.7 45.4 %all-to-all-start.1 = ((bf16[8,2,24576]{2,1,0:T(2,128)(2,1)}), bf16[8,2,24576]{2,1,0:T(2,128)(2,1)S(1)}, u32[]{:S(2)}, u32[]{:S(2)}) async-start(bf16[8,2,24576]{2,1,0:T(2,128)(2,1)} %reshape.190), calls=%async_computation.1 | async-start | bytes 1572864 | tf_op jit(solution)/shard_map/all_to_all | solution.py:253
  287.4 319.2 %all-gather.15.cloned.1.call-start = ((), (), s32[]{:S(2)}) async-start(), calls=%async_computation.14 | async-start | bytes 7077888 | tf_op jit(solution)/shard_map/all_gather | solution.py:259
  331.3 0.9 copy-start.5
  337.6 330.5 %reduce-scatter.4.cloned.1.call-start = ((), (), s32[]{:S(2)}) async-start(), calls=%async_computation.11 | async-start | bytes 4718592 | tf_op jit(solution)/shard_map/reduce_scatter | solution.py:320
  337.8 9.9 %copy-start = (bf16[8192,1024]{1,0:T(8,128)(2,1)S(1)}, bf16[8192,1024]{1,0:T(8,128)(2,1)}, u32[]{:S(2)}) copy-start(bf16[8192,1024]{1,0:T(8,128)(2,1)} %all-gather.9.cloned.1.call-done) | copy-start | bytes 50331652
  420.6 8.8 %copy-start.8 = (bf16[384,1024]{1,0:T(8,128)(2,1)S(1)}, bf16[384,1024]{1,0:T(8,128)(2,1)}, u32[]{:S(2)}) copy-start(bf16[384,1024]{1,0:T(8,128)(2,1)} %param.8) | copy-start | bytes 2359300
  429.4 8.1 copy-start.6
  437.5 6.1 copy-start.3
  444.7 31.9 %all-to-all-start.2 = ((bf16[384,1,8,2,64]{0,4,3,1,2:T(8,128)(2,1)}), bf16[384,1,8,2,64]{0,4,3,1,2:T(8,128)(2,1)S(1)}, u32[]{:S(2)}, u32[]{:S(2)}) async-start(bf16[384,1,8,2,64]{0,4,3,1,2:T(8,128)(2,1)} %bitcast.31), calls=%async_computation.2 | async-start | bytes 1572864 | tf_op jit(solution)/shard_map/all_to_all | solution.py:330
  450.4 238.3 %all-gather.13.cloned.1.call-start = ((), (), s32[]{:S(2)}) async-start(), calls=%async_computation.13 | async-start | bytes 7077888 | tf_op jit(solution)/shard_map/all_gather | solution.py:298
  570.4 4.6 copy-start.7
  575.2 1.1 copy-start.1
  593.4 69.2 %all-to-all-start.4 = ((f32[8,1,50688]{2,1,0:T(1,128)}), f32[8,1,50688]{2,1,0:T(1,128)}, u32[]{:S(2)}, u32[]{:S(2)}) async-start(f32[8,1,50688]{2,1,0:T(1,128)} %copy.91), calls=%async_computation.4 | async-start | bytes 3244032 | tf_op jit(solution)/shard_map/all_to_all | solution.py:369
  597.7 267.4 %reduce-scatter.6.cloned.1.call-start = ((), (), s32[]{:S(2)}) async-start(), calls=%async_computation.12 | async-start | bytes 2785280 | tf_op jit(solution)/shard_map/reduce_scatter | solution.py:193
  671.4 196.9 %reduce-scatter.8.cloned.1.call-start = ((), (), s32[]{:S(2)}) async-start(), calls=%async_computation.15 | async-start | bytes 5242880 | tf_op jit(solution)/shard_map/reduce_scatter | solution.py:312
  705.7 20.6 %copy-start.9 = (f32[512,1024]{1,0:T(8,128)S(1)}, f32[512,1024]{1,0:T(8,128)}, u32[]{:S(2)}) copy-start(f32[512,1024]{1,0:T(8,128)} %fusion.59) | copy-start | bytes 6291460
  773.6 12.2 %copy-start.12 = (f32[4]{0:T(128)S(1)}, f32[4]{0:T(128)}, u32[]{:S(2)}) copy-start(f32[4]{0:T(128)} %get-tuple-element.20) | copy-start | bytes 52
  781.6 59.0 %all-to-all-start.3 = ((bf16[8,2,73728]{2,1,0:T(2,128)(2,1)}), bf16[8,2,73728]{2,1,0:T(2,128)(2,1)S(1)}, u32[]{:S(2)}, u32[]{:S(2)}) async-start(bf16[8,2,73728]{2,1,0:T(2,128)(2,1)} %reshape.192), calls=%async_computation.3 | async-start | bytes 4718592 | tf_op jit(solution)/shard_map/all_to_all | solution.py:380
  845.9 11.9 %copy-start.4 = (f32[384,1024]{1,0:T(8,128)S(1)}, f32[384,1024]{1,0:T(8,128)}, u32[]{:S(2)}) copy-start(f32[384,1024]{1,0:T(8,128)} %copy-done.3) | copy-start | bytes 4718596
Sparse Core Ops, SparseCore 0:
  11.0 79.8 all-gather.6
  93.9 151.4 all-gather.8
  247.6 111.6 all-gather.10
  361.4 104.7 all-gather.14
  469.6 90.5 reduce-scatter.3
  562.2 126.4 all-gather.12
  691.3 32.2 reduce-scatter.5
  729.0 45.6 reduce-scatter.7

commit v6 on v5

--- a/solution.py
+++ b/solution.py
@@ -240,18 +240,19 @@
         jnp.einsum("td,ide->tie", layer_in, qkv_weights, preferred_element_type=jnp.float32)
         + qkv_bias[None]
     )
-    qkv_split = projected.astype(jnp.bfloat16).reshape(tokens, 3, seq_count, local_heads, head_size)
-    head_piece = lax.all_to_all(qkv_split, "seq", split_axis=2, concat_axis=0, tiled=True)
-    queries = head_piece[:, 0, 0]
-    attend_key_rows = head_piece[:, 1, 0]
-    attend_value_rows = head_piece[:, 2, 0]
-    head_count = queries.shape[1]
-    by_head = lambda rows: jnp.transpose(rows, (1, 0, 2))
-    head_q, head_k, head_v = by_head(queries), by_head(attend_key_rows), by_head(attend_value_rows)
+    head_width = local_heads * head_size
+    qkv_send = jnp.transpose(
+        projected.astype(jnp.bfloat16).reshape(tokens, 3, seq_count, head_width), (2, 0, 1, 3)
+    ).reshape(seq_count, tokens, 3 * head_width)
+    qkv_recv = lax.all_to_all(qkv_send, "seq", split_axis=0, concat_axis=0, tiled=True)
+    head_all = jnp.transpose(
+        qkv_recv.reshape(seg_len, 3, local_heads, head_size), (1, 2, 0, 3)
+    )
+    head_q, head_k, head_v = head_all[0], head_all[1], head_all[2]
     head_mixed, log_total = attn_forward(head_q, head_k, head_v, segment_doc, score_scale)
-    mixed_rows = jnp.transpose(head_mixed, (1, 0, 2)).reshape(seg_len, 1, head_count, head_size)
-    token_mixed = lax.all_to_all(mixed_rows, "seq", split_axis=0, concat_axis=1, tiled=True)
-    attn_mixed = token_mixed.reshape(tokens, model_width)
+    mixed_rows = jnp.transpose(head_mixed, (1, 0, 2)).reshape(seq_count, tokens, head_width)
+    token_mixed = lax.all_to_all(mixed_rows, "seq", split_axis=0, concat_axis=0, tiled=True)
+    attn_mixed = jnp.transpose(token_mixed, (1, 0, 2)).reshape(tokens, model_width)
     branch = jnp.dot(attn_mixed, out_weights, preferred_element_type=jnp.float32) + bias_o
     resid_one = layer_in.astype(jnp.float32) + branch
     normed, scaled_one, inverse_one = norm_forward(resid_one, gain_one, shift_one)
@@ -326,9 +327,11 @@
         tiled=True,
     )[:, 0]
     grad_mixed_low = contract_cols(grad_branch_low, out_weights).astype(jnp.bfloat16)
-    grad_split = grad_mixed_low.reshape(tokens, 1, seq_count, local_heads, head_size)
-    grad_heads = lax.all_to_all(grad_split, "seq", split_axis=2, concat_axis=0, tiled=True)
-    head_grad = by_head(grad_heads[:, 0, 0])
+    grad_split = jnp.transpose(
+        grad_mixed_low.reshape(tokens, seq_count, head_width), (1, 0, 2)
+    )
+    grad_heads = lax.all_to_all(grad_split, "seq", split_axis=0, concat_axis=0, tiled=True)
+    head_grad = jnp.transpose(grad_heads.reshape(seg_len, local_heads, head_size), (1, 0, 2))
 
     grad_queries, grad_keys, grad_values = attn_backward(
         head_q, head_k, head_v, head_grad, log_total, segment_doc, score_scale
@@ -340,7 +343,6 @@
         "td,tihe->dihe", segment_in, head_grads, preferred_element_type=jnp.float32
     )
     qkv_blocks = 3 * out_blocks
-    head_width = local_heads * head_size
     head_bias_sums = jnp.sum(head_grads.astype(jnp.float32), axis=0).reshape(3, head_width)
     bias_qv = lax.dynamic_update_slice(
         jnp.zeros((2, model_width), jnp.float32),
@@ -376,9 +378,13 @@
     qkv_rows = jnp.transpose(row_blocks, (1, 2, 0, 3)).reshape(qkv_blocks, block_height, model_width)
     vector_rows = jnp.sum(exchanged[:, row_size:].reshape(seq_count, fsdp_count, slot), axis=0)
     vector_rows = jnp.pad(vector_rows, ((0, 0), (0, model_width - slot)))[:, None]
-    head_grads = head_grads[:, :, None]
-    token_grads = lax.all_to_all(head_grads, "seq", split_axis=0, concat_axis=2, tiled=True)
-    grad_qkv = token_grads.reshape(tokens, 3, model_width)
+    token_grads = lax.all_to_all(
+        head_grads.reshape(seq_count, tokens, 3 * head_width),
+        "seq", split_axis=0, concat_axis=0, tiled=True,
+    )
+    grad_qkv = jnp.transpose(
+        token_grads.reshape(seq_count, tokens, 3, head_width), (1, 2, 0, 3)
+    ).reshape(tokens, 3, model_width)
     input_grad = grad_resid_one + jnp.einsum(
         "tie,ide->td", grad_qkv, qkv_weights, preferred_element_type=jnp.float32
     )

time: 884 us -> 821 us (0.929)
  local copies, waits for them, and re-layouts: 129 us -> 61.3 us
  waiting for transfers between devices: 274 us -> 283 us
    broadcast_in_dim x1 -> x0, local copies, waits for them, and re-layouts: 42.4 us -> none  [layer_body(): head_grads = head_grads[:, :, None]]
    unnamed x40 -> x33, local copies, waits for them, and re-layouts: 24.1 us -> 3.05 us
    all_to_all x5 -> x2, local copies, waits for them, and re-layouts: 18.6 us -> 3.28 us  [the longest x1 2.82 us: layer_body(): lax.all_to_all(qkv_send, 'seq', split_axis=0, concat_axis=0, tiled=True)]
    reshape x2 -> x9, local copies, waits for them, and re-layouts: 5.54 us -> 20.3 us  [the longest x2 8.15 us: layer_body(): qkv_recv.reshape(seg_len, 3, local_heads, head_size)]
    all_gather x1, waiting for transfers between devices: 17.1 us -> 27.9 us  [layer_body(): grad_mlp_seg = lax.all_gather(grad_mlp_low, 'seq', axis=0, tiled=True)]
  transfers between devices with their start and end apart: 13 -> 13, of which waited for: 7 -> 7; matrix products, arithmetic and copies ran while one was open for 31% -> 25% of each run, Pallas kernels for 19% -> 21%
where the time goes in v6:
time: 821 us; the launch traced here: 813 us
  waiting for transfers between devices  283 us (34%)
  Pallas kernels  171 us (21%)
  blocking collectives  119 us (14%)
  matrix products  114 us (14%)
  local copies, waits for them, and re-layouts  61.3 us (7%)
  other arithmetic  26.7 us (3%)
  starting transfers between devices  21.5 us (3%)
  between operations  16.2 us (2%)
    pallas_call x1, Pallas kernels, attn_backward(): pl.pallas_call(functools.partial(_bwd_kernel, scale=scale, block=block),...  92.2 us
    all_to_all x1, waiting for transfers between devices, layer_body(): lax.all_to_all(qkv_send, 'seq', split_axis=0, concat_axis=0, tiled=True)  82.3 us
    pallas_call x1, Pallas kernels, attn_forward(): pl.pallas_call(functools.partial(_fwd_kernel, scale=scale, block=block),...  78.4 us
    all_gather x1, blocking collectives, layer_body(): lax.all_gather(param_vector, ('fsdp', 'seq'), axis=0, tiled=True)  71.1 us
    all_to_all x1, waiting for transfers between devices, layer_body(): lax.all_to_all(head_grads.reshape(seq_count, tokens, 3 * head_width), 'se...  52.8 us
    psum x1, blocking collectives, layer_body(): lax.psum((squares, jnp.sum(valid_rows)), ('fsdp', 'seq'))  48 us
    all_to_all x1, waiting for transfers between devices, layer_body(): lax.all_to_all(jnp.concatenate([row_part.reshape(seq_count, -1), vector_p...  44.8 us
    dot_general x3, matrix products, contract_rows(): lax.dot_general(left, right, (((0,), (0,)), ((), ())), preferred_element_...  39.1 us
  transfers between devices with their start and end apart: 13, of which 7 were waited for; matrix products, arithmetic and copies ran while one was open for 25% of the time, Pallas kernels for 21%

profile of v6, /device:TPU:0, one launch (start us, length us, event | category | flops | bytes accessed | tf_op | source)
XLA Modules:
  0.0 812.9 jit_solution(8279202723810058195)
XLA Ops:
  7.2 0.7 all-gather.7.cloned.1.call-update
  7.9 0.7 all-gather.9.cloned.1.call-update
  9.4 0.7 reshape.198
  10.1 71.1 %all-gather = bf16[32,1,384]{2,1,0:T(2,128)(2,1)S(1)} all-gather(bf16[1,1,384]{2,1,0:T(2,128)(2,1)S(1)} %reshape.198), channel_id=1, replica_groups=mesh['fsdp'=4,'seq'=8] {'fsdp','seq'}, dimensions={0}, use_global_device_ids=true | all-gather | bytes 25344 | tf_op jit(solution)/shard_map/all_gather | solution.py:218
  81.4 9.5 %all-gather.7.cloned.1.call-done = bf16[4096,1024]{1,0:T(8,128)(2,1)} async-done(((bf16[128,1024]{1,0:T(8,128)(2,1)}), bf16[4096,1024]{1,0:T(8,128)(2,1)}) %all-gather.7.cloned.1.call-update) | async-done | bytes 8388624 | tf_op jit(solution)/shard_map/all_gather | solution.py:216
  90.9 3.5 slice.109
  94.4 2.8 add_convert_fusion
  97.9 2.8 copy.58
  100.7 4.0 all-to-all-start
  104.9 1.7 copy.61.dq_ref
  107.3 82.3 %all-to-all-done = bf16[8,384,384]{1,2,0:T(8,128)(2,1)S(1)} async-done(((bf16[8,384,384]{1,2,0:T(8,128)(2,1)}), bf16[8,384,384]{1,2,0:T(8,128)(2,1)S(1)}, u32[]{:S(2)}, u32[]{:S(2)}) %all-to-all-start) | async-done | bytes 2359328 | tf_op jit(solution)/shard_map/all_to_all | solution.py:247
  189.6 2.8 copy.59
  192.4 4.0 reshape.174
  196.5 4.1 copy.60
  200.6 4.6 slice_bitcast_fusion
  205.2 78.4 %shard_map.118 = (bf16[2,3072,64]{2,1,0:T(8,128)(2,1)}, f32[2,3072,1]{2,1,0:T(8,128)}) custom-call(s32[12]{0:T(128)} %get-tuple-element.70.lo_ref, s32[12]{0:T(128)} %get-tuple-element.69.hi_ref, bf16[2,3072,64]{2,1,0:T(8,128)(2,1)} %get-tuple-element.54.q_ref, bf16[2,3072,64]{2,1,0:T(8,128)(2,1)} %get-tuple-element.53.k_ref, ...), custom_call_target="tpu_custom_call" | custom-call | tf_op jit(solution)/shard_map/pallas_call | solution.py:73
  283.6 1.7 copy.62
  285.5 1.0 copy.63
  286.4 3.6 all-to-all-start.1
  291.4 38.4 %all-to-all-done.1 = bf16[8,384,128]{1,2,0:T(8,128)(2,1)S(1)} async-done(((bf16[8,384,128]{1,2,0:T(8,128)(2,1)}), bf16[8,384,128]{1,2,0:T(8,128)(2,1)S(1)}, u32[]{:S(2)}, u32[]{:S(2)}) %all-to-all-start.1) | async-done | bytes 786464 | tf_op jit(solution)/shard_map/all_to_all | solution.py:254
  329.8 3.0 fusion.139
  332.8 1.3 fusion.46
  334.1 1.2 fusion.57
  335.9 9.9 %fusion.135 = f32[384,4096]{1,0:T(8,128)} fusion(bf16[384,1024]{1,0:T(8,128)(2,1)} %fusion.57, bf16[8192,1024]{1,0:T(8,128)(2,1)} %all-gather.9.cloned.1.call-done), kind=kOutput, calls=%fused_computation.225 | convolution fusion | flops 3221225472 | bytes 15466496 | tf_op jit(solution)/shard_map/dot_general | solution.py:203
  345.8 19.2 %fusion.138 = (f32[384]{0:T(512)S(1)}, f32[384,1024]{1,0:T(8,128)S(1)}, f32[384,1024]{1,0:T(8,128)S(1)}) fusion(f32[1024]{0:T(1024)S(1)} %get-tuple-element.58, f32[1024]{0:T(1024)S(1)} %get-tuple-element.59, f32[1024]{0:T(1024)S(1)} %get-tuple-element.60, f32[384]{0:T(512)S(1)} %add_rsqrt_fusion.1, f32[384,1024]{1,0:T(8,128)S(1)} %get-tuple-element.49, ...), kind=kOutput, calls=%fused_computation.227 | convolution fusion | flops 3327786496 | bytes 19432960 | tf_op jit(solution)/shard_map/dot_general | solution.py:263
  365.0 1.4 fusion.48
  366.4 2.7 pad_maximum_fusion.3
  369.1 48.0 %all-reduce.1 = (f32[4]{0:T(128)}, f32[]{:T(128)}) all-reduce(f32[4]{0:T(128)S(1)} %pad_maximum_fusion.3, f32[]{:T(128)} %fusion.63), channel_id=1, replica_groups=mesh['fsdp'=4,'seq'=8] {'fsdp','seq'}, use_global_device_ids=true, to_apply=%region_10.11 | all-reduce | flops 5 | bytes 40 | tf_op jit(solution)/shard_map/psum | solution.py:274
  417.1 1.9 fusion.50
  419.0 3.0 convert_reduce_fusion.3
  422.0 8.9 %convert_reduce_fusion.1 = (f32[4096]{0:T(1024)S(1)}, bf16[384,4096]{1,0:T(8,128)(2,1)S(1)}) fusion(f32[384,4096]{1,0:T(8,128)} %fusion.135, f32[4096]{0:T(1024)S(1)} %slice.120, bf16[384,1024]{1,0:T(8,128)(2,1)} %get-tuple-element.41, bf16[8192,1024]{1,0:T(8,128)(2,1)} %all-gather.9.cloned.1.call-done), kind=kOutput, calls=%fused_computation.36 | convolution fusion | flops 3241668608 | bytes 18644992 | tf_op jit(solution)/shard_map/dot_general | solution.py:203
  430.9 7.6 multiply_reduce_fusion
  439.0 3.2 convolution_bitcast_fusion
  442.3 2.6 fusion.54
  444.9 1.2 copy.77
  446.1 5.0 all-to-all-start.2
  451.7 25.0 %all-to-all-done.2 = bf16[8,384,128]{1,2,0:T(8,128)(2,1)S(1)} async-done(((bf16[8,384,128]{1,2,0:T(8,128)(2,1)}), bf16[8,384,128]{1,2,0:T(8,128)(2,1)S(1)}, u32[]{:S(2)}, u32[]{:S(2)}) %all-to-all-start.2) | async-done | bytes 786464 | tf_op jit(solution)/shard_map/all_to_all | solution.py:333
  477.4 1.5 copy.66
  479.0 92.2 %shard_map.119 = (f32[2,3072,64]{2,1,0:T(8,128)}, f32[2,3072,64]{2,1,0:T(8,128)}, f32[2,3072,64]{2,1,0:T(8,128)}) custom-call(s32[12]{0:T(128)} %get-tuple-element.70.lo_ref, s32[12]{0:T(128)} %get-tuple-element.69.hi_ref, bf16[2,3072,64]{2,1,0:T(8,128)(2,1)} %get-tuple-element.54.q_ref, bf16[2,3072,64]{2,1,0:T(8,128)(2,1)} %get-tuple-element.53.k_ref, ...), custom_call_target="tpu_custom_call" | custom-call | tf_op jit(solution)/shard_map/pallas_call | solution.py:152
  571.2 2.2 convert_bitcast_fusion
  573.4 2.1 convert_bitcast_fusion.1
  575.8 3.0 convert_reduce_fusion
  579.0 6.2 fusion.16
  585.8 0.9 copy.88
  586.9 2.9 copy.74
  589.7 3.6 all-to-all-start.4
  593.4 6.8 fusion.140
  600.3 1.0 constant_dynamic-slice_fusion.2
  601.4 8.2 %fusion.142 = f32[3072,512]{1,0:T(8,128)} fusion(bf16[3072,1024]{1,0:T(8,128)(2,1)} %all-gather.15.cloned.1.call-done, bf16[512,1024]{1,0:T(8,128)(2,1)S(1)} %bitcast.171), kind=kOutput, calls=%fused_computation.231 | convolution fusion | flops 3221225472 | bytes 13631488 | tf_op jit(solution)/shard_map/dot_general | solution.py:203
  609.6 44.8 %all-to-all-done.4 = f32[8,1,50688]{2,1,0:T(1,128)S(1)} async-done(((f32[8,1,50688]{2,1,0:T(1,128)}), f32[8,1,50688]{2,1,0:T(1,128)S(1)}, u32[]{:S(2)}, u32[]{:S(2)}) %all-to-all-start.4) | async-done | bytes 1622048 | tf_op jit(solution)/shard_map/all_to_all | solution.py:371
  655.0 2.6 pad_maximum_fusion.1
  657.8 27.9 %all-gather.13.cloned.1.call-done = bf16[3072,1024]{1,0:T(8,128)(2,1)} async-done(((bf16[384,1024]{1,0:T(8,128)(2,1)}), bf16[3072,1024]{1,0:T(8,128)(2,1)}) %all-gather.13.cloned.1.call-update) | async-done | bytes 6291472 | tf_op jit(solution)/shard_map/all_gather | solution.py:299
  685.7 15.6 %fusion.58 = f32[512,1024]{1,0:T(8,128)S(1)} fusion(bf16[3072,1024]{1,0:T(8,128)(2,1)} %all-gather.15.cloned.1.call-done, f32[3072,512]{1,0:T(8,128)} %fusion.142, bf16[3072,1024]{1,0:T(8,128)(2,1)} %all-gather.13.cloned.1.call-done, bf16[512,1024]{1,0:T(8,128)(2,1)} %bitcast.170, f32[512]{0:T(512)S(1)} %bitcast.184), kind=kOutput, calls=%fused_computation.111 | convolution fusion | flops 6459752448 | bytes 22022144 | tf_op jit(solution)/shard_map/dot_general | solution.py:197
  701.3 20.2 %fusion.34 = f32[512,1024]{1,0:T(8,128)S(1)} fusion(bf16[3072,1024]{1,0:T(8,128)(2,1)} %all-gather.13.cloned.1.call-done, f32[3072,512]{1,0:T(8,128)} %fusion.142, f32[512]{0:T(512)S(1)} %bitcast.185), kind=kOutput, calls=%fused_computation.58 | convolution fusion | flops 3325034496 | bytes 14682112 | tf_op jit(solution)/shard_map/dot_general | solution.py:197
  721.5 2.4 pad_maximum_fusion
  724.0 4.9 copy.68
  729.5 1.7 copy.69
  731.2 3.9 all-to-all-start.3
  736.3 52.8 %all-to-all-done.3 = bf16[8,384,384]{1,2,0:T(8,128)(2,1)S(1)} async-done(((bf16[8,384,384]{1,2,0:T(8,128)(2,1)}), bf16[8,384,384]{1,2,0:T(8,128)(2,1)S(1)}, u32[]{:S(2)}, u32[]{:S(2)}) %all-to-all-start.3) | async-done | bytes 2359328 | tf_op jit(solution)/shard_map/all_to_all | solution.py:381
  789.1 2.8 copy.70
  791.9 3.6 reshape.181
  795.6 7.0 bitcast_add_fusion
  802.6 1.3 slice_reduce_fusion.1
  803.9 1.9 slice_bitcast_fusion.3
  (93 shorter events, 9.0 us)
Async XLA Ops:
  7.2 83.7 %all-gather.7.cloned.1.call-start = ((), (), s32[]{:S(2)}) async-start(), calls=%async_computation.8 | async-start | bytes 8650752 | tf_op jit(solution)/shard_map/all_gather | solution.py:216
  7.9 328.0 %all-gather.9.cloned.1.call-start = ((), (), s32[]{:S(2)}) async-start(), calls=%async_computation.9 | async-start | bytes 17301504 | tf_op jit(solution)/shard_map/all_gather | solution.py:217
  8.6 570.3 %all-gather.11.cloned.1.call-start = ((), (), s32[]{:S(2)}) async-start(), calls=%async_computation.10 | async-start | bytes 7077888 | tf_op jit(solution)/shard_map/all_gather | solution.py:232
  81.4 13.0 %copy-start.7 = (bf16[384,1024]{1,0:T(8,128)(2,1)S(1)}, bf16[384,1024]{1,0:T(8,128)(2,1)}, u32[]{:S(2)}) copy-start(bf16[384,1024]{1,0:T(8,128)(2,1)} %param.7) | copy-start | bytes 2359300
  94.4 2.9 copy-start.1
  97.3 7.4 copy-start.8
  100.7 88.9 %all-to-all-start = ((bf16[8,384,384]{1,2,0:T(8,128)(2,1)}), bf16[8,384,384]{1,2,0:T(8,128)(2,1)S(1)}, u32[]{:S(2)}, u32[]{:S(2)}) async-start(bf16[8,384,384]{1,2,0:T(8,128)(2,1)} %bitcast.149), calls=%async_computation | async-start | bytes 4718592 | tf_op jit(solution)/shard_map/all_to_all | solution.py:247
  286.4 43.3 %all-to-all-start.1 = ((bf16[8,384,128]{1,2,0:T(8,128)(2,1)}), bf16[8,384,128]{1,2,0:T(8,128)(2,1)S(1)}, u32[]{:S(2)}, u32[]{:S(2)}) async-start(bf16[8,384,128]{1,2,0:T(8,128)(2,1)} %copy.63), calls=%async_computation.1 | async-start | bytes 1572864 | tf_op jit(solution)/shard_map/all_to_all | solution.py:254
  290.0 311.3 %all-gather.15.cloned.1.call-start = ((), (), s32[]{:S(2)}) async-start(), calls=%async_computation.14 | async-start | bytes 7077888 | tf_op jit(solution)/shard_map/all_gather | solution.py:260
  329.8 5.5 copy-start.3
  335.3 319.7 %reduce-scatter.4.cloned.1.call-start = ((), (), s32[]{:S(2)}) async-start(), calls=%async_computation.11 | async-start | bytes 4718592 | tf_op jit(solution)/shard_map/reduce_scatter | solution.py:321
  335.9 9.9 %copy-start = (bf16[8192,1024]{1,0:T(8,128)(2,1)S(1)}, bf16[8192,1024]{1,0:T(8,128)(2,1)}, u32[]{:S(2)}) copy-start(bf16[8192,1024]{1,0:T(8,128)(2,1)} %all-gather.9.cloned.1.call-done) | copy-start | bytes 50331652
  422.0 8.9 %copy-start.6 = (bf16[384,1024]{1,0:T(8,128)(2,1)S(1)}, bf16[384,1024]{1,0:T(8,128)(2,1)}, u32[]{:S(2)}) copy-start(bf16[384,1024]{1,0:T(8,128)(2,1)} %param.8) | copy-start | bytes 2359300
  430.9 8.1 %copy-start.4 = (bf16[8,384,128]{1,2,0:T(8,128)(2,1)S(1)}, bf16[8,384,128]{1,2,0:T(8,128)(2,1)}, u32[]{:S(2)}) copy-start(bf16[8,384,128]{1,2,0:T(8,128)(2,1)} %copy-done.3) | copy-start | bytes 2359300
  439.0 5.9 copy-start.2
  446.1 30.5 %all-to-all-start.2 = ((bf16[8,384,128]{1,2,0:T(8,128)(2,1)}), bf16[8,384,128]{1,2,0:T(8,128)(2,1)S(1)}, u32[]{:S(2)}, u32[]{:S(2)}) async-start(bf16[8,384,128]{1,2,0:T(8,128)(2,1)} %bitcast.22), calls=%async_computation.2 | async-start | bytes 1572864 | tf_op jit(solution)/shard_map/all_to_all | solution.py:333
  451.1 234.6 %all-gather.13.cloned.1.call-start = ((), (), s32[]{:S(2)}) async-start(), calls=%async_computation.13 | async-start | bytes 7077888 | tf_op jit(solution)/shard_map/all_gather | solution.py:299
  571.2 4.4 copy-start.5
  589.7 64.7 %all-to-all-start.4 = ((f32[8,1,50688]{2,1,0:T(1,128)}), f32[8,1,50688]{2,1,0:T(1,128)S(1)}, u32[]{:S(2)}, u32[]{:S(2)}) async-start(f32[8,1,50688]{2,1,0:T(1,128)} %copy.74), calls=%async_computation.4 | async-start | bytes 3244032 | tf_op jit(solution)/shard_map/all_to_all | solution.py:371
  593.3 209.3 %reduce-scatter.6.cloned.1.call-start = ((), (), s32[]{:S(2)}) async-start(), calls=%async_computation.12 | async-start | bytes 2785280 | tf_op jit(solution)/shard_map/reduce_scatter | solution.py:193
  657.6 148.2 %reduce-scatter.8.cloned.1.call-start = ((), (), s32[]{:S(2)}) async-start(), calls=%async_computation.15 | async-start | bytes 5242880 | tf_op jit(solution)/shard_map/reduce_scatter | solution.py:313
  728.9 6.8 copy-start.9
  731.2 57.9 %all-to-all-start.3 = ((bf16[8,384,384]{1,2,0:T(8,128)(2,1)}), bf16[8,384,384]{1,2,0:T(8,128)(2,1)S(1)}, u32[]{:S(2)}, u32[]{:S(2)}) async-start(bf16[8,384,384]{1,2,0:T(8,128)(2,1)} %copy.69), calls=%async_computation.3 | async-start | bytes 4718592 | tf_op jit(solution)/shard_map/all_to_all | solution.py:381
Sparse Core Ops, SparseCore 0:
  11.0 79.8 all-gather.6
  93.9 151.4 all-gather.8
  247.6 111.6 all-gather.10
  361.3 104.5 all-gather.14
  469.4 90.4 reduce-scatter.3
  562.0 123.6 all-gather.12
  688.3 31.1 reduce-scatter.5
  724.1 43.3 reduce-scatter.7

commit v7 on v6

--- a/solution.py
+++ b/solution.py
@@ -189,6 +189,28 @@
     )
 
 
+def ring_gather(rows, count, index):
+    half = count // 2
+    order = [2 * a for a in range(half)] + [2 * a + 1 for a in reversed(range(half))]
+    place = [order.index(s) for s in range(count)]
+    forward_pairs = [(order[i], order[(i + 1) % count]) for i in range(count)]
+    backward_pairs = [(b, a) for a, b in forward_pairs]
+    by_offset = [None] * count
+    by_offset[0] = rows
+    moving = rows
+    for step in range(1, count - count // 2):
+        moving = lax.ppermute(moving, "seq", forward_pairs)
+        by_offset[count - step] = moving
+    moving = rows
+    for step in range(1, count // 2 + 1):
+        moving = lax.ppermute(moving, "seq", backward_pairs)
+        by_offset[step] = moving
+    position = jnp.asarray(place, jnp.int32)[index]
+    pick = (jnp.asarray(place, jnp.int32) - position) % count
+    stacked = jnp.stack(by_offset)
+    return jnp.take(stacked, pick, axis=0).reshape((count * rows.shape[0],) + rows.shape[1:])
+
+
 def attn_sum(values):
     return lax.psum_scatter(values, "fsdp", scatter_dimension=0, tiled=True)[0]
 
@@ -212,11 +234,14 @@
     head_size = model_width // H
     local_heads = H // seq_count
     score_scale = head_size ** (-0.5)
-    attn_full, mlp_full, vector_full = (
-        lax.all_gather(attn_weights, ("fsdp", "seq"), axis=0, tiled=True),
-        lax.all_gather(mlp_weights, ("fsdp", "seq"), axis=0, tiled=True),
-        lax.all_gather(param_vector, ("fsdp", "seq"), axis=0, tiled=True),
-    )
+    attn_rows, vector_slot = attn_weights.shape[0], param_vector.shape[0]
+    packed = jnp.concatenate(
+        [attn_weights, jnp.pad(param_vector, (0, model_width - vector_slot))[None]], axis=0
+    )
+    packed_full = lax.all_gather(packed, ("fsdp", "seq"), axis=0, tiled=False)
+    attn_full = packed_full[:, :attn_rows].reshape(-1, model_width)
+    vector_full = packed_full[:, attn_rows, :vector_slot].reshape(-1)
+    mlp_full = lax.all_gather(mlp_weights, ("fsdp", "seq"), axis=0, tiled=True)
     hidden = mlp_full.shape[0] // 2
     vector_wide = vector_full.astype(jnp.float32)
     pieces = [
@@ -229,24 +254,23 @@
     out_weights = attn_full[3 * model_width :]
     in_weights = mlp_full[:hidden]
     down_weights = mlp_full[hidden:]
-    segment_in = lax.all_gather(layer_in, "seq", axis=0, tiled=True)
+    segment_in = ring_gather(layer_in, seq_count, seq_index)
     segment_doc = doc_ids[0]
     seg_len = segment_doc.shape[0]
     positions = seq_index * tokens + lax.iota(jnp.int32, tokens)
     valid_rows = (positions < valid_len[0]).astype(jnp.float32)[:, None]
     zero_row = jnp.zeros((1, model_width), jnp.float32)
     qkv_bias = jnp.concatenate([bias_q[None], zero_row, bias_v[None]], axis=0)
+    head_width = local_heads * head_size
+    own_columns = seq_index * head_width
+    own_weights = lax.dynamic_slice_in_dim(qkv_weights, own_columns, head_width, axis=2)
+    own_bias = lax.dynamic_slice_in_dim(qkv_bias, own_columns, head_width, axis=1)
     projected = (
-        jnp.einsum("td,ide->tie", layer_in, qkv_weights, preferred_element_type=jnp.float32)
-        + qkv_bias[None]
-    )
-    head_width = local_heads * head_size
-    qkv_send = jnp.transpose(
-        projected.astype(jnp.bfloat16).reshape(tokens, 3, seq_count, head_width), (2, 0, 1, 3)
-    ).reshape(seq_count, tokens, 3 * head_width)
-    qkv_recv = lax.all_to_all(qkv_send, "seq", split_axis=0, concat_axis=0, tiled=True)
+        jnp.einsum("td,ide->tie", segment_in, own_weights, preferred_element_type=jnp.float32)
+        + own_bias[None]
+    )
     head_all = jnp.transpose(
-        qkv_recv.reshape(seg_len, 3, local_heads, head_size), (1, 2, 0, 3)
+        projected.astype(jnp.bfloat16).reshape(seg_len, 3, local_heads, head_size), (1, 2, 0, 3)
     )
     head_q, head_k, head_v = head_all[0], head_all[1], head_all[2]
     head_mixed, log_total = attn_forward(head_q, head_k, head_v, segment_doc, score_scale)

time: 821 us -> 766 us (0.933)
  blocking collectives: 119 us -> 42.9 us
  waiting for transfers between devices: 283 us -> 249 us
  local copies, waits for them, and re-layouts: 61.3 us -> 86.2 us
  other arithmetic: 26.7 us -> 43.1 us
  starting transfers between devices: 21.5 us -> 32.8 us
    ppermute x0 -> x7, waiting for transfers between devices: none -> 90.6 us  [the longest x4 90.1 us: ring_gather(): moving = lax.ppermute(moving, 'seq', backward_pairs)]
    all_to_all x1 -> x0, waiting for transfers between devices: 82.3 us -> none  [layer_body(): lax.all_to_all(qkv_send, 'seq', split_axis=0, concat_axis=0, tiled=True)]
    all_gather x1 -> x0, blocking collectives: 71.1 us -> none  [layer_body(): lax.all_gather(param_vector, ('fsdp', 'seq'), axis=0, tiled=True)]
    all_gather x1, waiting for transfers between devices: 27.9 us -> 0.02 us  [layer_body(): grad_mlp_seg = lax.all_gather(grad_mlp_low, 'seq', axis=0, tiled=True)]
    all_to_all x1, waiting for transfers between devices: 38.4 us -> 19.1 us  [layer_body(): lax.all_to_all(mixed_rows, 'seq', split_axis=0, concat_axis=0, tiled=True)]
    select_n x0 -> x2, other arithmetic: none -> 12.7 us  [ring_gather(): jnp.take(stacked, pick, axis=0)]
    unnamed x33 -> x34, local copies, waits for them, and re-layouts: 3.05 us -> 14.6 us
    all_gather x3 -> x2, waiting for transfers between devices: 9.53 us -> 0.02 us  [the longest x1 0.02 us: layer_body(): mlp_full = lax.all_gather(mlp_weights, ('fsdp', 'seq'), axis=0, tiled=True)]
  transfers between devices with their start and end apart: 13 -> 18, of which waited for: 7 -> 9; matrix products, arithmetic and copies ran while one was open for 25% -> 31% of each run, Pallas kernels for 21% -> 23%
where the time goes in v7:
time: 766 us; the launch traced here: 756 us
  waiting for transfers between devices  249 us (33%)
  Pallas kernels  171 us (22%)
  matrix products  115 us (15%)
  local copies, waits for them, and re-layouts  86.2 us (11%)
  other arithmetic  43.1 us (6%)
  blocking collectives  42.9 us (6%)
  starting transfers between devices  32.8 us (4%)
  between operations  16.2 us (2%)
    pallas_call x1, Pallas kernels, attn_backward(): pl.pallas_call(functools.partial(_bwd_kernel, scale=scale, block=block),...  92.2 us
    ppermute x4, waiting for transfers between devices, ring_gather(): moving = lax.ppermute(moving, 'seq', backward_pairs)  90.1 us
    pallas_call x1, Pallas kernels, attn_forward(): pl.pallas_call(functools.partial(_fwd_kernel, scale=scale, block=block),...  78.5 us
    all_to_all x1, waiting for transfers between devices, layer_body(): lax.all_to_all(head_grads.reshape(seq_count, tokens, 3 * head_width), 'se...  53.5 us
    all_to_all x1, waiting for transfers between devices, layer_body(): lax.all_to_all(jnp.concatenate([row_part.reshape(seq_count, -1), vector_p...  52.7 us
    psum x1, blocking collectives, layer_body(): lax.psum((squares, jnp.sum(valid_rows)), ('fsdp', 'seq'))  42.9 us
    dot_general x3, matrix products, contract_rows(): lax.dot_general(left, right, (((0,), (0,)), ((), ())), preferred_element_...  39.3 us
    all_to_all x1, waiting for transfers between devices, layer_body(): lax.all_to_all(grad_split, 'seq', split_axis=0, concat_axis=0, tiled=True)  32.8 us
  transfers between devices with their start and end apart: 18, of which 9 were waited for; matrix products, arithmetic and copies ran while one was open for 31% of the time, Pallas kernels for 23%

profile of v7, /device:TPU:0, one launch (start us, length us, event | category | flops | bytes accessed | tf_op | source)
XLA Modules:
  0.0 756.2 jit_solution(17606593247140456040)
XLA Ops:
  7.9 1.7 maximum_bitcast_fusion.1
  10.4 3.0 collective-permute-start
  13.4 22.9 %collective-permute-done = bf16[384,1024]{1,0:T(8,128)(2,1)S(1)} collective-permute-done((bf16[384,1024]{1,0:T(8,128)(2,1)}, bf16[384,1024]{1,0:T(8,128)(2,1)S(1)}, u32[]{:S(2)}, u32[]{:S(2)}) %collective-permute-start) | collective-permute-done | bytes 786464 | tf_op jit(solution)/shard_map/ppermute | solution.py:206
  36.3 1.7 collective-permute-start.1
  42.3 25.3 %collective-permute-done.1 = bf16[384,1024]{1,0:T(8,128)(2,1)S(1)} collective-permute-done((bf16[384,1024]{1,0:T(8,128)(2,1)S(1)}, bf16[384,1024]{1,0:T(8,128)(2,1)S(1)}, u32[]{:S(2)}, u32[]{:S(2)}) %collective-permute-start.1) | collective-permute-done | bytes 786464 | tf_op jit(solution)/shard_map/ppermute | solution.py:206
  68.0 1.3 compare_and_fusion
  69.4 1.7 collective-permute-start.5
  71.2 2.4 copy.51.dq_ref
  74.2 2.2 bitcast_dynamic-update-slice_fusion.7
  76.4 35.1 %collective-permute-done.2 = bf16[384,1024]{1,0:T(8,128)(2,1)} collective-permute-done((bf16[384,1024]{1,0:T(8,128)(2,1)S(1)}, bf16[384,1024]{1,0:T(8,128)(2,1)}, u32[]{:S(2)}, u32[]{:S(2)}) %collective-permute-start.2) | collective-permute-done | bytes 786464 | tf_op jit(solution)/shard_map/ppermute | solution.py:206
  112.5 2.0 collective-permute-start.6
  115.4 2.1 bitcast_dynamic-update-slice_fusion.4
  117.5 6.8 collective-permute-done.3
  128.5 6.5 gather_fusion
  135.0 6.6 bitcast_select_fusion
  141.6 3.5 slice.120
  145.2 2.6 copy-done.1
  149.5 4.8 fusion.133
  154.9 4.1 copy.50
  159.0 4.7 slice_bitcast_fusion
  163.7 78.5 %shard_map.136 = (bf16[2,3072,64]{2,1,0:T(8,128)(2,1)}, f32[2,3072,1]{2,1,0:T(8,128)}) custom-call(s32[12]{0:T(128)} %get-tuple-element.74.lo_ref, s32[12]{0:T(128)} %get-tuple-element.73.hi_ref, bf16[2,3072,64]{2,1,0:T(8,128)(2,1)} %get-tuple-element.58.q_ref, bf16[2,3072,64]{2,1,0:T(8,128)(2,1)} %get-tuple-element.57.k_ref, ...), custom_call_target="tpu_custom_call" | custom-call | tf_op jit(solution)/shard_map/pallas_call | solution.py:73
  242.3 3.9 copy.67
  246.1 1.5 reshape.248
  247.6 7.9 %all-to-all-start = ((bf16[8,384,128]{2,1,0:T(8,128)(2,1)}), bf16[8,384,128]{2,1,0:T(8,128)(2,1)S(1)}, u32[]{:S(2)}, u32[]{:S(2)}) async-start(bf16[8,384,128]{2,1,0:T(8,128)(2,1)} %reshape.248), calls=%async_computation | async-start | bytes 1572864 | tf_op jit(solution)/shard_map/all_to_all | solution.py:278
  256.9 19.1 %all-to-all-done = bf16[8,384,128]{2,1,0:T(8,128)(2,1)S(1)} async-done(((bf16[8,384,128]{2,1,0:T(8,128)(2,1)}), bf16[8,384,128]{2,1,0:T(8,128)(2,1)S(1)}, u32[]{:S(2)}, u32[]{:S(2)}) %all-to-all-start) | async-done | bytes 786464 | tf_op jit(solution)/shard_map/all_to_all | solution.py:278
  275.9 3.0 fusion.130
  278.9 1.3 fusion.40
  282.1 10.4 %fusion.126 = f32[384,4096]{1,0:T(8,128)} fusion(bf16[384,1024]{1,0:T(8,128)(2,1)} %fusion.45, bf16[8192,1024]{1,0:T(8,128)(2,1)} %all-gather.7.cloned.1.call-done), kind=kOutput, calls=%fused_computation.241 | convolution fusion | flops 3221225472 | bytes 15466496 | tf_op jit(solution)/shard_map/dot_general | solution.py:225
  293.6 19.2 %fusion.129 = (f32[384]{0:T(512)S(1)}, f32[384,1024]{1,0:T(8,128)S(1)}, f32[384,1024]{1,0:T(8,128)S(1)}) fusion(f32[1024]{0:T(1024)S(1)} %get-tuple-element.62, f32[1024]{0:T(1024)S(1)} %get-tuple-element.63, f32[1024]{0:T(1024)S(1)} %get-tuple-element.64, f32[384]{0:T(512)S(1)} %add_rsqrt_fusion.1, f32[384,1024]{1,0:T(8,128)S(1)} %get-tuple-element.49, ...), kind=kOutput, calls=%fused_computation.243 | convolution fusion | flops 3327786496 | bytes 19432960 | tf_op jit(solution)/shard_map/dot_general | solution.py:287
  312.8 1.4 fusion.42
  314.2 2.7 pad_maximum_fusion.2
  316.9 2.3 copy.65
  319.2 42.9 %all-reduce.2 = (f32[4]{0:T(128)}, f32[]{:T(128)}) all-reduce(f32[4]{0:T(128)S(1)} %pad_maximum_fusion.2, f32[]{:T(128)} %fusion.52), channel_id=1, replica_groups=mesh['fsdp'=4,'seq'=8] {'fsdp','seq'}, use_global_device_ids=true, to_apply=%region_10.11 | all-reduce | flops 5 | bytes 40 | tf_op jit(solution)/shard_map/psum | solution.py:298
  362.0 1.9 fusion.44
  363.9 3.0 convert_reduce_fusion.3
  366.9 8.8 %convert_reduce_fusion.1 = (f32[4096]{0:T(1024)S(1)}, bf16[384,4096]{1,0:T(8,128)(2,1)S(1)}) fusion(f32[384,4096]{1,0:T(8,128)} %fusion.126, f32[4096]{0:T(1024)S(1)} %slice.132, bf16[384,1024]{1,0:T(8,128)(2,1)} %get-tuple-element.41, bf16[8192,1024]{1,0:T(8,128)(2,1)} %all-gather.7.cloned.1.call-done), kind=kOutput, calls=%fused_computation.37 | convolution fusion | flops 3241668608 | bytes 18644992 | tf_op jit(solution)/shard_map/dot_general | solution.py:225
  375.8 7.5 multiply_reduce_fusion
  383.8 3.2 convolution_bitcast_fusion
  387.1 1.8 slice.127
  391.1 6.2 all-to-all-start.1
  397.7 6.0 broadcast_select_fusion
  403.8 32.8 %all-to-all-done.1 = bf16[8,384,128]{1,2,0:T(8,128)(2,1)S(1)} async-done(((bf16[8,384,128]{1,2,0:T(8,128)(2,1)}), bf16[8,384,128]{1,2,0:T(8,128)(2,1)S(1)}, u32[]{:S(2)}, u32[]{:S(2)}) %all-to-all-start.1) | async-done | bytes 786464 | tf_op jit(solution)/shard_map/all_to_all | solution.py:357
  437.4 1.5 copy.56
  439.0 92.2 %shard_map.137 = (f32[2,3072,64]{2,1,0:T(8,128)}, f32[2,3072,64]{2,1,0:T(8,128)}, f32[2,3072,64]{2,1,0:T(8,128)}) custom-call(s32[12]{0:T(128)} %get-tuple-element.74.lo_ref, s32[12]{0:T(128)} %get-tuple-element.73.hi_ref, bf16[2,3072,64]{2,1,0:T(8,128)(2,1)} %get-tuple-element.58.q_ref, bf16[2,3072,64]{2,1,0:T(8,128)(2,1)} %get-tuple-element.57.k_ref, ...), custom_call_target="tpu_custom_call" | custom-call | tf_op jit(solution)/shard_map/pallas_call | solution.py:152
  531.2 5.8 convert_reduce_fusion
  537.2 4.9 copy.61
  542.1 5.6 fusion.134
  548.9 2.8 copy.64
  551.7 3.6 all-to-all-start.3
  555.6 6.9 fusion.131
  563.6 8.2 %fusion.135 = f32[3072,512]{1,0:T(8,128)} fusion(bf16[3072,1024]{1,0:T(8,128)(2,1)} %all-gather.11.cloned.1.call-done, bf16[512,1024]{1,0:T(8,128)(2,1)S(1)} %bitcast.182), kind=kOutput, calls=%fused_computation.249 | convolution fusion | flops 3221225472 | bytes 13631488 | tf_op jit(solution)/shard_map/dot_general | solution.py:225
  571.9 52.7 %all-to-all-done.3 = f32[8,1,50688]{2,1,0:T(1,128)S(1)} async-done(((f32[8,1,50688]{2,1,0:T(1,128)}), f32[8,1,50688]{2,1,0:T(1,128)S(1)}, u32[]{:S(2)}, u32[]{:S(2)}) %all-to-all-start.3) | async-done | bytes 1622048 | tf_op jit(solution)/shard_map/all_to_all | solution.py:395
  625.1 2.6 pad_maximum_fusion.1
  627.8 16.0 %fusion.46 = f32[512,1024]{1,0:T(8,128)S(1)} fusion(bf16[3072,1024]{1,0:T(8,128)(2,1)} %all-gather.11.cloned.1.call-done, f32[3072,512]{1,0:T(8,128)} %fusion.135, bf16[3072,1024]{1,0:T(8,128)(2,1)} %all-gather.9.cloned.1.call-done, bf16[512,1024]{1,0:T(8,128)(2,1)} %bitcast.181, f32[512]{0:T(512)S(1)} %bitcast.196), kind=kOutput, calls=%fused_computation.105 | convolution fusion | flops 6459752448 | bytes 22022144 | tf_op jit(solution)/shard_map/dot_general | solution.py:219
  643.8 20.1 %fusion.32 = f32[512,1024]{1,0:T(8,128)S(1)} fusion(bf16[3072,1024]{1,0:T(8,128)(2,1)} %all-gather.9.cloned.1.call-done, f32[3072,512]{1,0:T(8,128)} %fusion.135, f32[512]{0:T(512)S(1)} %bitcast.197), kind=kOutput, calls=%fused_computation.59 | convolution fusion | flops 3325034496 | bytes 14682112 | tf_op jit(solution)/shard_map/dot_general | solution.py:219
  663.9 2.4 pad_maximum_fusion
  666.4 4.8 copy.58
  671.7 1.7 copy.59
  673.4 4.2 all-to-all-start.2
  678.8 53.5 %all-to-all-done.2 = bf16[8,384,384]{1,2,0:T(8,128)(2,1)S(1)} async-done(((bf16[8,384,384]{1,2,0:T(8,128)(2,1)}), bf16[8,384,384]{1,2,0:T(8,128)(2,1)S(1)}, u32[]{:S(2)}, u32[]{:S(2)}) %all-to-all-start.2) | async-done | bytes 2359328 | tf_op jit(solution)/shard_map/all_to_all | solution.py:405
  732.3 2.9 copy.60
  735.2 3.6 reshape.211
  738.9 7.0 bitcast_add_fusion
  747.2 1.9 slice_bitcast_fusion.3
  (113 shorter events, 28.5 us)
Async XLA Ops:
  7.2 134.5 %all-gather.13.cloned.1.call-start = ((), (), s32[]{:S(2)}) async-start(), calls=%async_computation.13 | async-start | bytes 9191424 | tf_op jit(solution)/shard_map/all_gather | solution.py:241
  9.6 272.5 %all-gather.7.cloned.1.call-start = ((), (), s32[]{:S(2)}) async-start(), calls=%async_computation.7 | async-start | bytes 17301504 | tf_op jit(solution)/shard_map/all_gather | solution.py:244
  10.4 26.0 %collective-permute-start = (bf16[384,1024]{1,0:T(8,128)(2,1)}, bf16[384,1024]{1,0:T(8,128)(2,1)S(1)}, u32[]{:S(2)}, u32[]{:S(2)}) collective-permute-start(bf16[384,1024]{1,0:T(8,128)(2,1)} %param.9), channel_id=1, source_target_pairs={{2,0},{4,2},{6,4},{7,6},{5,7},{3,5},{1,3},{0,1},{10,8},{12,10},{14... | collective-permute-start | bytes 2359304 | tf_op jit(solution)/shard_map/ppermute | solution.py:206
  36.3 31.3 %collective-permute-start.1 = (bf16[384,1024]{1,0:T(8,128)(2,1)S(1)}, bf16[384,1024]{1,0:T(8,128)(2,1)S(1)}, u32[]{:S(2)}, u32[]{:S(2)}) collective-permute-start(bf16[384,1024]{1,0:T(8,128)(2,1)S(1)} %collective-permute-done), channel_id=1, source_target_pairs={{2,0},{4,2},{6,4},{7,6},{5,7},{3,5},{1,3},{0,1},{10,8},{12,10},{14... | collective-permute-start | bytes 2359304 | tf_op jit(solution)/shard_map/ppermute | solution.py:206
  38.0 31.3 %collective-permute-start.4 = (bf16[384,1024]{1,0:T(8,128)(2,1)}, bf16[384,1024]{1,0:T(8,128)(2,1)S(1)}, u32[]{:S(2)}, u32[]{:S(2)}) collective-permute-start(bf16[384,1024]{1,0:T(8,128)(2,1)} %param.9), channel_id=1, source_target_pairs={{0,2},{2,4},{4,6},{6,7},{7,5},{5,3},{3,1},{1,0},{8,10},{10,12},{12... | collective-permute-start | bytes 2359304 | tf_op jit(solution)/shard_map/ppermute | solution.py:202
  67.6 43.9 %collective-permute-start.2 = (bf16[384,1024]{1,0:T(8,128)(2,1)S(1)}, bf16[384,1024]{1,0:T(8,128)(2,1)}, u32[]{:S(2)}, u32[]{:S(2)}) collective-permute-start(bf16[384,1024]{1,0:T(8,128)(2,1)S(1)} %collective-permute-done.1), channel_id=1, source_target_pairs={{2,0},{4,2},{6,4},{7,6},{5,7},{3,5},{1,3},{0,1},{10,8},{12,10},{14... | collective-permute-start | bytes 2359304 | tf_op jit(solution)/shard_map/ppermute | solution.py:206
  69.4 43.1 %collective-permute-start.5 = (bf16[384,1024]{1,0:T(8,128)(2,1)S(1)}, bf16[384,1024]{1,0:T(8,128)(2,1)S(1)}, u32[]{:S(2)}, u32[]{:S(2)}) collective-permute-start(bf16[384,1024]{1,0:T(8,128)(2,1)S(1)} %collective-permute-done.4), channel_id=1, source_target_pairs={{0,2},{2,4},{4,6},{6,7},{7,5},{5,3},{3,1},{1,0},{8,10},{10,12},{12... | collective-permute-start | bytes 2359304 | tf_op jit(solution)/shard_map/ppermute | solution.py:202
  111.5 12.7 %collective-permute-start.3 = (bf16[384,1024]{1,0:T(8,128)(2,1)}, bf16[384,1024]{1,0:T(8,128)(2,1)S(1)}, u32[]{:S(2)}, u32[]{:S(2)}) collective-permute-start(bf16[384,1024]{1,0:T(8,128)(2,1)} %collective-permute-done.2), channel_id=1, source_target_pairs={{2,0},{4,2},{6,4},{7,6},{5,7},{3,5},{1,3},{0,1},{10,8},{12,10},{14... | collective-permute-start | bytes 2359304 | tf_op jit(solution)/shard_map/ppermute | solution.py:206
  112.5 13.2 %collective-permute-start.6 = (bf16[384,1024]{1,0:T(8,128)(2,1)S(1)}, bf16[384,1024]{1,0:T(8,128)(2,1)S(1)}, u32[]{:S(2)}, u32[]{:S(2)}) collective-permute-start(bf16[384,1024]{1,0:T(8,128)(2,1)S(1)} %collective-permute-done.5), channel_id=1, source_target_pairs={{0,2},{2,4},{4,6},{6,7},{7,5},{5,3},{3,1},{1,0},{8,10},{10,12},{12... | collective-permute-start | bytes 2359304 | tf_op jit(solution)/shard_map/ppermute | solution.py:202
  145.2 2.7 copy-start.1
  163.7 112.2 %copy-start.6 = (bf16[384,1024]{1,0:T(8,128)(2,1)S(1)}, bf16[384,1024]{1,0:T(8,128)(2,1)}, u32[]{:S(2)}) copy-start(bf16[384,1024]{1,0:T(8,128)(2,1)} %param.9) | copy-start | bytes 2359300
  247.6 28.3 %all-to-all-start = ((bf16[8,384,128]{2,1,0:T(8,128)(2,1)}), bf16[8,384,128]{2,1,0:T(8,128)(2,1)S(1)}, u32[]{:S(2)}, u32[]{:S(2)}) async-start(bf16[8,384,128]{2,1,0:T(8,128)(2,1)} %reshape.248), calls=%async_computation | async-start | bytes 1572864 | tf_op jit(solution)/shard_map/all_to_all | solution.py:278
  255.6 308.1 %all-gather.11.cloned.1.call-start = ((), (), s32[]{:S(2)}) async-start(), calls=%async_computation.11 | async-start | bytes 7077888 | tf_op jit(solution)/shard_map/all_gather | solution.py:284
  275.9 5.6 copy-start.2
  281.5 343.6 %reduce-scatter.4.cloned.1.call-start = ((), (), s32[]{:S(2)}) async-start(), calls=%async_computation.8 | async-start | bytes 4718592 | tf_op jit(solution)/shard_map/reduce_scatter | solution.py:345
  282.1 11.5 %copy-start = (bf16[8192,1024]{1,0:T(8,128)(2,1)S(1)}, bf16[8192,1024]{1,0:T(8,128)(2,1)}, u32[]{:S(2)}) copy-start(bf16[8192,1024]{1,0:T(8,128)(2,1)} %all-gather.7.cloned.1.call-done) | copy-start | bytes 50331652
  366.9 8.8 %copy-start.5 = (bf16[384,1024]{1,0:T(8,128)(2,1)S(1)}, bf16[384,1024]{1,0:T(8,128)(2,1)}, u32[]{:S(2)}) copy-start(bf16[384,1024]{1,0:T(8,128)(2,1)} %param.10) | copy-start | bytes 2359300
  375.7 8.1 %copy-start.4 = (bf16[384,8,128]{0,2,1:T(8,128)(2,1)S(1)}, bf16[384,8,128]{0,2,1:T(8,128)(2,1)}, u32[]{:S(2)}) copy-start(bf16[384,8,128]{0,2,1:T(8,128)(2,1)} %copy.65) | copy-start | bytes 2359300
  383.8 5.1 copy-start.3
  391.1 45.5 %all-to-all-start.1 = ((bf16[8,384,128]{1,2,0:T(8,128)(2,1)}), bf16[8,384,128]{1,2,0:T(8,128)(2,1)S(1)}, u32[]{:S(2)}, u32[]{:S(2)}) async-start(bf16[8,384,128]{1,2,0:T(8,128)(2,1)} %bitcast.35), calls=%async_computation.1 | async-start | bytes 1572864 | tf_op jit(solution)/shard_map/all_to_all | solution.py:357
  397.3 230.6 %all-gather.9.cloned.1.call-start = ((), (), s32[]{:S(2)}) async-start(), calls=%async_computation.10 | async-start | bytes 7077888 | tf_op jit(solution)/shard_map/all_gather | solution.py:323
  551.7 72.9 %all-to-all-start.3 = ((f32[8,1,50688]{2,1,0:T(1,128)}), f32[8,1,50688]{2,1,0:T(1,128)S(1)}, u32[]{:S(2)}, u32[]{:S(2)}) async-start(f32[8,1,50688]{2,1,0:T(1,128)} %copy.64), calls=%async_computation.3 | async-start | bytes 3244032 | tf_op jit(solution)/shard_map/all_to_all | solution.py:395
  555.3 190.6 %reduce-scatter.6.cloned.1.call-start = ((), (), s32[]{:S(2)}) async-start(), calls=%async_computation.9 | async-start | bytes 2785280 | tf_op jit(solution)/shard_map/reduce_scatter | solution.py:215
  627.8 121.3 %reduce-scatter.8.cloned.1.call-start = ((), (), s32[]{:S(2)}) async-start(), calls=%async_computation.12 | async-start | bytes 5242880 | tf_op jit(solution)/shard_map/reduce_scatter | solution.py:337
  671.2 7.1 copy-start.7
  673.4 58.9 %all-to-all-start.2 = ((bf16[8,384,384]{1,2,0:T(8,128)(2,1)}), bf16[8,384,384]{1,2,0:T(8,128)(2,1)S(1)}, u32[]{:S(2)}, u32[]{:S(2)}) async-start(bf16[8,384,384]{1,2,0:T(8,128)(2,1)} %copy.59), calls=%async_computation.2 | async-start | bytes 4718592 | tf_op jit(solution)/shard_map/all_to_all | solution.py:405
Sparse Core Ops, SparseCore 0:
  11.5 104.1 all-gather.12
  118.7 118.7 all-gather.6
  281.6 97.4 all-gather.10
  387.2 105.8 reduce-scatter.3
  495.2 129.0 all-gather.8
  627.9 31.9 reduce-scatter.5
  666.5 44.3 reduce-scatter.7

commit v8 on v7

--- a/solution.py
+++ b/solution.py
@@ -342,14 +342,19 @@
     grad_bias_o = jnp.sum(grad_branch_low.astype(jnp.float32), axis=0)
     block_height = 4 * model_width // (fsdp_count * seq_count)
     out_blocks = model_width // (seq_count * block_height)
-    out_rows = lax.psum_scatter(
-        contract_rows(attn_mixed, grad_branch_low).reshape(
-            out_blocks, seq_count, block_height, model_width
-        ),
-        "seq",
-        scatter_dimension=1,
-        tiled=True,
-    )[:, 0]
+    if out_blocks == 1 and block_height == head_width:
+        grad_branch_seg = ring_gather(grad_branch_low, seq_count, seq_index)
+        head_rows = jnp.transpose(head_mixed, (1, 0, 2)).reshape(seg_len, head_width)
+        out_rows = contract_rows(head_rows, grad_branch_seg)[None]
+    else:
+        out_rows = lax.psum_scatter(
+            contract_rows(attn_mixed, grad_branch_low).reshape(
+                out_blocks, seq_count, block_height, model_width
+            ),
+            "seq",
+            scatter_dimension=1,
+            tiled=True,
+        )[:, 0]
     grad_mixed_low = contract_cols(grad_branch_low, out_weights).astype(jnp.bfloat16)
     grad_split = jnp.transpose(
         grad_mixed_low.reshape(tokens, seq_count, head_width), (1, 0, 2)

time: 766 us -> 771 us (level)
  waiting for transfers between devices: 249 us -> 216 us
  starting transfers between devices: 32.8 us -> 56 us
  local copies, waits for them, and re-layouts: 86.2 us -> 105 us
    all_to_all x1, waiting for transfers between devices: 52.7 us -> 0.01 us  [layer_body(): lax.all_to_all(jnp.concatenate([row_part.reshape(seq_count, -1), vector_p...]
    ppermute x4 -> x8, waiting for transfers between devices: 90.1 us -> 128 us  [ring_gather(): moving = lax.ppermute(moving, 'seq', backward_pairs)]
    ppermute x4 -> x8, starting transfers between devices: 5.17 us -> 21.1 us  [ring_gather(): moving = lax.ppermute(moving, 'seq', backward_pairs)]
    all_to_all x1, waiting for transfers between devices: 32.8 us -> 21 us  [layer_body(): lax.all_to_all(grad_split, 'seq', split_axis=0, concat_axis=0, tiled=True)]
    all_to_all x1, starting transfers between devices: 4.21 us -> 13.3 us  [layer_body(): lax.all_to_all(head_grads.reshape(seq_count, tokens, 3 * head_width), 'se...]
    unnamed x34 -> x46, local copies, waits for them, and re-layouts: 14.6 us -> 23.5 us
  transfers between devices with their start and end apart: 18 -> 24, of which waited for: 9 -> 10; matrix products, arithmetic and copies ran while one was open for 31% -> 33% of each run, Pallas kernels for 23% -> 22%
where the time goes in v8:
time: 771 us; the launch traced here: 762 us
  waiting for transfers between devices  216 us (28%)
  Pallas kernels  171 us (22%)
  matrix products  113 us (15%)
  local copies, waits for them, and re-layouts  105 us (14%)
  starting transfers between devices  56 us (7%)
  blocking collectives  43.2 us (6%)
  other arithmetic  42 us (5%)
  between operations  16.2 us (2%)
    ppermute x8, waiting for transfers between devices, ring_gather(): moving = lax.ppermute(moving, 'seq', backward_pairs)  128 us
    pallas_call x1, Pallas kernels, attn_backward(): pl.pallas_call(functools.partial(_bwd_kernel, scale=scale, block=block),...  92.2 us
    pallas_call x1, Pallas kernels, attn_forward(): pl.pallas_call(functools.partial(_fwd_kernel, scale=scale, block=block),...  78.4 us
    all_to_all x1, waiting for transfers between devices, layer_body(): lax.all_to_all(head_grads.reshape(seq_count, tokens, 3 * head_width), 'se...  48.8 us
    psum x1, blocking collectives, layer_body(): lax.psum((squares, jnp.sum(valid_rows)), ('fsdp', 'seq'))  43.2 us
    dot_general x3, matrix products, contract_rows(): lax.dot_general(left, right, (((0,), (0,)), ((), ())), preferred_element_...  37.5 us
    dot_general x4, matrix products, contract_cols(): lax.dot_general(left, right, (((1,), (1,)), ((), ())), preferred_element_...  28.7 us
    unnamed x46, local copies, waits for them, and re-layouts  23.5 us
  transfers between devices with their start and end apart: 24, of which 10 were waited for; matrix products, arithmetic and copies ran while one was open for 33% of the time, Pallas kernels for 22%

profile of v8, /device:TPU:0, one launch (start us, length us, event | category | flops | bytes accessed | tf_op | source)
XLA Modules:
  0.0 761.7 jit_solution(851947574109849776)
XLA Ops:
  10.4 3.0 collective-permute-start
  13.4 22.9 %collective-permute-done = bf16[384,1024]{1,0:T(8,128)(2,1)S(1)} collective-permute-done((bf16[384,1024]{1,0:T(8,128)(2,1)}, bf16[384,1024]{1,0:T(8,128)(2,1)S(1)}, u32[]{:S(2)}, u32[]{:S(2)}) %collective-permute-start) | collective-permute-done | bytes 786464 | tf_op jit(solution)/shard_map/ppermute | solution.py:206
  42.3 25.3 %collective-permute-done.1 = bf16[384,1024]{1,0:T(8,128)(2,1)S(1)} collective-permute-done((bf16[384,1024]{1,0:T(8,128)(2,1)S(1)}, bf16[384,1024]{1,0:T(8,128)(2,1)S(1)}, u32[]{:S(2)}, u32[]{:S(2)}) %collective-permute-start.1) | collective-permute-done | bytes 786464 | tf_op jit(solution)/shard_map/ppermute | solution.py:206
  71.1 2.4 copy.53.dq_ref
  74.2 2.3 bitcast_dynamic-update-slice_fusion.15
  76.5 35.0 %collective-permute-done.2 = bf16[384,1024]{1,0:T(8,128)(2,1)} collective-permute-done((bf16[384,1024]{1,0:T(8,128)(2,1)S(1)}, bf16[384,1024]{1,0:T(8,128)(2,1)}, u32[]{:S(2)}, u32[]{:S(2)}) %collective-permute-start.2) | collective-permute-done | bytes 786464 | tf_op jit(solution)/shard_map/ppermute | solution.py:206
  112.5 2.0 collective-permute-start.6
  115.4 2.1 bitcast_dynamic-update-slice_fusion.12
  117.5 6.8 collective-permute-done.3
  128.6 6.5 gather_fusion
  135.1 6.1 broadcast_select_fusion.1
  141.1 3.5 slice.122
  144.7 2.7 copy-done.1
  149.0 4.8 fusion.129
  154.4 4.2 copy.52
  158.6 4.6 slice_bitcast_fusion
  163.3 78.4 %shard_map.154 = (bf16[2,3072,64]{2,1,0:T(8,128)(2,1)}, f32[2,3072,1]{2,1,0:T(8,128)}) custom-call(s32[12]{0:T(128)} %get-tuple-element.76.lo_ref, s32[12]{0:T(128)} %get-tuple-element.75.hi_ref, bf16[2,3072,64]{2,1,0:T(8,128)(2,1)} %get-tuple-element.60.q_ref, bf16[2,3072,64]{2,1,0:T(8,128)(2,1)} %get-tuple-element.59.k_ref, ...), custom_call_target="tpu_custom_call" | custom-call | tf_op jit(solution)/shard_map/pallas_call | solution.py:73
  241.7 4.0 copy.69
  247.1 8.1 %all-to-all-start = ((bf16[8,384,128]{2,1,0:T(8,128)(2,1)}), bf16[8,384,128]{2,1,0:T(8,128)(2,1)S(1)}, u32[]{:S(2)}, u32[]{:S(2)}) async-start(bf16[8,384,128]{2,1,0:T(8,128)(2,1)} %reshape.228), calls=%async_computation | async-start | bytes 1572864 | tf_op jit(solution)/shard_map/all_to_all | solution.py:278
  256.5 1.9 copy.54
  259.1 16.4 %all-to-all-done = bf16[8,384,128]{2,1,0:T(8,128)(2,1)S(1)} async-done(((bf16[8,384,128]{2,1,0:T(8,128)(2,1)}), bf16[8,384,128]{2,1,0:T(8,128)(2,1)S(1)}, u32[]{:S(2)}, u32[]{:S(2)}) %all-to-all-start) | async-done | bytes 786464 | tf_op jit(solution)/shard_map/all_to_all | solution.py:278
  275.4 2.9 fusion.126
  280.9 10.3 %fusion.122 = f32[384,4096]{1,0:T(8,128)} fusion(bf16[384,1024]{1,0:T(8,128)(2,1)} %fusion.45, bf16[8192,1024]{1,0:T(8,128)(2,1)} %all-gather.7.cloned.1.call-done), kind=kOutput, calls=%fused_computation.246 | convolution fusion | flops 3221225472 | bytes 15466496 | tf_op jit(solution)/shard_map/dot_general | solution.py:225
  292.1 19.2 %fusion.125 = (f32[384]{0:T(512)S(1)}, f32[384,1024]{1,0:T(8,128)S(1)}, f32[384,1024]{1,0:T(8,128)S(1)}) fusion(f32[1024]{0:T(1024)S(1)} %get-tuple-element.64, f32[1024]{0:T(1024)S(1)} %get-tuple-element.65, f32[1024]{0:T(1024)S(1)} %get-tuple-element.66, f32[384]{0:T(512)S(1)} %add_rsqrt_fusion.1, f32[384,1024]{1,0:T(8,128)S(1)} %get-tuple-element.51, ...), kind=kOutput, calls=%fused_computation.248 | convolution fusion | flops 3327786496 | bytes 19432960 | tf_op jit(solution)/shard_map/dot_general | solution.py:287
  312.6 2.6 pad_maximum_fusion.2
  315.2 3.1 slice.129
  318.2 43.2 %all-reduce.2 = (f32[4]{0:T(128)}, f32[]{:T(128)}) all-reduce(f32[4]{0:T(128)S(1)} %pad_maximum_fusion.2, f32[]{:T(128)} %fusion.51), channel_id=1, replica_groups=mesh['fsdp'=4,'seq'=8] {'fsdp','seq'}, use_global_device_ids=true, to_apply=%region_10.12 | all-reduce | flops 5 | bytes 40 | tf_op jit(solution)/shard_map/psum | solution.py:298
  363.3 3.0 convert_reduce_fusion.3
  366.3 8.8 %convert_reduce_fusion.1 = (f32[4096]{0:T(1024)S(1)}, bf16[384,4096]{1,0:T(8,128)(2,1)S(1)}) fusion(f32[384,4096]{1,0:T(8,128)} %fusion.122, f32[4096]{0:T(1024)S(1)} %slice.134, bf16[384,1024]{1,0:T(8,128)(2,1)} %get-tuple-element.45, bf16[8192,1024]{1,0:T(8,128)(2,1)} %all-gather.7.cloned.1.call-done), kind=kOutput, calls=%fused_computation.37 | convolution fusion | flops 3241668608 | bytes 18644992 | tf_op jit(solution)/shard_map/dot_general | solution.py:225
  375.1 7.5 multiply_reduce_fusion
  382.6 1.9 bitcast_dynamic-update-slice_fusion.7
  384.5 2.5 collective-permute-start.7
  389.2 5.2 all-to-all-start.1
  395.0 7.3 fusion.127
  403.6 8.6 %fusion.131 = f32[3072,512]{1,0:T(8,128)} fusion(bf16[3072,1024]{1,0:T(8,128)(2,1)} %all-gather.11.cloned.1.call-done, bf16[512,1024]{1,0:T(8,128)(2,1)S(1)} %bitcast.193), kind=kOutput, calls=%fused_computation.254 | convolution fusion | flops 3221225472 | bytes 13631488 | tf_op jit(solution)/shard_map/dot_general | solution.py:225
  412.1 2.1 collective-permute-start.8
  414.3 21.0 %all-to-all-done.1 = bf16[8,384,128]{1,2,0:T(8,128)(2,1)S(1)} async-done(((bf16[8,384,128]{1,2,0:T(8,128)(2,1)}), bf16[8,384,128]{1,2,0:T(8,128)(2,1)S(1)}, u32[]{:S(2)}, u32[]{:S(2)}) %all-to-all-start.1) | async-done | bytes 786464 | tf_op jit(solution)/shard_map/all_to_all | solution.py:362
  437.6 92.2 %shard_map.155 = (f32[2,3072,64]{2,1,0:T(8,128)}, f32[2,3072,64]{2,1,0:T(8,128)}, f32[2,3072,64]{2,1,0:T(8,128)}) custom-call(s32[12]{0:T(128)} %get-tuple-element.76.lo_ref, s32[12]{0:T(128)} %get-tuple-element.75.hi_ref, bf16[2,3072,64]{2,1,0:T(8,128)(2,1)} %get-tuple-element.60.q_ref, bf16[2,3072,64]{2,1,0:T(8,128)(2,1)} %get-tuple-element.59.k_ref, ...), custom_call_target="tpu_custom_call" | custom-call | tf_op jit(solution)/shard_map/pallas_call | solution.py:152
  529.8 5.8 convert_reduce_fusion
  535.8 4.8 copy.63
  540.6 5.6 fusion.130
  547.2 8.9 %collective-permute-start.9 = (bf16[384,1024]{1,0:T(8,128)(2,1)}, bf16[384,1024]{1,0:T(8,128)(2,1)}, u32[]{:S(2)}, u32[]{:S(2)}) collective-permute-start(bf16[384,1024]{1,0:T(8,128)(2,1)} %collective-permute-done.8), channel_id=1, source_target_pairs={{2,0},{4,2},{6,4},{7,6},{5,7},{3,5},{1,3},{0,1},{10,8},{12,10},{14... | collective-permute-start | bytes 2359304 | tf_op jit(solution)/shard_map/ppermute | solution.py:206
  556.3 2.8 copy.66
  559.1 3.6 all-to-all-start.3
  562.7 22.5 %collective-permute-done.9 = bf16[384,1024]{1,0:T(8,128)(2,1)} collective-permute-done((bf16[384,1024]{1,0:T(8,128)(2,1)}, bf16[384,1024]{1,0:T(8,128)(2,1)}, u32[]{:S(2)}, u32[]{:S(2)}) %collective-permute-start.9) | collective-permute-done | bytes 786464 | tf_op jit(solution)/shard_map/ppermute | solution.py:206
  585.3 2.5 collective-permute-start.10
  587.7 2.0 bitcast_dynamic-update-slice_fusion.6
  590.0 2.1 bitcast_dynamic-update-slice_fusion.5
  592.1 2.1 bitcast_dynamic-update-slice_fusion.4
  594.1 15.4 %collective-permute-done.10 = bf16[384,1024]{1,0:T(8,128)(2,1)S(1)} collective-permute-done((bf16[384,1024]{1,0:T(8,128)(2,1)}, bf16[384,1024]{1,0:T(8,128)(2,1)S(1)}, u32[]{:S(2)}, u32[]{:S(2)}) %collective-permute-start.10) | collective-permute-done | bytes 786464 | tf_op jit(solution)/shard_map/ppermute | solution.py:206
  612.4 2.1 bitcast_dynamic-update-slice_fusion
  614.4 6.5 gather_fusion.1
  620.9 3.5 broadcast_select_fusion
  626.8 2.6 pad_maximum_fusion.1
  629.6 15.8 %fusion.46 = f32[512,1024]{1,0:T(8,128)S(1)} fusion(bf16[3072,1024]{1,0:T(8,128)(2,1)} %all-gather.11.cloned.1.call-done, f32[3072,512]{1,0:T(8,128)} %fusion.131, bf16[3072,1024]{1,0:T(8,128)(2,1)} %all-gather.9.cloned.1.call-done, bf16[512,1024]{1,0:T(8,128)(2,1)} %bitcast.192, f32[512]{0:T(512)S(1)} %bitcast.206), kind=kOutput, calls=%fused_computation.106 | convolution fusion | flops 6459752448 | bytes 22022144 | tf_op jit(solution)/shard_map/dot_general | solution.py:219
  645.4 19.9 %fusion.32 = f32[512,1024]{1,0:T(8,128)S(1)} fusion(bf16[3072,1024]{1,0:T(8,128)(2,1)} %all-gather.9.cloned.1.call-done, f32[3072,512]{1,0:T(8,128)} %fusion.131, f32[512]{0:T(512)S(1)} %bitcast.207), kind=kOutput, calls=%fused_computation.60 | convolution fusion | flops 3325034496 | bytes 14682112 | tf_op jit(solution)/shard_map/dot_general | solution.py:219
  665.3 2.4 pad_maximum_fusion
  667.7 4.8 copy.60
  674.7 13.3 %all-to-all-start.2 = ((bf16[8,384,384]{1,2,0:T(8,128)(2,1)}), bf16[8,384,384]{1,2,0:T(8,128)(2,1)S(1)}, u32[]{:S(2)}, u32[]{:S(2)}) async-start(bf16[8,384,384]{1,2,0:T(8,128)(2,1)} %copy.61), calls=%async_computation.2 | async-start | bytes 4718592 | tf_op jit(solution)/shard_map/all_to_all | solution.py:410
  689.1 48.8 %all-to-all-done.2 = bf16[8,384,384]{1,2,0:T(8,128)(2,1)S(1)} async-done(((bf16[8,384,384]{1,2,0:T(8,128)(2,1)}), bf16[8,384,384]{1,2,0:T(8,128)(2,1)S(1)}, u32[]{:S(2)}, u32[]{:S(2)}) %all-to-all-start.2) | async-done | bytes 2359328 | tf_op jit(solution)/shard_map/all_to_all | solution.py:410
  737.9 2.8 copy.62
  740.8 3.6 reshape.179
  744.4 7.0 bitcast_add_fusion
  752.7 1.9 slice_bitcast_fusion.3
  (137 shorter events, 48.5 us)
Async XLA Ops:
  7.2 134.0 %all-gather.13.cloned.1.call-start = ((), (), s32[]{:S(2)}) async-start(), calls=%async_computation.11 | async-start | bytes 9191424 | tf_op jit(solution)/shard_map/all_gather | solution.py:241
  9.6 271.3 %all-gather.7.cloned.1.call-start = ((), (), s32[]{:S(2)}) async-start(), calls=%async_computation.6 | async-start | bytes 17301504 | tf_op jit(solution)/shard_map/all_gather | solution.py:244
  10.4 26.0 %collective-permute-start = (bf16[384,1024]{1,0:T(8,128)(2,1)}, bf16[384,1024]{1,0:T(8,128)(2,1)S(1)}, u32[]{:S(2)}, u32[]{:S(2)}) collective-permute-start(bf16[384,1024]{1,0:T(8,128)(2,1)} %param.13), channel_id=1, source_target_pairs={{2,0},{4,2},{6,4},{7,6},{5,7},{3,5},{1,3},{0,1},{10,8},{12,10},{14... | collective-permute-start | bytes 2359304 | tf_op jit(solution)/shard_map/ppermute | solution.py:206
  36.3 31.3 %collective-permute-start.1 = (bf16[384,1024]{1,0:T(8,128)(2,1)S(1)}, bf16[384,1024]{1,0:T(8,128)(2,1)S(1)}, u32[]{:S(2)}, u32[]{:S(2)}) collective-permute-start(bf16[384,1024]{1,0:T(8,128)(2,1)S(1)} %collective-permute-done), channel_id=1, source_target_pairs={{2,0},{4,2},{6,4},{7,6},{5,7},{3,5},{1,3},{0,1},{10,8},{12,10},{14... | collective-permute-start | bytes 2359304 | tf_op jit(solution)/shard_map/ppermute | solution.py:206
  38.0 31.3 %collective-permute-start.4 = (bf16[384,1024]{1,0:T(8,128)(2,1)}, bf16[384,1024]{1,0:T(8,128)(2,1)S(1)}, u32[]{:S(2)}, u32[]{:S(2)}) collective-permute-start(bf16[384,1024]{1,0:T(8,128)(2,1)} %param.13), channel_id=1, source_target_pairs={{0,2},{2,4},{4,6},{6,7},{7,5},{5,3},{3,1},{1,0},{8,10},{10,12},{12... | collective-permute-start | bytes 2359304 | tf_op jit(solution)/shard_map/ppermute | solution.py:202
  67.6 43.9 %collective-permute-start.2 = (bf16[384,1024]{1,0:T(8,128)(2,1)S(1)}, bf16[384,1024]{1,0:T(8,128)(2,1)}, u32[]{:S(2)}, u32[]{:S(2)}) collective-permute-start(bf16[384,1024]{1,0:T(8,128)(2,1)S(1)} %collective-permute-done.1), channel_id=1, source_target_pairs={{2,0},{4,2},{6,4},{7,6},{5,7},{3,5},{1,3},{0,1},{10,8},{12,10},{14... | collective-permute-start | bytes 2359304 | tf_op jit(solution)/shard_map/ppermute | solution.py:206
  69.3 65.7 %copy-start.7 = (pred[8]{0:T(512)(128)(4,1)}, pred[8]{0:T(512)(128)(4,1)S(1)}, u32[]{:S(2)}) copy-start(pred[8]{0:T(512)(128)(4,1)S(1)} %get-tuple-element.52) | copy-start | bytes 28
  69.4 43.1 %collective-permute-start.5 = (bf16[384,1024]{1,0:T(8,128)(2,1)S(1)}, bf16[384,1024]{1,0:T(8,128)(2,1)S(1)}, u32[]{:S(2)}, u32[]{:S(2)}) collective-permute-start(bf16[384,1024]{1,0:T(8,128)(2,1)S(1)} %collective-permute-done.4), channel_id=1, source_target_pairs={{0,2},{2,4},{4,6},{6,7},{7,5},{5,3},{3,1},{1,0},{8,10},{10,12},{12... | collective-permute-start | bytes 2359304 | tf_op jit(solution)/shard_map/ppermute | solution.py:202
  71.1 57.5 %copy-start.6 = (s32[1024]{0:T(1024)}, s32[1024]{0:T(1024)S(1)}, u32[]{:S(2)}) copy-start(s32[1024]{0:T(1024)S(1)} %pad_clamp_fusion) | copy-start | bytes 12292
  111.5 12.7 %collective-permute-start.3 = (bf16[384,1024]{1,0:T(8,128)(2,1)}, bf16[384,1024]{1,0:T(8,128)(2,1)S(1)}, u32[]{:S(2)}, u32[]{:S(2)}) collective-permute-start(bf16[384,1024]{1,0:T(8,128)(2,1)} %collective-permute-done.2), channel_id=1, source_target_pairs={{2,0},{4,2},{6,4},{7,6},{5,7},{3,5},{1,3},{0,1},{10,8},{12,10},{14... | collective-permute-start | bytes 2359304 | tf_op jit(solution)/shard_map/ppermute | solution.py:206
  112.5 13.2 %collective-permute-start.6 = (bf16[384,1024]{1,0:T(8,128)(2,1)S(1)}, bf16[384,1024]{1,0:T(8,128)(2,1)S(1)}, u32[]{:S(2)}, u32[]{:S(2)}) collective-permute-start(bf16[384,1024]{1,0:T(8,128)(2,1)S(1)} %collective-permute-done.5), channel_id=1, source_target_pairs={{0,2},{2,4},{4,6},{6,7},{7,5},{5,3},{3,1},{1,0},{8,10},{10,12},{12... | collective-permute-start | bytes 2359304 | tf_op jit(solution)/shard_map/ppermute | solution.py:202
  144.7 2.7 copy-start.1
  241.7 14.9 %copy-start.3 = (bf16[2,3072,64]{2,1,0:T(8,128)(2,1)S(1)}, bf16[2,3072,64]{2,1,0:T(8,128)(2,1)}, u32[]{:S(2)}) copy-start(bf16[2,3072,64]{2,1,0:T(8,128)(2,1)} %get-tuple-element.15) | copy-start | bytes 2359300
  247.1 28.3 %all-to-all-start = ((bf16[8,384,128]{2,1,0:T(8,128)(2,1)}), bf16[8,384,128]{2,1,0:T(8,128)(2,1)S(1)}, u32[]{:S(2)}, u32[]{:S(2)}) async-start(bf16[8,384,128]{2,1,0:T(8,128)(2,1)} %reshape.228), calls=%async_computation | async-start | bytes 1572864 | tf_op jit(solution)/shard_map/all_to_all | solution.py:278
  255.2 148.3 %all-gather.11.cloned.1.call-start = ((), (), s32[]{:S(2)}) async-start(), calls=%async_computation.9 | async-start | bytes 7077888 | tf_op jit(solution)/shard_map/all_gather | solution.py:284
  280.9 11.1 %copy-start = (bf16[8192,1024]{1,0:T(8,128)(2,1)S(1)}, bf16[8192,1024]{1,0:T(8,128)(2,1)}, u32[]{:S(2)}) copy-start(bf16[8192,1024]{1,0:T(8,128)(2,1)} %all-gather.7.cloned.1.call-done) | copy-start | bytes 50331652
  366.3 8.8 %copy-start.4 = (bf16[384,1024]{1,0:T(8,128)(2,1)S(1)}, bf16[384,1024]{1,0:T(8,128)(2,1)}, u32[]{:S(2)}) copy-start(bf16[384,1024]{1,0:T(8,128)(2,1)} %param.14) | copy-start | bytes 2359300
  382.6 4.4 copy-start.5
  384.5 27.6 %collective-permute-start.7 = (bf16[384,1024]{1,0:T(8,128)(2,1)S(1)}, bf16[384,1024]{1,0:T(8,128)(2,1)}, u32[]{:S(2)}, u32[]{:S(2)}) collective-permute-start(bf16[384,1024]{1,0:T(8,128)(2,1)S(1)} %get-tuple-element.42), channel_id=1, source_target_pairs={{2,0},{4,2},{6,4},{7,6},{5,7},{3,5},{1,3},{0,1},{10,8},{12,10},{14... | collective-permute-start | bytes 2359304 | tf_op jit(solution)/shard_map/ppermute | solution.py:206
  387.0 27.2 %collective-permute-start.11 = (bf16[384,1024]{1,0:T(8,128)(2,1)S(1)}, bf16[384,1024]{1,0:T(8,128)(2,1)}, u32[]{:S(2)}, u32[]{:S(2)}) collective-permute-start(bf16[384,1024]{1,0:T(8,128)(2,1)S(1)} %get-tuple-element.42), channel_id=1, source_target_pairs={{0,2},{2,4},{4,6},{6,7},{7,5},{5,3},{3,1},{1,0},{8,10},{10,12},{12... | collective-permute-start | bytes 2359304 | tf_op jit(solution)/shard_map/ppermute | solution.py:202
  389.2 46.0 %all-to-all-start.1 = ((bf16[8,384,128]{1,2,0:T(8,128)(2,1)}), bf16[8,384,128]{1,2,0:T(8,128)(2,1)S(1)}, u32[]{:S(2)}, u32[]{:S(2)}) async-start(bf16[8,384,128]{1,2,0:T(8,128)(2,1)} %bitcast.35), calls=%async_computation.1 | async-start | bytes 1572864 | tf_op jit(solution)/shard_map/all_to_all | solution.py:362
  394.4 235.1 %all-gather.9.cloned.1.call-start = ((), (), s32[]{:S(2)}) async-start(), calls=%async_computation.8 | async-start | bytes 7077888 | tf_op jit(solution)/shard_map/all_gather | solution.py:323
  412.1 135.1 %collective-permute-start.8 = (bf16[384,1024]{1,0:T(8,128)(2,1)}, bf16[384,1024]{1,0:T(8,128)(2,1)}, u32[]{:S(2)}, u32[]{:S(2)}) collective-permute-start(bf16[384,1024]{1,0:T(8,128)(2,1)} %collective-permute-done.7), channel_id=1, source_target_pairs={{2,0},{4,2},{6,4},{7,6},{5,7},{3,5},{1,3},{0,1},{10,8},{12,10},{14... | collective-permute-start | bytes 2359304 | tf_op jit(solution)/shard_map/ppermute | solution.py:206
  414.2 175.6 %collective-permute-start.12 = (bf16[384,1024]{1,0:T(8,128)(2,1)}, bf16[384,1024]{1,0:T(8,128)(2,1)S(1)}, u32[]{:S(2)}, u32[]{:S(2)}) collective-permute-start(bf16[384,1024]{1,0:T(8,128)(2,1)} %collective-permute-done.11), channel_id=1, source_target_pairs={{0,2},{2,4},{4,6},{6,7},{7,5},{5,3},{3,1},{1,0},{8,10},{10,12},{12... | collective-permute-start | bytes 2359304 | tf_op jit(solution)/shard_map/ppermute | solution.py:202
  547.2 38.1 %collective-permute-start.9 = (bf16[384,1024]{1,0:T(8,128)(2,1)}, bf16[384,1024]{1,0:T(8,128)(2,1)}, u32[]{:S(2)}, u32[]{:S(2)}) collective-permute-start(bf16[384,1024]{1,0:T(8,128)(2,1)} %collective-permute-done.8), channel_id=1, source_target_pairs={{2,0},{4,2},{6,4},{7,6},{5,7},{3,5},{1,3},{0,1},{10,8},{12,10},{14... | collective-permute-start | bytes 2359304 | tf_op jit(solution)/shard_map/ppermute | solution.py:206
  559.1 67.2 %all-to-all-start.3 = ((f32[8,1,50688]{2,1,0:T(1,128)}), f32[8,1,50688]{2,1,0:T(1,128)S(1)}, u32[]{:S(2)}, u32[]{:S(2)}) async-start(f32[8,1,50688]{2,1,0:T(1,128)} %copy.66), calls=%async_computation.3 | async-start | bytes 3244032 | tf_op jit(solution)/shard_map/all_to_all | solution.py:400
  562.7 188.7 %reduce-scatter.3.cloned.1.call-start = ((), (), s32[]{:S(2)}) async-start(), calls=%async_computation.7 | async-start | bytes 2785280 | tf_op jit(solution)/shard_map/reduce_scatter | solution.py:215
  585.3 24.2 %collective-permute-start.10 = (bf16[384,1024]{1,0:T(8,128)(2,1)}, bf16[384,1024]{1,0:T(8,128)(2,1)S(1)}, u32[]{:S(2)}, u32[]{:S(2)}) collective-permute-start(bf16[384,1024]{1,0:T(8,128)(2,1)} %collective-permute-done.9), channel_id=1, source_target_pairs={{2,0},{4,2},{6,4},{7,6},{5,7},{3,5},{1,3},{0,1},{10,8},{12,10},{14... | collective-permute-start | bytes 2359304 | tf_op jit(solution)/shard_map/ppermute | solution.py:206
  589.8 20.7 %collective-permute-start.13 = (bf16[384,1024]{1,0:T(8,128)(2,1)S(1)}, bf16[384,1024]{1,0:T(8,128)(2,1)S(1)}, u32[]{:S(2)}, u32[]{:S(2)}) collective-permute-start(bf16[384,1024]{1,0:T(8,128)(2,1)S(1)} %collective-permute-done.12), channel_id=1, source_target_pairs={{0,2},{2,4},{4,6},{6,7},{7,5},{5,3},{3,1},{1,0},{8,10},{10,12},{12... | collective-permute-start | bytes 2359304 | tf_op jit(solution)/shard_map/ppermute | solution.py:202
  614.4 6.5 copy-start.8
  620.9 3.5 copy-start.2
  626.4 3.2 copy-start.9
  629.5 125.1 %reduce-scatter.5.cloned.1.call-start = ((), (), s32[]{:S(2)}) async-start(), calls=%async_computation.10 | async-start | bytes 5242880 | tf_op jit(solution)/shard_map/reduce_scatter | solution.py:337
  672.5 16.1 %copy-start.10 = (f32[4]{0:T(128)S(1)}, f32[4]{0:T(128)}, u32[]{:S(2)}) copy-start(f32[4]{0:T(128)} %get-tuple-element.21) | copy-start | bytes 52
  674.7 63.2 %all-to-all-start.2 = ((bf16[8,384,384]{1,2,0:T(8,128)(2,1)}), bf16[8,384,384]{1,2,0:T(8,128)(2,1)S(1)}, u32[]{:S(2)}, u32[]{:S(2)}) async-start(bf16[8,384,384]{1,2,0:T(8,128)(2,1)} %copy.61), calls=%async_computation.2 | async-start | bytes 4718592 | tf_op jit(solution)/shard_map/all_to_all | solution.py:410
Sparse Core Ops, SparseCore 0:
  11.5 104.1 all-gather.12
  118.7 118.4 all-gather.6
  281.0 97.4 all-gather.10
  397.1 122.6 all-gather.8
  629.6 39.1 reduce-scatter.2
  671.7 48.1 reduce-scatter.4

commit v9 on v7

--- a/solution.py
+++ b/solution.py
@@ -10,7 +10,7 @@
 
 H = 16
 
-BLOCK = 256
+BLOCK = 512
 NEG = -1e30
 
 
@@ -27,34 +27,36 @@
     return jnp.where(doc_q == doc_k, s, NEG)
 
 
-def _fwd_kernel(lo_ref, hi_ref, q_ref, k_ref, v_ref, dq_ref, dk_ref, out_ref, lse_ref, *, scale, block):
+def _fwd_kernel(lo_ref, hi_ref, q_ref, k_ref, v_ref, dq_ref, dk_ref, out_ref, lse_ref, s_buf,
+                *, scale, block):
     i = pl.program_id(1)
     lo = lo_ref[i]
     hi = hi_ref[i]
     q = q_ref[...]
     doc_q = dq_ref[...]
-
-    def pass_one(kb, carry):
-        m, l = carry
+    rows = q.shape[0]
+
+    def pass_one(kb, m):
         start = pl.multiple_of(kb * block, block)
         s = _scores(q, k_ref[pl.ds(start, block), :], doc_q, dk_ref[:, pl.ds(start, block)], scale)
-        m_new = jnp.maximum(m, jnp.max(s, axis=1, keepdims=True))
-        l = l * jnp.exp(m - m_new) + jnp.sum(jnp.exp(s - m_new), axis=1, keepdims=True)
-        return m_new, l
-
-    rows = q.shape[0]
-    m, l = lax.fori_loop(
-        lo, hi, pass_one,
-        (jnp.full((rows, 1), NEG, jnp.float32), jnp.zeros((rows, 1), jnp.float32)),
-    )
-
-    def pass_two(kb, acc):
+        s_buf[kb - lo] = s
+        return jnp.maximum(m, jnp.max(s, axis=1, keepdims=True))
+
+    m = lax.fori_loop(lo, hi, pass_one, jnp.full((rows, 1), NEG, jnp.float32))
+
+    def pass_two(kb, l):
+        e = jnp.exp(s_buf[kb - lo] - m)
+        s_buf[kb - lo] = e
+        return l + jnp.sum(e, axis=1, keepdims=True)
+
+    l = lax.fori_loop(lo, hi, pass_two, jnp.zeros((rows, 1), jnp.float32))
+
+    def pass_three(kb, acc):
         start = pl.multiple_of(kb * block, block)
-        s = _scores(q, k_ref[pl.ds(start, block), :], doc_q, dk_ref[:, pl.ds(start, block)], scale)
-        p = (jnp.exp(s - m) / l).astype(jnp.bfloat16)
+        p = (s_buf[kb - lo] / l).astype(jnp.bfloat16)
         return acc + jnp.dot(p, v_ref[pl.ds(start, block), :], preferred_element_type=jnp.float32)
 
-    acc = lax.fori_loop(lo, hi, pass_two, jnp.zeros(out_ref.shape, jnp.float32))
+    acc = lax.fori_loop(lo, hi, pass_three, jnp.zeros(out_ref.shape, jnp.float32))
     out_ref[...] = acc.astype(out_ref.dtype)
     lse_ref[...] = m + jnp.log(l)
 
@@ -77,6 +79,7 @@
             grid=grid,
             in_specs=[spec_q, spec_kv, spec_kv, spec_dq, spec_dk],
             out_specs=[spec_q, spec_lse],
+            scratch_shapes=[pltpu.VMEM((seg_len // block, block, block), jnp.float32)],
         ),
         out_shape=[
             jax.ShapeDtypeStruct((heads, seg_len, d), jnp.bfloat16),
@@ -87,7 +90,7 @@
 
 
 def _bwd_kernel(lo_ref, hi_ref, q_ref, k_ref, v_ref, da_ref, lse_ref, dq_ref, dk_ref,
-                gq_ref, gk_ref, gv_ref, *, scale, block):
+                gq_ref, gk_ref, gv_ref, p_buf, dp_buf, *, scale, block):
     i = pl.program_id(1)
     lo = lo_ref[i]
     hi = hi_ref[i]
@@ -101,29 +104,26 @@
     da = da_ref[...]
     lse = lse_ref[...]
     doc_q = dq_ref[...]
-
-    def probs(start):
+    rows = q.shape[0]
+
+    def pass_one(kb, delta):
+        start = pl.multiple_of(kb * block, block)
         s = _scores(q, k_ref[pl.ds(start, block), :], doc_q, dk_ref[:, pl.ds(start, block)], scale)
         p = jnp.exp(s - lse)
         dp = lax.dot_general(da, v_ref[pl.ds(start, block), :], (((1,), (1,)), ((), ())),
                              preferred_element_type=jnp.float32)
-        return p, dp
-
-    def pass_one(kb, delta):
-        start = pl.multiple_of(kb * block, block)
-        p, dp = probs(start)
+        p_buf[kb - lo] = p
+        dp_buf[kb - lo] = dp
         return delta + jnp.sum(dp * p, axis=1, keepdims=True)
 
-    rows = q.shape[0]
     delta = lax.fori_loop(lo, hi, pass_one, jnp.zeros((rows, 1), jnp.float32))
 
     def pass_two(kb, gq):
         start = pl.multiple_of(kb * block, block)
-        p, dp = probs(start)
-        ds = (p * (dp - delta)).astype(jnp.bfloat16)
+        p = p_buf[kb - lo]
+        ds = (p * (dp_buf[kb - lo] - delta)).astype(jnp.bfloat16)
         pb = p.astype(jnp.bfloat16)
-        k_blk = k_ref[pl.ds(start, block), :]
-        gq = gq + jnp.dot(ds, k_blk, preferred_element_type=jnp.float32)
+        gq = gq + jnp.dot(ds, k_ref[pl.ds(start, block), :], preferred_element_type=jnp.float32)
         gk_ref[pl.ds(start, block), :] += lax.dot_general(
             ds, q, (((0,), (0,)), ((), ())), preferred_element_type=jnp.float32)
         gv_ref[pl.ds(start, block), :] += lax.dot_general(
@@ -156,6 +156,7 @@
             grid=grid,
             in_specs=[spec_q, spec_kv, spec_kv, spec_q, spec_lse, spec_dq, spec_dk],
             out_specs=[spec_q, spec_kv, spec_kv],
+            scratch_shapes=[pltpu.VMEM((seg_len // block, block, block), jnp.float32)] * 2,
         ),
         out_shape=[jax.ShapeDtypeStruct((heads, seg_len, d), jnp.float32)] * 3,
         compiler_params=pltpu.CompilerParams(dimension_semantics=("arbitrary", "arbitrary")),

time: 766 us -> 730 us (0.953)
  Pallas kernels: 171 us -> 91 us
  waiting for transfers between devices: 249 us -> 294 us
    pallas_call x1, Pallas kernels: 92.2 us -> 51.6 us  [attn_backward(): pl.pallas_call(functools.partial(_bwd_kernel, scale=scale, block=block),...]
    pallas_call x1, Pallas kernels: 78.5 us -> 39.4 us  [attn_forward(): pl.pallas_call(functools.partial(_fwd_kernel, scale=scale, block=block),...]
    all_gather x1, waiting for transfers between devices: 0.02 us -> 30.3 us  [layer_body(): grad_mlp_seg = lax.all_gather(grad_mlp_low, 'seq', axis=0, tiled=True)]
    all_to_all x1, waiting for transfers between devices: 19.1 us -> 32 us  [layer_body(): lax.all_to_all(mixed_rows, 'seq', split_axis=0, concat_axis=0, tiled=True)]
  transfers between devices with their start and end apart: 18 -> 18, of which waited for: 9 -> 10; matrix products, arithmetic and copies ran while one was open for 31% -> 33% of each run, Pallas kernels for 23% -> 13%
where the time goes in v9:
time: 730 us; the launch traced here: 720 us
  waiting for transfers between devices  294 us (40%)
  matrix products  115 us (16%)
  Pallas kernels  91 us (12%)
  local copies, waits for them, and re-layouts  85.7 us (12%)
  other arithmetic  43.2 us (6%)
  blocking collectives  42.5 us (6%)
  starting transfers between devices  32.5 us (4%)
  between operations  16.4 us (2%)
    ppermute x4, waiting for transfers between devices, ring_gather(): moving = lax.ppermute(moving, 'seq', backward_pairs)  90.1 us
    all_to_all x1, waiting for transfers between devices, layer_body(): lax.all_to_all(jnp.concatenate([row_part.reshape(seq_count, -1), vector_p...  54.3 us
    all_to_all x1, waiting for transfers between devices, layer_body(): lax.all_to_all(head_grads.reshape(seq_count, tokens, 3 * head_width), 'se...  52.8 us
    pallas_call x1, Pallas kernels, attn_backward(): pl.pallas_call(functools.partial(_bwd_kernel, scale=scale, block=block),...  51.6 us
    psum x1, blocking collectives, layer_body(): lax.psum((squares, jnp.sum(valid_rows)), ('fsdp', 'seq'))  42.5 us
    dot_general x3, matrix products, contract_rows(): lax.dot_general(left, right, (((0,), (0,)), ((), ())), preferred_element_...  39.4 us
    pallas_call x1, Pallas kernels, attn_forward(): pl.pallas_call(functools.partial(_fwd_kernel, scale=scale, block=block),...  39.4 us
    all_to_all x1, waiting for transfers between devices, layer_body(): lax.all_to_all(grad_split, 'seq', split_axis=0, concat_axis=0, tiled=True)  32.9 us
  transfers between devices with their start and end apart: 18, of which 10 were waited for; matrix products, arithmetic and copies ran while one was open for 33% of the time, Pallas kernels for 13%

profile of v9, /device:TPU:0, one launch (start us, length us, event | category | flops | bytes accessed | tf_op | source)
XLA Modules:
  0.0 720.2 jit_solution(384541307275939478)
XLA Ops:
  7.9 1.7 maximum_bitcast_fusion.1
  10.4 3.0 collective-permute-start
  13.4 22.9 %collective-permute-done = bf16[384,1024]{1,0:T(8,128)(2,1)S(1)} collective-permute-done((bf16[384,1024]{1,0:T(8,128)(2,1)}, bf16[384,1024]{1,0:T(8,128)(2,1)S(1)}, u32[]{:S(2)}, u32[]{:S(2)}) %collective-permute-start) | collective-permute-done | bytes 786464 | tf_op jit(solution)/shard_map/ppermute | solution.py:207
  36.3 1.7 collective-permute-start.1
  42.3 25.3 %collective-permute-done.1 = bf16[384,1024]{1,0:T(8,128)(2,1)S(1)} collective-permute-done((bf16[384,1024]{1,0:T(8,128)(2,1)S(1)}, bf16[384,1024]{1,0:T(8,128)(2,1)S(1)}, u32[]{:S(2)}, u32[]{:S(2)}) %collective-permute-start.1) | collective-permute-done | bytes 786464 | tf_op jit(solution)/shard_map/ppermute | solution.py:207
  69.4 1.7 collective-permute-start.5
  71.2 2.4 copy.51.dq_ref
  74.2 2.2 bitcast_dynamic-update-slice_fusion.7
  76.4 35.1 %collective-permute-done.2 = bf16[384,1024]{1,0:T(8,128)(2,1)} collective-permute-done((bf16[384,1024]{1,0:T(8,128)(2,1)S(1)}, bf16[384,1024]{1,0:T(8,128)(2,1)}, u32[]{:S(2)}, u32[]{:S(2)}) %collective-permute-start.2) | collective-permute-done | bytes 786464 | tf_op jit(solution)/shard_map/ppermute | solution.py:207
  112.5 2.0 collective-permute-start.6
  115.4 2.1 bitcast_dynamic-update-slice_fusion.4
  117.5 6.8 collective-permute-done.3
  128.5 6.5 gather_fusion
  135.0 6.6 bitcast_select_fusion
  141.6 3.5 slice.120
  145.2 2.6 copy-done.1
  149.5 4.8 fusion.133
  154.9 4.1 copy.50
  159.0 4.7 slice_bitcast_fusion
  163.7 39.4 %shard_map.136 = (bf16[2,3072,64]{2,1,0:T(8,128)(2,1)}, f32[2,3072,1]{2,1,0:T(8,128)}) custom-call(s32[6]{0:T(128)} %get-tuple-element.74.lo_ref, s32[6]{0:T(128)} %get-tuple-element.73.hi_ref, bf16[2,3072,64]{2,1,0:T(8,128)(2,1)} %get-tuple-element.58.q_ref, bf16[2,3072,64]{2,1,0:T(8,128)(2,1)} %get-tuple-element.57.k_ref, ...), custom_call_target="tpu_custom_call" | custom-call | tf_op jit(solution)/shard_map/pallas_call | solution.py:75
  203.1 3.9 copy.67
  207.0 1.5 reshape.248
  208.4 7.9 %all-to-all-start = ((bf16[8,384,128]{2,1,0:T(8,128)(2,1)}), bf16[8,384,128]{2,1,0:T(8,128)(2,1)S(1)}, u32[]{:S(2)}, u32[]{:S(2)}) async-start(bf16[8,384,128]{2,1,0:T(8,128)(2,1)} %reshape.248), calls=%async_computation | async-start | bytes 1572864 | tf_op jit(solution)/shard_map/all_to_all | solution.py:279
  217.7 32.0 %all-to-all-done = bf16[8,384,128]{2,1,0:T(8,128)(2,1)S(1)} async-done(((bf16[8,384,128]{2,1,0:T(8,128)(2,1)}), bf16[8,384,128]{2,1,0:T(8,128)(2,1)S(1)}, u32[]{:S(2)}, u32[]{:S(2)}) %all-to-all-start) | async-done | bytes 786464 | tf_op jit(solution)/shard_map/all_to_all | solution.py:279
  249.7 3.0 fusion.130
  252.8 1.3 fusion.40
  255.6 10.2 %fusion.126 = f32[384,4096]{1,0:T(8,128)} fusion(bf16[384,1024]{1,0:T(8,128)(2,1)} %fusion.45, bf16[8192,1024]{1,0:T(8,128)(2,1)} %all-gather.7.cloned.1.call-done), kind=kOutput, calls=%fused_computation.241 | convolution fusion | flops 3221225472 | bytes 15466496 | tf_op jit(solution)/shard_map/dot_general | solution.py:226
  266.5 19.2 %fusion.129 = (f32[384]{0:T(512)S(1)}, f32[384,1024]{1,0:T(8,128)S(1)}, f32[384,1024]{1,0:T(8,128)S(1)}) fusion(f32[1024]{0:T(1024)S(1)} %get-tuple-element.62, f32[1024]{0:T(1024)S(1)} %get-tuple-element.63, f32[1024]{0:T(1024)S(1)} %get-tuple-element.64, f32[384]{0:T(512)S(1)} %add_rsqrt_fusion.1, f32[384,1024]{1,0:T(8,128)S(1)} %get-tuple-element.49, ...), kind=kOutput, calls=%fused_computation.243 | convolution fusion | flops 3327786496 | bytes 19432960 | tf_op jit(solution)/shard_map/dot_general | solution.py:288
  285.7 1.4 fusion.42
  287.1 2.7 pad_maximum_fusion.2
  289.8 2.3 copy.65
  292.1 42.5 %all-reduce.2 = (f32[4]{0:T(128)}, f32[]{:T(128)}) all-reduce(f32[4]{0:T(128)S(1)} %pad_maximum_fusion.2, f32[]{:T(128)} %fusion.52), channel_id=1, replica_groups=mesh['fsdp'=4,'seq'=8] {'fsdp','seq'}, use_global_device_ids=true, to_apply=%region_10.11 | all-reduce | flops 5 | bytes 40 | tf_op jit(solution)/shard_map/psum | solution.py:299
  334.6 1.9 fusion.44
  336.5 3.0 convert_reduce_fusion.3
  339.5 8.8 %convert_reduce_fusion.1 = (f32[4096]{0:T(1024)S(1)}, bf16[384,4096]{1,0:T(8,128)(2,1)S(1)}) fusion(f32[384,4096]{1,0:T(8,128)} %fusion.126, f32[4096]{0:T(1024)S(1)} %slice.132, bf16[384,1024]{1,0:T(8,128)(2,1)} %get-tuple-element.41, bf16[8192,1024]{1,0:T(8,128)(2,1)} %all-gather.7.cloned.1.call-done), kind=kOutput, calls=%fused_computation.37 | convolution fusion | flops 3241668608 | bytes 18644992 | tf_op jit(solution)/shard_map/dot_general | solution.py:226
  348.4 7.5 %multiply_reduce_fusion = (f32[1024]{0:T(1024)S(1)}, f32[384]{0:T(512)S(1)}, f32[384]{0:T(512)S(1)}, f32[1024]{0:T(1024)S(1)}, f32[384,1024]{1,0:T(8,128)S(1)}) fusion(f32[384,1024]{1,0:T(8,128)S(1)} %get-tuple-element.49, f32[384]{0:T(512)S(1)} %add_rsqrt_fusion.1, f32[384]{0:T(512)S(1)} %broadcast_multiply_fusion.5, f32[1024]{0:T(1024)S(1)} %get-tuple-element.64, ...), kind=kOutput, calls=%fused_computation.89 | convolution fusion | flops 3228300288 | bytes 17068032 | tf_op jit(solution)/shard_map/dot_general | solution.py:312
  356.4 3.2 convolution_bitcast_fusion
  359.7 1.8 slice.127
  363.7 6.8 all-to-all-start.1
  370.7 6.0 broadcast_select_fusion
  376.8 32.9 %all-to-all-done.1 = bf16[8,384,128]{1,2,0:T(8,128)(2,1)S(1)} async-done(((bf16[8,384,128]{1,2,0:T(8,128)(2,1)}), bf16[8,384,128]{1,2,0:T(8,128)(2,1)S(1)}, u32[]{:S(2)}, u32[]{:S(2)}) %all-to-all-start.1) | async-done | bytes 786464 | tf_op jit(solution)/shard_map/all_to_all | solution.py:358
  410.5 1.5 copy.56
  412.1 51.6 %shard_map.137 = (f32[2,3072,64]{2,1,0:T(8,128)}, f32[2,3072,64]{2,1,0:T(8,128)}, f32[2,3072,64]{2,1,0:T(8,128)}) custom-call(s32[6]{0:T(128)} %get-tuple-element.74.lo_ref, s32[6]{0:T(128)} %get-tuple-element.73.hi_ref, bf16[2,3072,64]{2,1,0:T(8,128)(2,1)} %get-tuple-element.58.q_ref, bf16[2,3072,64]{2,1,0:T(8,128)(2,1)} %get-tuple-element.57.k_ref, ...), custom_call_target="tpu_custom_call" | custom-call | tf_op jit(solution)/shard_map/pallas_call | solution.py:152
  463.7 5.9 convert_reduce_fusion
  469.7 4.8 copy.61
  474.5 5.9 fusion.134
  481.6 2.8 copy.64
  484.4 3.6 all-to-all-start.3
  488.3 6.9 fusion.131
  496.3 8.3 %fusion.135 = f32[3072,512]{1,0:T(8,128)} fusion(bf16[3072,1024]{1,0:T(8,128)(2,1)} %all-gather.11.cloned.1.call-done, bf16[512,1024]{1,0:T(8,128)(2,1)S(1)} %bitcast.182), kind=kOutput, calls=%fused_computation.249 | convolution fusion | flops 3221225472 | bytes 13631488 | tf_op jit(solution)/shard_map/dot_general | solution.py:226
  504.6 54.3 %all-to-all-done.3 = f32[8,1,50688]{2,1,0:T(1,128)S(1)} async-done(((f32[8,1,50688]{2,1,0:T(1,128)}), f32[8,1,50688]{2,1,0:T(1,128)S(1)}, u32[]{:S(2)}, u32[]{:S(2)}) %all-to-all-start.3) | async-done | bytes 1622048 | tf_op jit(solution)/shard_map/all_to_all | solution.py:396
  559.5 2.6 pad_maximum_fusion.1
  562.1 30.3 %all-gather.9.cloned.1.call-done = bf16[3072,1024]{1,0:T(8,128)(2,1)} async-done(((bf16[384,1024]{1,0:T(8,128)(2,1)}), bf16[3072,1024]{1,0:T(8,128)(2,1)}) %all-gather.9.cloned.1.call-update) | async-done | bytes 6291472 | tf_op jit(solution)/shard_map/all_gather | solution.py:324
  592.5 16.0 %fusion.46 = f32[512,1024]{1,0:T(8,128)S(1)} fusion(bf16[3072,1024]{1,0:T(8,128)(2,1)} %all-gather.11.cloned.1.call-done, f32[3072,512]{1,0:T(8,128)} %fusion.135, bf16[3072,1024]{1,0:T(8,128)(2,1)} %all-gather.9.cloned.1.call-done, bf16[512,1024]{1,0:T(8,128)(2,1)} %bitcast.181, f32[512]{0:T(512)S(1)} %bitcast.196), kind=kOutput, calls=%fused_computation.105 | convolution fusion | flops 6459752448 | bytes 22022144 | tf_op jit(solution)/shard_map/dot_general | solution.py:220
  608.4 20.2 %fusion.32 = f32[512,1024]{1,0:T(8,128)S(1)} fusion(bf16[3072,1024]{1,0:T(8,128)(2,1)} %all-gather.9.cloned.1.call-done, f32[3072,512]{1,0:T(8,128)} %fusion.135, f32[512]{0:T(512)S(1)} %bitcast.197), kind=kOutput, calls=%fused_computation.59 | convolution fusion | flops 3325034496 | bytes 14682112 | tf_op jit(solution)/shard_map/dot_general | solution.py:220
  628.7 2.4 pad_maximum_fusion
  631.2 4.9 copy.58
  636.6 1.7 copy.59
  638.3 3.9 all-to-all-start.2
  643.4 52.8 %all-to-all-done.2 = bf16[8,384,384]{1,2,0:T(8,128)(2,1)S(1)} async-done(((bf16[8,384,384]{1,2,0:T(8,128)(2,1)}), bf16[8,384,384]{1,2,0:T(8,128)(2,1)S(1)}, u32[]{:S(2)}, u32[]{:S(2)}) %all-to-all-start.2) | async-done | bytes 2359328 | tf_op jit(solution)/shard_map/all_to_all | solution.py:406
  696.1 2.9 copy.60
  699.0 3.6 reshape.211
  702.7 7.0 bitcast_add_fusion
  711.0 1.9 slice_bitcast_fusion.3
  (113 shorter events, 28.9 us)
Async XLA Ops:
  7.2 134.5 %all-gather.13.cloned.1.call-start = ((), (), s32[]{:S(2)}) async-start(), calls=%async_computation.13 | async-start | bytes 9191424 | tf_op jit(solution)/shard_map/all_gather | solution.py:242
  9.6 246.0 %all-gather.7.cloned.1.call-start = ((), (), s32[]{:S(2)}) async-start(), calls=%async_computation.7 | async-start | bytes 17301504 | tf_op jit(solution)/shard_map/all_gather | solution.py:245
  10.4 26.0 %collective-permute-start = (bf16[384,1024]{1,0:T(8,128)(2,1)}, bf16[384,1024]{1,0:T(8,128)(2,1)S(1)}, u32[]{:S(2)}, u32[]{:S(2)}) collective-permute-start(bf16[384,1024]{1,0:T(8,128)(2,1)} %param.9), channel_id=1, source_target_pairs={{2,0},{4,2},{6,4},{7,6},{5,7},{3,5},{1,3},{0,1},{10,8},{12,10},{14... | collective-permute-start | bytes 2359304 | tf_op jit(solution)/shard_map/ppermute | solution.py:207
  36.3 31.3 %collective-permute-start.1 = (bf16[384,1024]{1,0:T(8,128)(2,1)S(1)}, bf16[384,1024]{1,0:T(8,128)(2,1)S(1)}, u32[]{:S(2)}, u32[]{:S(2)}) collective-permute-start(bf16[384,1024]{1,0:T(8,128)(2,1)S(1)} %collective-permute-done), channel_id=1, source_target_pairs={{2,0},{4,2},{6,4},{7,6},{5,7},{3,5},{1,3},{0,1},{10,8},{12,10},{14... | collective-permute-start | bytes 2359304 | tf_op jit(solution)/shard_map/ppermute | solution.py:207
  38.0 31.3 %collective-permute-start.4 = (bf16[384,1024]{1,0:T(8,128)(2,1)}, bf16[384,1024]{1,0:T(8,128)(2,1)S(1)}, u32[]{:S(2)}, u32[]{:S(2)}) collective-permute-start(bf16[384,1024]{1,0:T(8,128)(2,1)} %param.9), channel_id=1, source_target_pairs={{0,2},{2,4},{4,6},{6,7},{7,5},{5,3},{3,1},{1,0},{8,10},{10,12},{12... | collective-permute-start | bytes 2359304 | tf_op jit(solution)/shard_map/ppermute | solution.py:203
  67.6 43.9 %collective-permute-start.2 = (bf16[384,1024]{1,0:T(8,128)(2,1)S(1)}, bf16[384,1024]{1,0:T(8,128)(2,1)}, u32[]{:S(2)}, u32[]{:S(2)}) collective-permute-start(bf16[384,1024]{1,0:T(8,128)(2,1)S(1)} %collective-permute-done.1), channel_id=1, source_target_pairs={{2,0},{4,2},{6,4},{7,6},{5,7},{3,5},{1,3},{0,1},{10,8},{12,10},{14... | collective-permute-start | bytes 2359304 | tf_op jit(solution)/shard_map/ppermute | solution.py:207
  69.4 43.1 %collective-permute-start.5 = (bf16[384,1024]{1,0:T(8,128)(2,1)S(1)}, bf16[384,1024]{1,0:T(8,128)(2,1)S(1)}, u32[]{:S(2)}, u32[]{:S(2)}) collective-permute-start(bf16[384,1024]{1,0:T(8,128)(2,1)S(1)} %collective-permute-done.4), channel_id=1, source_target_pairs={{0,2},{2,4},{4,6},{6,7},{7,5},{5,3},{3,1},{1,0},{8,10},{10,12},{12... | collective-permute-start | bytes 2359304 | tf_op jit(solution)/shard_map/ppermute | solution.py:203
  111.5 12.7 %collective-permute-start.3 = (bf16[384,1024]{1,0:T(8,128)(2,1)}, bf16[384,1024]{1,0:T(8,128)(2,1)S(1)}, u32[]{:S(2)}, u32[]{:S(2)}) collective-permute-start(bf16[384,1024]{1,0:T(8,128)(2,1)} %collective-permute-done.2), channel_id=1, source_target_pairs={{2,0},{4,2},{6,4},{7,6},{5,7},{3,5},{1,3},{0,1},{10,8},{12,10},{14... | collective-permute-start | bytes 2359304 | tf_op jit(solution)/shard_map/ppermute | solution.py:207
  112.5 13.2 %collective-permute-start.6 = (bf16[384,1024]{1,0:T(8,128)(2,1)S(1)}, bf16[384,1024]{1,0:T(8,128)(2,1)S(1)}, u32[]{:S(2)}, u32[]{:S(2)}) collective-permute-start(bf16[384,1024]{1,0:T(8,128)(2,1)S(1)} %collective-permute-done.5), channel_id=1, source_target_pairs={{0,2},{2,4},{4,6},{6,7},{7,5},{5,3},{3,1},{1,0},{8,10},{10,12},{12... | collective-permute-start | bytes 2359304 | tf_op jit(solution)/shard_map/ppermute | solution.py:203
  145.2 2.7 copy-start.1
  163.7 86.0 %copy-start.6 = (bf16[384,1024]{1,0:T(8,128)(2,1)S(1)}, bf16[384,1024]{1,0:T(8,128)(2,1)}, u32[]{:S(2)}) copy-start(bf16[384,1024]{1,0:T(8,128)(2,1)} %param.9) | copy-start | bytes 2359300
  208.4 41.3 %all-to-all-start = ((bf16[8,384,128]{2,1,0:T(8,128)(2,1)}), bf16[8,384,128]{2,1,0:T(8,128)(2,1)S(1)}, u32[]{:S(2)}, u32[]{:S(2)}) async-start(bf16[8,384,128]{2,1,0:T(8,128)(2,1)} %reshape.248), calls=%async_computation | async-start | bytes 1572864 | tf_op jit(solution)/shard_map/all_to_all | solution.py:279
  216.4 279.9 %all-gather.11.cloned.1.call-start = ((), (), s32[]{:S(2)}) async-start(), calls=%async_computation.11 | async-start | bytes 7077888 | tf_op jit(solution)/shard_map/all_gather | solution.py:285
  249.7 5.6 copy-start.2
  255.4 304.1 %reduce-scatter.4.cloned.1.call-start = ((), (), s32[]{:S(2)}) async-start(), calls=%async_computation.8 | async-start | bytes 4718592 | tf_op jit(solution)/shard_map/reduce_scatter | solution.py:346
  255.6 10.9 %copy-start = (bf16[8192,1024]{1,0:T(8,128)(2,1)S(1)}, bf16[8192,1024]{1,0:T(8,128)(2,1)}, u32[]{:S(2)}) copy-start(bf16[8192,1024]{1,0:T(8,128)(2,1)} %all-gather.7.cloned.1.call-done) | copy-start | bytes 50331652
  339.5 8.8 %copy-start.5 = (bf16[384,1024]{1,0:T(8,128)(2,1)S(1)}, bf16[384,1024]{1,0:T(8,128)(2,1)}, u32[]{:S(2)}) copy-start(bf16[384,1024]{1,0:T(8,128)(2,1)} %param.10) | copy-start | bytes 2359300
  348.3 8.1 %copy-start.4 = (bf16[384,8,128]{0,2,1:T(8,128)(2,1)S(1)}, bf16[384,8,128]{0,2,1:T(8,128)(2,1)}, u32[]{:S(2)}) copy-start(bf16[384,8,128]{0,2,1:T(8,128)(2,1)} %copy.65) | copy-start | bytes 2359300
  356.4 5.1 copy-start.3
  363.7 46.0 %all-to-all-start.1 = ((bf16[8,384,128]{1,2,0:T(8,128)(2,1)}), bf16[8,384,128]{1,2,0:T(8,128)(2,1)S(1)}, u32[]{:S(2)}, u32[]{:S(2)}) async-start(bf16[8,384,128]{1,2,0:T(8,128)(2,1)} %bitcast.35), calls=%async_computation.1 | async-start | bytes 1572864 | tf_op jit(solution)/shard_map/all_to_all | solution.py:358
  370.5 222.0 %all-gather.9.cloned.1.call-start = ((), (), s32[]{:S(2)}) async-start(), calls=%async_computation.10 | async-start | bytes 7077888 | tf_op jit(solution)/shard_map/all_gather | solution.py:324
  484.4 74.5 %all-to-all-start.3 = ((f32[8,1,50688]{2,1,0:T(1,128)}), f32[8,1,50688]{2,1,0:T(1,128)S(1)}, u32[]{:S(2)}, u32[]{:S(2)}) async-start(f32[8,1,50688]{2,1,0:T(1,128)} %copy.64), calls=%async_computation.3 | async-start | bytes 3244032 | tf_op jit(solution)/shard_map/all_to_all | solution.py:396
  488.0 221.7 %reduce-scatter.6.cloned.1.call-start = ((), (), s32[]{:S(2)}) async-start(), calls=%async_computation.9 | async-start | bytes 2785280 | tf_op jit(solution)/shard_map/reduce_scatter | solution.py:216
  562.1 150.8 %reduce-scatter.8.cloned.1.call-start = ((), (), s32[]{:S(2)}) async-start(), calls=%async_computation.12 | async-start | bytes 5242880 | tf_op jit(solution)/shard_map/reduce_scatter | solution.py:338
  636.0 6.8 copy-start.7
  638.3 57.9 %all-to-all-start.2 = ((bf16[8,384,384]{1,2,0:T(8,128)(2,1)}), bf16[8,384,384]{1,2,0:T(8,128)(2,1)S(1)}, u32[]{:S(2)}, u32[]{:S(2)}) async-start(bf16[8,384,384]{1,2,0:T(8,128)(2,1)} %copy.59), calls=%async_computation.2 | async-start | bytes 4718592 | tf_op jit(solution)/shard_map/all_to_all | solution.py:406
Sparse Core Ops, SparseCore 0:
  11.5 104.1 all-gather.12
  118.7 133.1 all-gather.6
  255.5 98.3 all-gather.10
  359.8 105.8 reduce-scatter.3
  467.7 124.6 all-gather.8
  594.9 30.0 reduce-scatter.5
  631.3 41.9 reduce-scatter.7

commit v10 on v9

--- a/solution.py
+++ b/solution.py
@@ -343,14 +343,14 @@
     grad_bias_o = jnp.sum(grad_branch_low.astype(jnp.float32), axis=0)
     block_height = 4 * model_width // (fsdp_count * seq_count)
     out_blocks = model_width // (seq_count * block_height)
-    out_rows = lax.psum_scatter(
+    out_partial = jnp.transpose(
         contract_rows(attn_mixed, grad_branch_low).reshape(
             out_blocks, seq_count, block_height, model_width
         ),
-        "seq",
-        scatter_dimension=1,
-        tiled=True,
-    )[:, 0]
+        (1, 0, 2, 3),
+    )
+    out_parts = lax.all_to_all(out_partial, "seq", split_axis=0, concat_axis=0, tiled=True)
+    out_rows = jnp.sum(out_parts, axis=0)
     grad_mixed_low = contract_cols(grad_branch_low, out_weights).astype(jnp.bfloat16)
     grad_split = jnp.transpose(
         grad_mixed_low.reshape(tokens, seq_count, head_width), (1, 0, 2)

time: 730 us -> 745 us (1.021)
  waiting for transfers between devices: 294 us -> 303 us
    all_to_all x0 -> x1, waiting for transfers between devices: none -> 77 us  [layer_body(): lax.all_to_all(out_partial, 'seq', split_axis=0, concat_axis=0, tiled=True)]
    all_gather x1, waiting for transfers between devices: 30.3 us -> 0.02 us  [layer_body(): grad_mlp_seg = lax.all_gather(grad_mlp_low, 'seq', axis=0, tiled=True)]
    all_to_all x1, waiting for transfers between devices: 32.9 us -> 11.9 us  [layer_body(): lax.all_to_all(grad_split, 'seq', split_axis=0, concat_axis=0, tiled=True)]
    all_to_all x1, waiting for transfers between devices: 54.3 us -> 38.3 us  [layer_body(): lax.all_to_all(jnp.concatenate([row_part.reshape(seq_count, -1), vector_p...]
    unnamed x34 -> x38, local copies, waits for them, and re-layouts: 14.1 us -> 15.3 us
  transfers between devices with their start and end apart: 18 -> 18, of which waited for: 10 -> 10; matrix products, arithmetic and copies ran while one was open for 33% -> 33% of each run, Pallas kernels for 13% -> 12%
where the time goes in v10:
time: 745 us; the launch traced here: 737 us
  waiting for transfers between devices  303 us (41%)
  matrix products  116 us (16%)
  Pallas kernels  91 us (12%)
  local copies, waits for them, and re-layouts  86.2 us (12%)
  other arithmetic  44.7 us (6%)
  blocking collectives  42.5 us (6%)
  starting transfers between devices  37.4 us (5%)
  between operations  16.2 us (2%)
    ppermute x4, waiting for transfers between devices, ring_gather(): moving = lax.ppermute(moving, 'seq', backward_pairs)  90.1 us
    all_to_all x1, waiting for transfers between devices, layer_body(): lax.all_to_all(out_partial, 'seq', split_axis=0, concat_axis=0, tiled=True)  77 us
    all_to_all x1, waiting for transfers between devices, layer_body(): lax.all_to_all(head_grads.reshape(seq_count, tokens, 3 * head_width), 'se...  52.8 us
    pallas_call x1, Pallas kernels, attn_backward(): pl.pallas_call(functools.partial(_bwd_kernel, scale=scale, block=block),...  51.6 us
    psum x1, blocking collectives, layer_body(): lax.psum((squares, jnp.sum(valid_rows)), ('fsdp', 'seq'))  42.5 us
    dot_general x3, matrix products, contract_rows(): lax.dot_general(left, right, (((0,), (0,)), ((), ())), preferred_element_...  40.4 us
    pallas_call x1, Pallas kernels, attn_forward(): pl.pallas_call(functools.partial(_fwd_kernel, scale=scale, block=block),...  39.4 us
    all_to_all x1, waiting for transfers between devices, layer_body(): lax.all_to_all(jnp.concatenate([row_part.reshape(seq_count, -1), vector_p...  38.3 us
  transfers between devices with their start and end apart: 18, of which 10 were waited for; matrix products, arithmetic and copies ran while one was open for 33% of the time, Pallas kernels for 12%

profile of v10, /device:TPU:0, one launch (start us, length us, event | category | flops | bytes accessed | tf_op | source)
XLA Modules:
  0.0 736.6 jit_solution(9216535399115599455)
XLA Ops:
  7.9 1.7 maximum_bitcast_fusion.1
  10.4 3.0 collective-permute-start
  13.4 22.9 %collective-permute-done = bf16[384,1024]{1,0:T(8,128)(2,1)S(1)} collective-permute-done((bf16[384,1024]{1,0:T(8,128)(2,1)}, bf16[384,1024]{1,0:T(8,128)(2,1)S(1)}, u32[]{:S(2)}, u32[]{:S(2)}) %collective-permute-start) | collective-permute-done | bytes 786464 | tf_op jit(solution)/shard_map/ppermute | solution.py:207
  36.3 1.7 collective-permute-start.1
  42.3 25.3 %collective-permute-done.1 = bf16[384,1024]{1,0:T(8,128)(2,1)S(1)} collective-permute-done((bf16[384,1024]{1,0:T(8,128)(2,1)S(1)}, bf16[384,1024]{1,0:T(8,128)(2,1)S(1)}, u32[]{:S(2)}, u32[]{:S(2)}) %collective-permute-start.1) | collective-permute-done | bytes 786464 | tf_op jit(solution)/shard_map/ppermute | solution.py:207
  69.4 1.7 collective-permute-start.5
  71.2 2.4 copy.52.dq_ref
  74.2 2.2 bitcast_dynamic-update-slice_fusion.7
  76.4 35.1 %collective-permute-done.2 = bf16[384,1024]{1,0:T(8,128)(2,1)} collective-permute-done((bf16[384,1024]{1,0:T(8,128)(2,1)S(1)}, bf16[384,1024]{1,0:T(8,128)(2,1)}, u32[]{:S(2)}, u32[]{:S(2)}) %collective-permute-start.2) | collective-permute-done | bytes 786464 | tf_op jit(solution)/shard_map/ppermute | solution.py:207
  112.5 2.0 collective-permute-start.6
  115.4 2.1 bitcast_dynamic-update-slice_fusion.4
  117.5 6.8 collective-permute-done.3
  128.5 6.6 gather_fusion
  135.1 6.6 bitcast_select_fusion
  141.8 3.5 slice.120
  145.3 2.6 copy-done.1
  149.6 4.8 fusion.133
  155.1 4.1 copy.51
  159.2 4.7 slice_bitcast_fusion
  163.8 39.4 %shard_map.136 = (bf16[2,3072,64]{2,1,0:T(8,128)(2,1)}, f32[2,3072,1]{2,1,0:T(8,128)}) custom-call(s32[6]{0:T(128)} %get-tuple-element.74.lo_ref, s32[6]{0:T(128)} %get-tuple-element.73.hi_ref, bf16[2,3072,64]{2,1,0:T(8,128)(2,1)} %get-tuple-element.58.q_ref, bf16[2,3072,64]{2,1,0:T(8,128)(2,1)} %get-tuple-element.57.k_ref, ...), custom_call_target="tpu_custom_call" | custom-call | tf_op jit(solution)/shard_map/pallas_call | solution.py:75
  203.2 3.9 copy.69
  207.1 1.5 reshape.248
  208.6 8.0 %all-to-all-start = ((bf16[8,384,128]{2,1,0:T(8,128)(2,1)}), bf16[8,384,128]{2,1,0:T(8,128)(2,1)S(1)}, u32[]{:S(2)}, u32[]{:S(2)}) async-start(bf16[8,384,128]{2,1,0:T(8,128)(2,1)} %reshape.248), calls=%async_computation | async-start | bytes 1572864 | tf_op jit(solution)/shard_map/all_to_all | solution.py:279
  218.4 31.4 %all-to-all-done = bf16[8,384,128]{2,1,0:T(8,128)(2,1)S(1)} async-done(((bf16[8,384,128]{2,1,0:T(8,128)(2,1)}), bf16[8,384,128]{2,1,0:T(8,128)(2,1)S(1)}, u32[]{:S(2)}, u32[]{:S(2)}) %all-to-all-start) | async-done | bytes 786464 | tf_op jit(solution)/shard_map/all_to_all | solution.py:279
  249.9 3.0 fusion.130
  255.5 10.2 %fusion.126 = f32[384,4096]{1,0:T(8,128)} fusion(bf16[384,1024]{1,0:T(8,128)(2,1)} %fusion.45, bf16[8192,1024]{1,0:T(8,128)(2,1)} %all-gather.7.cloned.1.call-done), kind=kOutput, calls=%fused_computation.241 | convolution fusion | flops 3221225472 | bytes 15466496 | tf_op jit(solution)/shard_map/dot_general | solution.py:226
  266.4 19.1 %fusion.129 = (f32[384]{0:T(512)S(1)}, f32[384,1024]{1,0:T(8,128)S(1)}, f32[384,1024]{1,0:T(8,128)S(1)}) fusion(f32[1024]{0:T(1024)S(1)} %get-tuple-element.62, f32[1024]{0:T(1024)S(1)} %get-tuple-element.63, f32[1024]{0:T(1024)S(1)} %get-tuple-element.64, f32[384]{0:T(512)S(1)} %add_rsqrt_fusion.1, f32[384,1024]{1,0:T(8,128)S(1)} %get-tuple-element.49, ...), kind=kOutput, calls=%fused_computation.243 | convolution fusion | flops 3327786496 | bytes 19432960 | tf_op jit(solution)/shard_map/dot_general | solution.py:288
  285.5 1.4 fusion.42
  286.9 2.6 pad_maximum_fusion.2
  289.6 3.1 slice.127
  292.7 42.5 %all-reduce.2 = (f32[4]{0:T(128)}, f32[]{:T(128)}) all-reduce(f32[4]{0:T(128)S(1)} %pad_maximum_fusion.2, f32[]{:T(128)} %fusion.52), channel_id=1, replica_groups=mesh['fsdp'=4,'seq'=8] {'fsdp','seq'}, use_global_device_ids=true, to_apply=%region_10.11 | all-reduce | flops 5 | bytes 40 | tf_op jit(solution)/shard_map/psum | solution.py:299
  335.2 1.9 fusion.44
  337.1 3.0 convert_reduce_fusion.3
  340.1 8.8 %convert_reduce_fusion.1 = (f32[4096]{0:T(1024)S(1)}, bf16[384,4096]{1,0:T(8,128)(2,1)S(1)}) fusion(f32[384,4096]{1,0:T(8,128)} %fusion.126, f32[4096]{0:T(1024)S(1)} %slice.132, bf16[384,1024]{1,0:T(8,128)(2,1)} %get-tuple-element.41, bf16[8192,1024]{1,0:T(8,128)(2,1)} %all-gather.7.cloned.1.call-done), kind=kOutput, calls=%fused_computation.37 | convolution fusion | flops 3241668608 | bytes 18644992 | tf_op jit(solution)/shard_map/dot_general | solution.py:226
  348.9 7.6 %multiply_reduce_fusion = (f32[1024]{0:T(1024)S(1)}, f32[384]{0:T(512)S(1)}, f32[384]{0:T(512)S(1)}, f32[1024]{0:T(1024)S(1)}, f32[384,1024]{1,0:T(8,128)S(1)}) fusion(f32[384,1024]{1,0:T(8,128)S(1)} %get-tuple-element.49, f32[384]{0:T(512)S(1)} %add_rsqrt_fusion.1, f32[384]{0:T(512)S(1)} %broadcast_multiply_fusion.5, f32[1024]{0:T(1024)S(1)} %get-tuple-element.64, ...), kind=kOutput, calls=%fused_computation.89 | convolution fusion | flops 3228300288 | bytes 17068032 | tf_op jit(solution)/shard_map/dot_general | solution.py:312
  360.4 6.6 all-to-all-start.1
  367.4 6.2 broadcast_select_fusion
  373.6 11.9 %all-to-all-done.1 = bf16[8,384,128]{1,2,0:T(8,128)(2,1)S(1)} async-done(((bf16[8,384,128]{1,2,0:T(8,128)(2,1)}), bf16[8,384,128]{1,2,0:T(8,128)(2,1)S(1)}, u32[]{:S(2)}, u32[]{:S(2)}) %all-to-all-start.1) | async-done | bytes 786464 | tf_op jit(solution)/shard_map/all_to_all | solution.py:358
  386.3 1.5 copy.57
  387.9 51.6 %shard_map.137 = (f32[2,3072,64]{2,1,0:T(8,128)}, f32[2,3072,64]{2,1,0:T(8,128)}, f32[2,3072,64]{2,1,0:T(8,128)}) custom-call(s32[6]{0:T(128)} %get-tuple-element.74.lo_ref, s32[6]{0:T(128)} %get-tuple-element.73.hi_ref, bf16[2,3072,64]{2,1,0:T(8,128)(2,1)} %get-tuple-element.58.q_ref, bf16[2,3072,64]{2,1,0:T(8,128)(2,1)} %get-tuple-element.57.k_ref, ...), custom_call_target="tpu_custom_call" | custom-call | tf_op jit(solution)/shard_map/pallas_call | solution.py:152
  439.5 5.8 convert_reduce_fusion
  445.5 4.8 copy.62
  450.3 5.6 fusion.134
  457.0 2.9 copy.65
  459.9 3.6 all-to-all-start.3
  463.9 4.6 convolution_bitcast_fusion
  468.5 38.3 %all-to-all-done.3 = f32[8,1,50688]{2,1,0:T(1,128)S(1)} async-done(((f32[8,1,50688]{2,1,0:T(1,128)}), f32[8,1,50688]{2,1,0:T(1,128)S(1)}, u32[]{:S(2)}, u32[]{:S(2)}) %all-to-all-start.3) | async-done | bytes 1622048 | tf_op jit(solution)/shard_map/all_to_all | solution.py:396
  506.8 4.6 all-to-all-start.4
  511.6 6.8 fusion.131
  519.6 8.2 %fusion.135 = f32[3072,512]{1,0:T(8,128)} fusion(bf16[3072,1024]{1,0:T(8,128)(2,1)} %all-gather.11.cloned.1.call-done, bf16[512,1024]{1,0:T(8,128)(2,1)S(1)} %bitcast.185), kind=kOutput, calls=%fused_computation.249 | convolution fusion | flops 3221225472 | bytes 13631488 | tf_op jit(solution)/shard_map/dot_general | solution.py:226
  528.3 77.0 %all-to-all-done.4 = f32[8,1,128,1024]{3,2,1,0:T(8,128)} async-done(((f32[8,1,128,1024]{3,2,1,0:T(8,128)}), f32[8,1,128,1024]{3,2,1,0:T(8,128)}, u32[]{:S(2)}, u32[]{:S(2)}) %all-to-all-start.4) | async-done | bytes 4194336 | tf_op jit(solution)/shard_map/all_to_all | solution.py:352
  605.3 2.6 reduce_sum.260
  607.9 1.5 pad_maximum_fusion.1
  609.6 16.0 %fusion.46 = f32[512,1024]{1,0:T(8,128)S(1)} fusion(bf16[3072,1024]{1,0:T(8,128)(2,1)} %all-gather.11.cloned.1.call-done, f32[3072,512]{1,0:T(8,128)} %fusion.135, bf16[3072,1024]{1,0:T(8,128)(2,1)} %all-gather.9.cloned.1.call-done, bf16[512,1024]{1,0:T(8,128)(2,1)S(1)} %bitcast.184, f32[512]{0:T(512)S(1)} %bitcast.198), kind=kOutput, calls=%fused_computation.105 | convolution fusion | flops 6459752448 | bytes 22022144 | tf_op jit(solution)/shard_map/dot_general | solution.py:220
  625.5 19.8 %fusion.32 = f32[512,1024]{1,0:T(8,128)S(1)} fusion(bf16[3072,1024]{1,0:T(8,128)(2,1)} %all-gather.9.cloned.1.call-done, f32[3072,512]{1,0:T(8,128)} %fusion.135, f32[512]{0:T(512)S(1)} %bitcast.199), kind=kOutput, calls=%fused_computation.59 | convolution fusion | flops 3325034496 | bytes 14682112 | tf_op jit(solution)/shard_map/dot_general | solution.py:220
  645.4 2.4 pad_maximum_fusion
  647.8 4.8 copy.59
  653.1 1.7 copy.60
  654.8 3.9 all-to-all-start.2
  659.9 52.8 %all-to-all-done.2 = bf16[8,384,384]{1,2,0:T(8,128)(2,1)S(1)} async-done(((bf16[8,384,384]{1,2,0:T(8,128)(2,1)}), bf16[8,384,384]{1,2,0:T(8,128)(2,1)S(1)}, u32[]{:S(2)}, u32[]{:S(2)}) %all-to-all-start.2) | async-done | bytes 2359328 | tf_op jit(solution)/shard_map/all_to_all | solution.py:406
  712.8 2.9 copy.61
  715.6 3.6 reshape.211
  719.3 7.0 bitcast_add_fusion
  727.6 1.9 slice_bitcast_fusion.3
  (117 shorter events, 32.2 us)
Async XLA Ops:
  7.2 134.6 %all-gather.13.cloned.1.call-start = ((), (), s32[]{:S(2)}) async-start(), calls=%async_computation.12 | async-start | bytes 9191424 | tf_op jit(solution)/shard_map/all_gather | solution.py:242
  9.6 245.9 %all-gather.7.cloned.1.call-start = ((), (), s32[]{:S(2)}) async-start(), calls=%async_computation.7 | async-start | bytes 17301504 | tf_op jit(solution)/shard_map/all_gather | solution.py:245
  10.4 26.0 %collective-permute-start = (bf16[384,1024]{1,0:T(8,128)(2,1)}, bf16[384,1024]{1,0:T(8,128)(2,1)S(1)}, u32[]{:S(2)}, u32[]{:S(2)}) collective-permute-start(bf16[384,1024]{1,0:T(8,128)(2,1)} %param.9), channel_id=1, source_target_pairs={{2,0},{4,2},{6,4},{7,6},{5,7},{3,5},{1,3},{0,1},{10,8},{12,10},{14... | collective-permute-start | bytes 2359304 | tf_op jit(solution)/shard_map/ppermute | solution.py:207
  36.3 31.3 %collective-permute-start.1 = (bf16[384,1024]{1,0:T(8,128)(2,1)S(1)}, bf16[384,1024]{1,0:T(8,128)(2,1)S(1)}, u32[]{:S(2)}, u32[]{:S(2)}) collective-permute-start(bf16[384,1024]{1,0:T(8,128)(2,1)S(1)} %collective-permute-done), channel_id=1, source_target_pairs={{2,0},{4,2},{6,4},{7,6},{5,7},{3,5},{1,3},{0,1},{10,8},{12,10},{14... | collective-permute-start | bytes 2359304 | tf_op jit(solution)/shard_map/ppermute | solution.py:207
  38.0 31.3 %collective-permute-start.4 = (bf16[384,1024]{1,0:T(8,128)(2,1)}, bf16[384,1024]{1,0:T(8,128)(2,1)S(1)}, u32[]{:S(2)}, u32[]{:S(2)}) collective-permute-start(bf16[384,1024]{1,0:T(8,128)(2,1)} %param.9), channel_id=1, source_target_pairs={{0,2},{2,4},{4,6},{6,7},{7,5},{5,3},{3,1},{1,0},{8,10},{10,12},{12... | collective-permute-start | bytes 2359304 | tf_op jit(solution)/shard_map/ppermute | solution.py:203
  67.6 43.9 %collective-permute-start.2 = (bf16[384,1024]{1,0:T(8,128)(2,1)S(1)}, bf16[384,1024]{1,0:T(8,128)(2,1)}, u32[]{:S(2)}, u32[]{:S(2)}) collective-permute-start(bf16[384,1024]{1,0:T(8,128)(2,1)S(1)} %collective-permute-done.1), channel_id=1, source_target_pairs={{2,0},{4,2},{6,4},{7,6},{5,7},{3,5},{1,3},{0,1},{10,8},{12,10},{14... | collective-permute-start | bytes 2359304 | tf_op jit(solution)/shard_map/ppermute | solution.py:207
  69.4 43.1 %collective-permute-start.5 = (bf16[384,1024]{1,0:T(8,128)(2,1)S(1)}, bf16[384,1024]{1,0:T(8,128)(2,1)S(1)}, u32[]{:S(2)}, u32[]{:S(2)}) collective-permute-start(bf16[384,1024]{1,0:T(8,128)(2,1)S(1)} %collective-permute-done.4), channel_id=1, source_target_pairs={{0,2},{2,4},{4,6},{6,7},{7,5},{5,3},{3,1},{1,0},{8,10},{10,12},{12... | collective-permute-start | bytes 2359304 | tf_op jit(solution)/shard_map/ppermute | solution.py:203
  111.5 12.7 %collective-permute-start.3 = (bf16[384,1024]{1,0:T(8,128)(2,1)}, bf16[384,1024]{1,0:T(8,128)(2,1)S(1)}, u32[]{:S(2)}, u32[]{:S(2)}) collective-permute-start(bf16[384,1024]{1,0:T(8,128)(2,1)} %collective-permute-done.2), channel_id=1, source_target_pairs={{2,0},{4,2},{6,4},{7,6},{5,7},{3,5},{1,3},{0,1},{10,8},{12,10},{14... | collective-permute-start | bytes 2359304 | tf_op jit(solution)/shard_map/ppermute | solution.py:207
  112.5 13.2 %collective-permute-start.6 = (bf16[384,1024]{1,0:T(8,128)(2,1)S(1)}, bf16[384,1024]{1,0:T(8,128)(2,1)S(1)}, u32[]{:S(2)}, u32[]{:S(2)}) collective-permute-start(bf16[384,1024]{1,0:T(8,128)(2,1)S(1)} %collective-permute-done.5), channel_id=1, source_target_pairs={{0,2},{2,4},{4,6},{6,7},{7,5},{5,3},{3,1},{1,0},{8,10},{10,12},{12... | collective-permute-start | bytes 2359304 | tf_op jit(solution)/shard_map/ppermute | solution.py:203
  145.3 2.7 copy-start.1
  163.8 86.0 %copy-start.6 = (bf16[384,1024]{1,0:T(8,128)(2,1)S(1)}, bf16[384,1024]{1,0:T(8,128)(2,1)}, u32[]{:S(2)}) copy-start(bf16[384,1024]{1,0:T(8,128)(2,1)} %param.9) | copy-start | bytes 2359300
  208.6 41.3 %all-to-all-start = ((bf16[8,384,128]{2,1,0:T(8,128)(2,1)}), bf16[8,384,128]{2,1,0:T(8,128)(2,1)S(1)}, u32[]{:S(2)}, u32[]{:S(2)}) async-start(bf16[8,384,128]{2,1,0:T(8,128)(2,1)} %reshape.248), calls=%async_computation | async-start | bytes 1572864 | tf_op jit(solution)/shard_map/all_to_all | solution.py:279
  216.6 303.0 %all-gather.11.cloned.1.call-start = ((), (), s32[]{:S(2)}) async-start(), calls=%async_computation.10 | async-start | bytes 7077888 | tf_op jit(solution)/shard_map/all_gather | solution.py:285
  249.9 5.6 copy-start.2
  255.5 10.9 %copy-start = (bf16[8192,1024]{1,0:T(8,128)(2,1)S(1)}, bf16[8192,1024]{1,0:T(8,128)(2,1)}, u32[]{:S(2)}) copy-start(bf16[8192,1024]{1,0:T(8,128)(2,1)} %all-gather.7.cloned.1.call-done) | copy-start | bytes 50331652
  340.1 8.8 %copy-start.5 = (bf16[384,1024]{1,0:T(8,128)(2,1)S(1)}, bf16[384,1024]{1,0:T(8,128)(2,1)}, u32[]{:S(2)}) copy-start(bf16[384,1024]{1,0:T(8,128)(2,1)} %param.10) | copy-start | bytes 2359300
  348.9 9.3 %copy-start.7 = (bf16[8,128,1024]{2,1,0:T(8,128)(2,1)S(1)}, bf16[8,128,1024]{2,1,0:T(8,128)(2,1)}, u32[]{:S(2)}) copy-start(bf16[8,128,1024]{2,1,0:T(8,128)(2,1)} %slice.127) | copy-start | bytes 6291460
  357.1 1.1 copy-start.4
  360.4 25.1 %all-to-all-start.1 = ((bf16[8,384,128]{1,2,0:T(8,128)(2,1)}), bf16[8,384,128]{1,2,0:T(8,128)(2,1)S(1)}, u32[]{:S(2)}, u32[]{:S(2)}) async-start(bf16[8,384,128]{1,2,0:T(8,128)(2,1)} %bitcast.35), calls=%async_computation.1 | async-start | bytes 1572864 | tf_op jit(solution)/shard_map/all_to_all | solution.py:358
  367.0 242.6 %all-gather.9.cloned.1.call-start = ((), (), s32[]{:S(2)}) async-start(), calls=%async_computation.9 | async-start | bytes 7077888 | tf_op jit(solution)/shard_map/all_gather | solution.py:324
  456.0 7.5 %copy-start.3 = (bf16[8,384,128]{2,1,0:T(8,128)(2,1)S(1)}, bf16[8,384,128]{2,1,0:T(8,128)(2,1)}, u32[]{:S(2)}) copy-start(bf16[8,384,128]{2,1,0:T(8,128)(2,1)} %copy-done.2) | copy-start | bytes 2359300
  459.9 46.9 %all-to-all-start.3 = ((f32[8,1,50688]{2,1,0:T(1,128)}), f32[8,1,50688]{2,1,0:T(1,128)S(1)}, u32[]{:S(2)}, u32[]{:S(2)}) async-start(f32[8,1,50688]{2,1,0:T(1,128)} %copy.65), calls=%async_computation.3 | async-start | bytes 3244032 | tf_op jit(solution)/shard_map/all_to_all | solution.py:396
  506.8 98.5 %all-to-all-start.4 = ((f32[8,1,128,1024]{3,2,1,0:T(8,128)}), f32[8,1,128,1024]{3,2,1,0:T(8,128)}, u32[]{:S(2)}, u32[]{:S(2)}) async-start(f32[8,1,128,1024]{3,2,1,0:T(8,128)} %convolution_bitcast_fusion), calls=%async_computation.4 | async-start | bytes 8388608 | tf_op jit(solution)/shard_map/all_to_all | solution.py:352
  511.3 215.0 %reduce-scatter.3.cloned.1.call-start = ((), (), s32[]{:S(2)}) async-start(), calls=%async_computation.8 | async-start | bytes 2785280 | tf_op jit(solution)/shard_map/reduce_scatter | solution.py:216
  528.3 81.2 %copy-start.8 = (bf16[2,1,256,1024]{3,2,1,0:T(8,128)(2,1)S(1)}, bf16[2,1,256,1024]{3,2,1,0:T(8,128)(2,1)}, u32[]{:S(2)}) copy-start(bf16[2,1,256,1024]{3,2,1,0:T(8,128)(2,1)} %constant_dynamic-slice_fusion.1) | copy-start | bytes 3145732
  609.5 120.0 %reduce-scatter.5.cloned.1.call-start = ((), (), s32[]{:S(2)}) async-start(), calls=%async_computation.11 | async-start | bytes 5242880 | tf_op jit(solution)/shard_map/reduce_scatter | solution.py:338
  652.6 6.8 copy-start.9
  654.8 57.9 %all-to-all-start.2 = ((bf16[8,384,384]{1,2,0:T(8,128)(2,1)}), bf16[8,384,384]{1,2,0:T(8,128)(2,1)S(1)}, u32[]{:S(2)}, u32[]{:S(2)}) async-start(bf16[8,384,384]{1,2,0:T(8,128)(2,1)} %copy.60), calls=%async_computation.2 | async-start | bytes 4718592 | tf_op jit(solution)/shard_map/all_to_all | solution.py:406
Sparse Core Ops, SparseCore 0:
  11.5 104.1 all-gather.12
  118.7 133.2 all-gather.6
  255.6 97.8 all-gather.10
  373.7 101.5 all-gather.8
  609.6 30.9 reduce-scatter.2
  648.0 43.6 reduce-scatter.4

commit v11 on v10

--- a/solution.py
+++ b/solution.py
@@ -10,7 +10,7 @@
 
 H = 16
 
-BLOCK = 512
+BLOCK = 768
 NEG = -1e30
 
 
@@ -296,10 +296,7 @@
             jnp.sum(valid_rows * mlp_branch * mlp_branch),
         ]
     )
-    square_sums, valid_total = lax.psum((squares, jnp.sum(valid_rows)), ("fsdp", "seq"))
-    square_sums, valid_total, cotangent = lax.optimization_barrier(
-        (square_sums, valid_total, cotangent)
-    )
+    own_sums = jnp.pad(jnp.concatenate([squares, jnp.sum(valid_rows)[None]]), (0, 3))
     grad_out = cotangent.astype(jnp.float32)
     grad_resid_two, grad_gain_two, grad_shift_two = norm_backward(
         grad_out, scaled_two, inverse_two, gain_two
@@ -388,6 +385,9 @@
     )
     slot = grad_vector.shape[0] // (fsdp_count * seq_count)
     vector_part = jnp.transpose(grad_vector.reshape(fsdp_count, seq_count, slot), (1, 0, 2))
+    sums_part = jnp.broadcast_to(own_sums, (seq_count, fsdp_count, own_sums.shape[0]))
+    vector_part = jnp.concatenate([vector_part, sums_part], axis=2)
+    wide_slot = slot + own_sums.shape[0]
     by_row = jnp.transpose(head_weight_grads.reshape(model_width, 3, head_width), (1, 0, 2))
     row_part = jnp.transpose(
         by_row.reshape(qkv_blocks, seq_count, block_height, head_width), (1, 0, 2, 3)
@@ -401,8 +401,26 @@
     )
     row_blocks = exchanged[:, :row_size].reshape(seq_count, qkv_blocks, block_height, head_width)
     qkv_rows = jnp.transpose(row_blocks, (1, 2, 0, 3)).reshape(qkv_blocks, block_height, model_width)
-    vector_rows = jnp.sum(exchanged[:, row_size:].reshape(seq_count, fsdp_count, slot), axis=0)
-    vector_rows = jnp.pad(vector_rows, ((0, 0), (0, model_width - slot)))[:, None]
+    vector_rows = jnp.sum(
+        exchanged[:, row_size:].reshape(seq_count, fsdp_count, wide_slot), axis=0
+    )
+    sums_width = own_sums.shape[0]
+    segment_sums = vector_rows[0, slot:]
+    sums_groups = lax.dynamic_update_slice(
+        jnp.zeros((fsdp_count * sums_width,), jnp.float32),
+        segment_sums,
+        (lax.axis_index("fsdp") * sums_width,),
+    )
+    vector_rows = jnp.concatenate(
+        [
+            vector_rows[:, :slot],
+            jnp.broadcast_to(sums_groups, (fsdp_count, fsdp_count * sums_width)),
+        ],
+        axis=1,
+    )
+    vector_rows = jnp.pad(
+        vector_rows, ((0, 0), (0, model_width - vector_rows.shape[1]))
+    )[:, None]
     token_grads = lax.all_to_all(
         head_grads.reshape(seq_count, tokens, 3 * head_width),
         "seq", split_axis=0, concat_axis=0, tiled=True,
@@ -417,6 +435,11 @@
     summed = attn_sum(jnp.concatenate([grad_attn_rows, vector_rows], axis=1))
     attn_shard = summed[:block_height]
     vector_shard = summed[block_height, :slot]
+    total_sums = jnp.sum(
+        summed[block_height, slot : slot + fsdp_count * sums_width].reshape(fsdp_count, sums_width),
+        axis=0,
+    )
+    square_sums, valid_total = total_sums[:4], total_sums[4]
     rms_values = jnp.sqrt(square_sums / (valid_total * model_width))
     return (
         layer_values.astype(jnp.bfloat16),

time: 745 us -> 738 us (level)
  waiting for transfers between devices: 303 us -> 287 us
  blocking collectives: 42.5 us -> 57.7 us
  starting transfers between devices: 37.4 us -> 29.9 us
    all_to_all x0 -> x1, blocking collectives: none -> 57.7 us  [layer_body(): lax.all_to_all(head_grads.reshape(seq_count, tokens, 3 * head_width), 'se...]
    all_to_all x1 -> x0, waiting for transfers between devices: 52.8 us -> none  [layer_body(): lax.all_to_all(head_grads.reshape(seq_count, tokens, 3 * head_width), 'se...]
    psum x1 -> x0, blocking collectives: 42.5 us -> none  [layer_body(): lax.psum((squares, jnp.sum(valid_rows)), ('fsdp', 'seq'))]
    all_to_all x1, waiting for transfers between devices: 38.3 us -> 59.6 us  [layer_body(): lax.all_to_all(jnp.concatenate([row_part.reshape(seq_count, -1), vector_p...]
    all_to_all x1, waiting for transfers between devices: 11.9 us -> 32.5 us  [layer_body(): lax.all_to_all(grad_split, 'seq', split_axis=0, concat_axis=0, tiled=True)]
    unnamed x38 -> x42, local copies, waits for them, and re-layouts: 15.3 us -> 16.8 us
  transfers between devices with their start and end apart: 18 -> 17, of which waited for: 10 -> 9; matrix products, arithmetic and copies ran while one was open for 33% -> 33% of each run, Pallas kernels for 12% -> 12%
where the time goes in v11:
time: 738 us; the launch traced here: 729 us
  waiting for transfers between devices  287 us (39%)
  matrix products  119 us (16%)
  local copies, waits for them, and re-layouts  92.1 us (12%)
  Pallas kernels  86 us (12%)
  blocking collectives  57.7 us (8%)
  other arithmetic  40.5 us (5%)
  starting transfers between devices  29.9 us (4%)
  between operations  16.2 us (2%)
    ppermute x4, waiting for transfers between devices, ring_gather(): moving = lax.ppermute(moving, 'seq', backward_pairs)  90.1 us
    all_to_all x1, waiting for transfers between devices, layer_body(): lax.all_to_all(out_partial, 'seq', split_axis=0, concat_axis=0, tiled=True)  74.1 us
    all_to_all x1, waiting for transfers between devices, layer_body(): lax.all_to_all(jnp.concatenate([row_part.reshape(seq_count, -1), vector_p...  59.6 us
    all_to_all x1, blocking collectives, layer_body(): lax.all_to_all(head_grads.reshape(seq_count, tokens, 3 * head_width), 'se...  57.7 us
    pallas_call x1, Pallas kernels, attn_backward(): pl.pallas_call(functools.partial(_bwd_kernel, scale=scale, block=block),...  49.6 us
    dot_general x3, matrix products, contract_rows(): lax.dot_general(left, right, (((0,), (0,)), ((), ())), preferred_element_...  40.5 us
    pallas_call x1, Pallas kernels, attn_forward(): pl.pallas_call(functools.partial(_fwd_kernel, scale=scale, block=block),...  36.5 us
    all_to_all x1, waiting for transfers between devices, layer_body(): lax.all_to_all(grad_split, 'seq', split_axis=0, concat_axis=0, tiled=True)  32.5 us
  transfers between devices with their start and end apart: 17, of which 9 were waited for; matrix products, arithmetic and copies ran while one was open for 33% of the time, Pallas kernels for 12%

profile of v11, /device:TPU:0, one launch (start us, length us, event | category | flops | bytes accessed | tf_op | source)
XLA Modules:
  0.0 728.7 jit_solution(14022176199231929893)
XLA Ops:
  7.9 1.7 maximum_bitcast_fusion.1
  10.4 3.0 collective-permute-start
  13.4 22.9 %collective-permute-done = bf16[384,1024]{1,0:T(8,128)(2,1)S(1)} collective-permute-done((bf16[384,1024]{1,0:T(8,128)(2,1)}, bf16[384,1024]{1,0:T(8,128)(2,1)S(1)}, u32[]{:S(2)}, u32[]{:S(2)}) %collective-permute-start) | collective-permute-done | bytes 786464 | tf_op jit(solution)/shard_map/ppermute | solution.py:207
  36.3 1.7 collective-permute-start.1
  40.1 1.2 dynamic_slice.20
  42.3 25.3 %collective-permute-done.1 = bf16[384,1024]{1,0:T(8,128)(2,1)S(1)} collective-permute-done((bf16[384,1024]{1,0:T(8,128)(2,1)S(1)}, bf16[384,1024]{1,0:T(8,128)(2,1)S(1)}, u32[]{:S(2)}, u32[]{:S(2)}) %collective-permute-start.1) | collective-permute-done | bytes 786464 | tf_op jit(solution)/shard_map/ppermute | solution.py:207
  68.0 1.3 compare_and_fusion
  69.4 1.7 collective-permute-start.5
  71.2 2.4 copy.54.dq_ref
  74.2 2.2 bitcast_dynamic-update-slice_fusion.7
  76.4 35.1 %collective-permute-done.2 = bf16[384,1024]{1,0:T(8,128)(2,1)} collective-permute-done((bf16[384,1024]{1,0:T(8,128)(2,1)S(1)}, bf16[384,1024]{1,0:T(8,128)(2,1)}, u32[]{:S(2)}, u32[]{:S(2)}) %collective-permute-start.2) | collective-permute-done | bytes 786464 | tf_op jit(solution)/shard_map/ppermute | solution.py:207
  112.5 2.0 collective-permute-start.6
  115.4 2.1 bitcast_dynamic-update-slice_fusion.4
  117.5 6.8 collective-permute-done.3
  128.5 6.6 gather_fusion
  135.1 6.6 bitcast_select_fusion
  141.8 3.5 slice.140
  145.3 2.6 copy-done.1
  149.6 4.8 fusion.134
  155.0 4.1 copy.53
  159.2 4.7 slice_bitcast_fusion
  163.9 36.5 %shard_map.136 = (bf16[2,3072,64]{2,1,0:T(8,128)(2,1)}, f32[2,3072,1]{2,1,0:T(8,128)}) custom-call(s32[4]{0:T(128)} %get-tuple-element.65.lo_ref, s32[4]{0:T(128)} %get-tuple-element.64.hi_ref, bf16[2,3072,64]{2,1,0:T(8,128)(2,1)} %get-tuple-element.48.q_ref, bf16[2,3072,64]{2,1,0:T(8,128)(2,1)} %get-tuple-element.47.k_ref, ...), custom_call_target="tpu_custom_call" | custom-call | tf_op jit(solution)/shard_map/pallas_call | solution.py:75
  200.3 4.0 copy.72
  204.3 1.5 reshape.250
  205.8 8.0 %all-to-all-start = ((bf16[8,384,128]{2,1,0:T(8,128)(2,1)}), bf16[8,384,128]{2,1,0:T(8,128)(2,1)S(1)}, u32[]{:S(2)}, u32[]{:S(2)}) async-start(bf16[8,384,128]{2,1,0:T(8,128)(2,1)} %reshape.250), calls=%async_computation | async-start | bytes 1572864 | tf_op jit(solution)/shard_map/all_to_all | solution.py:279
  215.0 3.1 slice.147
  218.1 29.3 %all-to-all-done = bf16[8,384,128]{2,1,0:T(8,128)(2,1)S(1)} async-done(((bf16[8,384,128]{2,1,0:T(8,128)(2,1)}), bf16[8,384,128]{2,1,0:T(8,128)(2,1)S(1)}, u32[]{:S(2)}, u32[]{:S(2)}) %all-to-all-start) | async-done | bytes 786464 | tf_op jit(solution)/shard_map/all_to_all | solution.py:279
  247.5 4.3 fusion.131
  252.1 1.2 fusion.45
  253.4 10.5 %fusion.127 = f32[384,4096]{1,0:T(8,128)} fusion(bf16[384,1024]{1,0:T(8,128)(2,1)} %fusion.45, bf16[8192,1024]{1,0:T(8,128)(2,1)} %all-gather.7.cloned.1.call-done), kind=kOutput, calls=%fused_computation.241 | convolution fusion | flops 3221225472 | bytes 15466496 | tf_op jit(solution)/shard_map/dot_general | solution.py:226
  264.9 20.1 %fusion.44 = (f32[]{:T(128)}, f32[]{:T(128)}, f32[384]{0:T(512)S(1)}, f32[384,1024]{1,0:T(8,128)S(1)}) fusion(f32[384]{0:T(512)S(1)} %fusion.50, f32[1024]{0:T(1024)S(1)} %get-tuple-element.54, f32[384,1024]{1,0:T(8,128)S(1)} %copy-done.10, f32[1024]{0:T(1024)S(1)} %get-tuple-element.55, f32[1024]{0:T(1024)S(1)} %get-tuple-element.56, ...), kind=kOutput, calls=%fused_computation.81 | convolution fusion | flops 3330145792 | bytes 19435016 | tf_op jit(solution)/shard_map/dot_general | solution.py:288
  285.4 1.7 fusion.40
  287.1 1.8 convert_reduce_fusion.3
  288.9 9.0 %convert_reduce_fusion.1 = (f32[4096]{0:T(1024)S(1)}, bf16[384,4096]{1,0:T(8,128)(2,1)S(1)}) fusion(f32[384,4096]{1,0:T(8,128)} %fusion.127, f32[4096]{0:T(1024)S(1)} %slice.152, bf16[384,1024]{1,0:T(8,128)(2,1)} %get-tuple-element.31, bf16[8192,1024]{1,0:T(8,128)(2,1)} %all-gather.7.cloned.1.call-done), kind=kOutput, calls=%fused_computation.37 | convolution fusion | flops 3241668608 | bytes 18644992 | tf_op jit(solution)/shard_map/dot_general | solution.py:226
  297.9 8.3 %multiply_reduce_fusion = (f32[1024]{0:T(1024)S(1)}, f32[384]{0:T(512)S(1)}, f32[384]{0:T(512)S(1)}, f32[]{:T(128)}, f32[1024]{0:T(1024)S(1)}, /*index=5*/f32[384,1024]{1,0:T(8,128)S(1)}) fusion(f32[384,1024]{1,0:T(8,128)S(1)} %get-tuple-element.39, f32[384]{0:T(512)S(1)} %add_rsqrt_fusion.1, f32[384]{0:T(512)S(1)} %broadcast_multiply_fusion.5, ...), kind=kOutput, calls=%fused_computation.89 | convolution fusion | flops 3229479936 | bytes 17069572 | tf_op jit(solution)/shard_map/dot_general | solution.py:309
  310.1 3.6 all-to-all-start.1
  314.4 6.2 broadcast_select_fusion
  320.7 3.3 concatenate.33
  324.0 32.5 %all-to-all-done.1 = bf16[8,384,128]{1,2,0:T(8,128)(2,1)S(1)} async-done(((bf16[8,384,128]{1,2,0:T(8,128)(2,1)}), bf16[8,384,128]{1,2,0:T(8,128)(2,1)S(1)}, u32[]{:S(2)}, u32[]{:S(2)}) %all-to-all-start.1) | async-done | bytes 786464 | tf_op jit(solution)/shard_map/all_to_all | solution.py:355
  357.4 1.9 copy.59
  359.3 49.6 %shard_map.137 = (f32[2,3072,64]{2,1,0:T(8,128)}, f32[2,3072,64]{2,1,0:T(8,128)}, f32[2,3072,64]{2,1,0:T(8,128)}) custom-call(s32[4]{0:T(128)} %get-tuple-element.65.lo_ref, s32[4]{0:T(128)} %get-tuple-element.64.hi_ref, bf16[2,3072,64]{2,1,0:T(8,128)(2,1)} %get-tuple-element.48.q_ref, bf16[2,3072,64]{2,1,0:T(8,128)(2,1)} %get-tuple-element.47.k_ref, ...), custom_call_target="tpu_custom_call" | custom-call | tf_op jit(solution)/shard_map/pallas_call | solution.py:152
  408.9 6.5 convert_reduce_fusion
  415.4 4.8 copy.64
  420.2 5.6 fusion.135
  427.3 2.8 copy.68
  430.2 3.6 all-to-all-start.3
  434.1 4.7 convolution_bitcast_fusion
  438.8 59.6 %all-to-all-done.3 = f32[8,1,50720]{2,1,0:T(1,128)S(1)} async-done(((f32[8,1,50720]{2,1,0:T(1,128)}), f32[8,1,50720]{2,1,0:T(1,128)S(1)}, u32[]{:S(2)}, u32[]{:S(2)}) %all-to-all-start.3) | async-done | bytes 1623072 | tf_op jit(solution)/shard_map/all_to_all | solution.py:396
  498.4 4.5 all-to-all-start.4
  503.1 7.0 fusion.132
  511.2 8.2 %fusion.136 = f32[3072,512]{1,0:T(8,128)} fusion(bf16[3072,1024]{1,0:T(8,128)(2,1)} %all-gather.11.cloned.1.call-done, bf16[512,1024]{1,0:T(8,128)(2,1)S(1)} %bitcast.189), kind=kOutput, calls=%fused_computation.249 | convolution fusion | flops 3221225472 | bytes 13631488 | tf_op jit(solution)/shard_map/dot_general | solution.py:226
  522.3 74.1 %all-to-all-done.4 = f32[8,1,128,1024]{3,2,1,0:T(8,128)} async-done(((f32[8,1,128,1024]{3,2,1,0:T(8,128)}), f32[8,1,128,1024]{3,2,1,0:T(8,128)}, u32[]{:S(2)}, u32[]{:S(2)}) %all-to-all-start.4) | async-done | bytes 4194336 | tf_op jit(solution)/shard_map/all_to_all | solution.py:349
  596.4 2.6 reduce_sum.269
  599.0 1.6 pad_maximum_fusion.1
  600.7 16.0 %fusion.46 = f32[512,1024]{1,0:T(8,128)S(1)} fusion(bf16[3072,1024]{1,0:T(8,128)(2,1)} %all-gather.11.cloned.1.call-done, f32[3072,512]{1,0:T(8,128)} %fusion.136, bf16[3072,1024]{1,0:T(8,128)(2,1)} %all-gather.9.cloned.1.call-done, bf16[512,1024]{1,0:T(8,128)(2,1)S(1)} %bitcast.188, f32[512]{0:T(512)S(1)} %bitcast.203), kind=kOutput, calls=%fused_computation.105 | convolution fusion | flops 6459752448 | bytes 22022144 | tf_op jit(solution)/shard_map/dot_general | solution.py:220
  616.7 19.8 %fusion.32 = f32[512,1024]{1,0:T(8,128)S(1)} fusion(bf16[3072,1024]{1,0:T(8,128)(2,1)} %all-gather.9.cloned.1.call-done, f32[3072,512]{1,0:T(8,128)} %fusion.136, f32[512]{0:T(512)S(1)} %bitcast.204), kind=kOutput, calls=%fused_computation.59 | convolution fusion | flops 3325034496 | bytes 14682112 | tf_op jit(solution)/shard_map/dot_general | solution.py:220
  636.5 2.4 pad_maximum_fusion
  639.0 4.8 copy.61
  644.6 57.7 %all_to_all.32 = bf16[8,384,384]{1,2,0:T(8,128)(2,1)S(1)} all-to-all(bf16[8,384,384]{1,2,0:T(8,128)(2,1)S(1)} %copy.62), channel_id=1, replica_groups=mesh['fsdp'=4,'seq'=8] {'seq'}, dimensions={0} | all-to-all | bytes 4718592 | tf_op jit(solution)/shard_map/all_to_all | solution.py:424
  702.2 2.9 copy.63
  705.1 3.6 reshape.213
  708.8 7.0 bitcast_add_fusion
  717.8 1.3 slice_reduce_fusion.2
  719.7 1.9 slice_bitcast_fusion.3
  (132 shorter events, 30.4 us)
Async XLA Ops:
  7.2 134.6 %all-gather.13.cloned.1.call-start = ((), (), s32[]{:S(2)}) async-start(), calls=%async_computation.12 | async-start | bytes 9191424 | tf_op jit(solution)/shard_map/all_gather | solution.py:242
  9.6 243.8 %all-gather.7.cloned.1.call-start = ((), (), s32[]{:S(2)}) async-start(), calls=%async_computation.7 | async-start | bytes 17301504 | tf_op jit(solution)/shard_map/all_gather | solution.py:245
  10.4 26.0 %collective-permute-start = (bf16[384,1024]{1,0:T(8,128)(2,1)}, bf16[384,1024]{1,0:T(8,128)(2,1)S(1)}, u32[]{:S(2)}, u32[]{:S(2)}) collective-permute-start(bf16[384,1024]{1,0:T(8,128)(2,1)} %param.9), channel_id=1, source_target_pairs={{2,0},{4,2},{6,4},{7,6},{5,7},{3,5},{1,3},{0,1},{10,8},{12,10},{14... | collective-permute-start | bytes 2359304 | tf_op jit(solution)/shard_map/ppermute | solution.py:207
  36.3 31.3 %collective-permute-start.1 = (bf16[384,1024]{1,0:T(8,128)(2,1)S(1)}, bf16[384,1024]{1,0:T(8,128)(2,1)S(1)}, u32[]{:S(2)}, u32[]{:S(2)}) collective-permute-start(bf16[384,1024]{1,0:T(8,128)(2,1)S(1)} %collective-permute-done), channel_id=1, source_target_pairs={{2,0},{4,2},{6,4},{7,6},{5,7},{3,5},{1,3},{0,1},{10,8},{12,10},{14... | collective-permute-start | bytes 2359304 | tf_op jit(solution)/shard_map/ppermute | solution.py:207
  38.0 31.3 %collective-permute-start.4 = (bf16[384,1024]{1,0:T(8,128)(2,1)}, bf16[384,1024]{1,0:T(8,128)(2,1)S(1)}, u32[]{:S(2)}, u32[]{:S(2)}) collective-permute-start(bf16[384,1024]{1,0:T(8,128)(2,1)} %param.9), channel_id=1, source_target_pairs={{0,2},{2,4},{4,6},{6,7},{7,5},{5,3},{3,1},{1,0},{8,10},{10,12},{12... | collective-permute-start | bytes 2359304 | tf_op jit(solution)/shard_map/ppermute | solution.py:203
  67.6 43.9 %collective-permute-start.2 = (bf16[384,1024]{1,0:T(8,128)(2,1)S(1)}, bf16[384,1024]{1,0:T(8,128)(2,1)}, u32[]{:S(2)}, u32[]{:S(2)}) collective-permute-start(bf16[384,1024]{1,0:T(8,128)(2,1)S(1)} %collective-permute-done.1), channel_id=1, source_target_pairs={{2,0},{4,2},{6,4},{7,6},{5,7},{3,5},{1,3},{0,1},{10,8},{12,10},{14... | collective-permute-start | bytes 2359304 | tf_op jit(solution)/shard_map/ppermute | solution.py:207
  69.4 43.1 %collective-permute-start.5 = (bf16[384,1024]{1,0:T(8,128)(2,1)S(1)}, bf16[384,1024]{1,0:T(8,128)(2,1)S(1)}, u32[]{:S(2)}, u32[]{:S(2)}) collective-permute-start(bf16[384,1024]{1,0:T(8,128)(2,1)S(1)} %collective-permute-done.4), channel_id=1, source_target_pairs={{0,2},{2,4},{4,6},{6,7},{7,5},{5,3},{3,1},{1,0},{8,10},{10,12},{12... | collective-permute-start | bytes 2359304 | tf_op jit(solution)/shard_map/ppermute | solution.py:203
  111.5 12.7 %collective-permute-start.3 = (bf16[384,1024]{1,0:T(8,128)(2,1)}, bf16[384,1024]{1,0:T(8,128)(2,1)S(1)}, u32[]{:S(2)}, u32[]{:S(2)}) collective-permute-start(bf16[384,1024]{1,0:T(8,128)(2,1)} %collective-permute-done.2), channel_id=1, source_target_pairs={{2,0},{4,2},{6,4},{7,6},{5,7},{3,5},{1,3},{0,1},{10,8},{12,10},{14... | collective-permute-start | bytes 2359304 | tf_op jit(solution)/shard_map/ppermute | solution.py:207
  112.5 13.2 %collective-permute-start.6 = (bf16[384,1024]{1,0:T(8,128)(2,1)S(1)}, bf16[384,1024]{1,0:T(8,128)(2,1)S(1)}, u32[]{:S(2)}, u32[]{:S(2)}) collective-permute-start(bf16[384,1024]{1,0:T(8,128)(2,1)S(1)} %collective-permute-done.5), channel_id=1, source_target_pairs={{0,2},{2,4},{4,6},{6,7},{7,5},{5,3},{3,1},{1,0},{8,10},{10,12},{12... | collective-permute-start | bytes 2359304 | tf_op jit(solution)/shard_map/ppermute | solution.py:203
  145.3 2.7 copy-start.1
  200.3 47.1 %copy-start.8 = (bf16[384,1024]{1,0:T(8,128)(2,1)S(1)}, bf16[384,1024]{1,0:T(8,128)(2,1)}, u32[]{:S(2)}) copy-start(bf16[384,1024]{1,0:T(8,128)(2,1)} %param.9) | copy-start | bytes 2359300
  205.8 41.7 %all-to-all-start = ((bf16[8,384,128]{2,1,0:T(8,128)(2,1)}), bf16[8,384,128]{2,1,0:T(8,128)(2,1)S(1)}, u32[]{:S(2)}, u32[]{:S(2)}) async-start(bf16[8,384,128]{2,1,0:T(8,128)(2,1)} %reshape.250), calls=%async_computation | async-start | bytes 1572864 | tf_op jit(solution)/shard_map/all_to_all | solution.py:279
  213.7 297.5 %all-gather.11.cloned.1.call-start = ((), (), s32[]{:S(2)}) async-start(), calls=%async_computation.10 | async-start | bytes 7077888 | tf_op jit(solution)/shard_map/all_gather | solution.py:285
  247.5 16.4 %copy-start.2 = (bf16[8,384,128]{2,1,0:T(8,128)(2,1)}, bf16[8,384,128]{2,1,0:T(8,128)(2,1)S(1)}, u32[]{:S(2)}) copy-start(bf16[8,384,128]{2,1,0:T(8,128)(2,1)S(1)} %all-to-all-done) | copy-start | bytes 2359300
  253.4 10.5 %copy-start = (bf16[8192,1024]{1,0:T(8,128)(2,1)S(1)}, bf16[8192,1024]{1,0:T(8,128)(2,1)}, u32[]{:S(2)}) copy-start(bf16[8192,1024]{1,0:T(8,128)(2,1)} %all-gather.7.cloned.1.call-done) | copy-start | bytes 50331652
  253.4 11.5 %copy-start.10 = (f32[384,1024]{1,0:T(8,128)S(1)}, f32[384,1024]{1,0:T(8,128)}, u32[]{:S(2)}) copy-start(f32[384,1024]{1,0:T(8,128)} %get-tuple-element.60) | copy-start | bytes 4718596
  264.9 20.4 %copy-start.6 = (bf16[384,1024]{1,0:T(8,128)(2,1)S(1)}, bf16[384,1024]{1,0:T(8,128)(2,1)}, u32[]{:S(2)}) copy-start(bf16[384,1024]{1,0:T(8,128)(2,1)} %param.10) | copy-start | bytes 2359300
  288.9 9.0 %copy-start.7 = (bf16[384,1024]{1,0:T(8,128)(2,1)S(1)}, bf16[384,1024]{1,0:T(8,128)(2,1)}, u32[]{:S(2)}) copy-start(bf16[384,1024]{1,0:T(8,128)(2,1)} %param.10) | copy-start | bytes 2359300
  297.9 10.0 %copy-start.9 = (bf16[8,128,1024]{2,1,0:T(8,128)(2,1)S(1)}, bf16[8,128,1024]{2,1,0:T(8,128)(2,1)}, u32[]{:S(2)}) copy-start(bf16[8,128,1024]{2,1,0:T(8,128)(2,1)} %slice.147) | copy-start | bytes 6291460
  306.8 1.2 copy-start.5
  310.1 46.4 %all-to-all-start.1 = ((bf16[8,384,128]{1,2,0:T(8,128)(2,1)}), bf16[8,384,128]{1,2,0:T(8,128)(2,1)S(1)}, u32[]{:S(2)}, u32[]{:S(2)}) async-start(bf16[8,384,128]{1,2,0:T(8,128)(2,1)} %bitcast.30), calls=%async_computation.1 | async-start | bytes 1572864 | tf_op jit(solution)/shard_map/all_to_all | solution.py:355
  313.7 286.9 %all-gather.9.cloned.1.call-start = ((), (), s32[]{:S(2)}) async-start(), calls=%async_computation.9 | async-start | bytes 7077888 | tf_op jit(solution)/shard_map/all_gather | solution.py:321
  425.9 7.9 %copy-start.3 = (bf16[8,384,128]{2,1,0:T(8,128)(2,1)S(1)}, bf16[8,384,128]{2,1,0:T(8,128)(2,1)}, u32[]{:S(2)}) copy-start(bf16[8,384,128]{2,1,0:T(8,128)(2,1)} %copy-done.2) | copy-start | bytes 2359300
  430.2 68.3 %all-to-all-start.3 = ((f32[8,1,50720]{2,1,0:T(1,128)}), f32[8,1,50720]{2,1,0:T(1,128)S(1)}, u32[]{:S(2)}, u32[]{:S(2)}) async-start(f32[8,1,50720]{2,1,0:T(1,128)} %copy.68), calls=%async_computation.3 | async-start | bytes 3252224 | tf_op jit(solution)/shard_map/all_to_all | solution.py:396
  498.4 97.9 %all-to-all-start.4 = ((f32[8,1,128,1024]{3,2,1,0:T(8,128)}), f32[8,1,128,1024]{3,2,1,0:T(8,128)}, u32[]{:S(2)}, u32[]{:S(2)}) async-start(f32[8,1,128,1024]{3,2,1,0:T(8,128)} %convolution_bitcast_fusion), calls=%async_computation.4 | async-start | bytes 8388608 | tf_op jit(solution)/shard_map/all_to_all | solution.py:349
  503.0 212.8 %reduce-scatter.3.cloned.1.call-start = ((), (), s32[]{:S(2)}) async-start(), calls=%async_computation.8 | async-start | bytes 2785280 | tf_op jit(solution)/shard_map/reduce_scatter | solution.py:216
  519.6 1.2 copy-start.4
  521.1 79.6 %copy-start.11 = (bf16[2,1,256,1024]{3,2,1,0:T(8,128)(2,1)S(1)}, bf16[2,1,256,1024]{3,2,1,0:T(8,128)(2,1)}, u32[]{:S(2)}) copy-start(bf16[2,1,256,1024]{3,2,1,0:T(8,128)(2,1)} %constant_dynamic-slice_fusion.1) | copy-start | bytes 3145732
  600.6 121.0 %reduce-scatter.5.cloned.1.call-start = ((), (), s32[]{:S(2)}) async-start(), calls=%async_computation.11 | async-start | bytes 5242880 | tf_op jit(solution)/shard_map/reduce_scatter | solution.py:335
Sparse Core Ops, SparseCore 0:
  11.5 104.1 all-gather.12
  118.7 133.1 all-gather.6
  254.1 112.3 all-gather.10
  368.6 128.2 all-gather.8
  600.7 30.9 reduce-scatter.2
  639.1 43.5 reduce-scatter.4

commit v12 on v11

--- a/solution.py
+++ b/solution.py
@@ -10,7 +10,7 @@
 
 H = 16
 
-BLOCK = 768
+BLOCK = 512
 NEG = -1e30
 
 
@@ -321,10 +321,10 @@
     grad_mlp_seg = lax.all_gather(grad_mlp_low, "seq", axis=0, tiled=True)
     upper_own = contract_cols(normed_seg, own_rows(in_weights)) + own_rows(bias_up)
     active_own = jax.nn.gelu(upper_own, approximate=False).astype(jnp.bfloat16)
+    grad_down_own = contract_rows(active_own, grad_mlp_seg)
     grad_active_own = contract_cols(grad_mlp_seg, own_rows(down_weights))
     grad_upper_own = (grad_active_own * gelu_slope(upper_own)).astype(jnp.bfloat16)
     grad_in_own = contract_rows(grad_upper_own, normed_seg)
-    grad_down_own = contract_rows(active_own, grad_mlp_seg)
     mlp_stack = jnp.concatenate(
         [
             grad_in_own.reshape(mlp_groups, mlp_height, model_width),
@@ -340,14 +340,15 @@
     grad_bias_o = jnp.sum(grad_branch_low.astype(jnp.float32), axis=0)
     block_height = 4 * model_width // (fsdp_count * seq_count)
     out_blocks = model_width // (seq_count * block_height)
+    quarter = block_height // fsdp_count
     out_partial = jnp.transpose(
         contract_rows(attn_mixed, grad_branch_low).reshape(
-            out_blocks, seq_count, block_height, model_width
+            out_blocks, seq_count, fsdp_count, quarter, model_width
         ),
-        (1, 0, 2, 3),
-    )
-    out_parts = lax.all_to_all(out_partial, "seq", split_axis=0, concat_axis=0, tiled=True)
-    out_rows = jnp.sum(out_parts, axis=0)
+        (2, 0, 1, 3, 4),
+    )
+    out_parts = lax.all_to_all(out_partial, "fsdp", split_axis=0, concat_axis=0, tiled=True)
+    out_quarters = jnp.transpose(jnp.sum(out_parts, axis=0), (1, 0, 2, 3))
     grad_mixed_low = contract_cols(grad_branch_low, out_weights).astype(jnp.bfloat16)
     grad_split = jnp.transpose(
         grad_mixed_low.reshape(tokens, seq_count, head_width), (1, 0, 2)
@@ -393,11 +394,31 @@
         by_row.reshape(qkv_blocks, seq_count, block_height, head_width), (1, 0, 2, 3)
     )
     row_size = qkv_blocks * block_height * head_width
+    out_size = out_blocks * quarter * model_width
     exchanged = lax.all_to_all(
         jnp.concatenate(
-            [row_part.reshape(seq_count, -1), vector_part.reshape(seq_count, -1)], axis=1
+            [
+                row_part.reshape(seq_count, -1),
+                out_quarters.reshape(seq_count, -1),
+                vector_part.reshape(seq_count, -1),
+            ],
+            axis=1,
         ),
         "seq", split_axis=0, concat_axis=0, tiled=True,
+    )
+    own_quarters = jnp.sum(
+        exchanged[:, row_size : row_size + out_size].reshape(
+            seq_count, out_blocks, quarter, model_width
+        ),
+        axis=0,
+    )
+    out_rows = lax.dynamic_update_slice(
+        jnp.zeros((out_blocks, block_height, model_width), jnp.float32),
+        own_quarters,
+        (0, lax.axis_index("fsdp") * quarter, 0),
+    )
+    exchanged = jnp.concatenate(
+        [exchanged[:, :row_size], exchanged[:, row_size + out_size :]], axis=1
     )
     row_blocks = exchanged[:, :row_size].reshape(seq_count, qkv_blocks, block_height, head_width)
     qkv_rows = jnp.transpose(row_blocks, (1, 2, 0, 3)).reshape(qkv_blocks, block_height, model_width)

time: 738 us -> 670 us (0.908)
  waiting for transfers between devices: 287 us -> 207 us
  local copies, waits for them, and re-layouts: 92.1 us -> 101 us
    all_to_all x2, waiting for transfers between devices: 134 us -> 50.1 us  [the longest x1 50.1 us: layer_body(): lax.all_to_all(jnp.concatenate([row_part.reshape(seq_count, -1), out_quar...]
    unnamed x42 -> x41, local copies, waits for them, and re-layouts: 16.8 us -> 18.3 us
  transfers between devices with their start and end apart: 17 -> 17, of which waited for: 9 -> 8; matrix products, arithmetic and copies ran while one was open for 33% -> 38% of each run, Pallas kernels for 12% -> 14%
where the time goes in v12:
time: 670 us; the launch traced here: 662 us
  waiting for transfers between devices  207 us (31%)
  matrix products  117 us (17%)
  local copies, waits for them, and re-layouts  101 us (15%)
  Pallas kernels  91 us (14%)
  blocking collectives  57.6 us (9%)
  other arithmetic  40.6 us (6%)
  starting transfers between devices  31 us (5%)
  between operations  16.2 us (2%)
    ppermute x4, waiting for transfers between devices, ring_gather(): moving = lax.ppermute(moving, 'seq', backward_pairs)  90.1 us
    all_to_all x1, blocking collectives, layer_body(): lax.all_to_all(head_grads.reshape(seq_count, tokens, 3 * head_width), 'se...  57.6 us
    pallas_call x1, Pallas kernels, attn_backward(): pl.pallas_call(functools.partial(_bwd_kernel, scale=scale, block=block),...  51.8 us
    all_to_all x1, waiting for transfers between devices, layer_body(): lax.all_to_all(jnp.concatenate([row_part.reshape(seq_count, -1), out_quar...  50.1 us
    pallas_call x1, Pallas kernels, attn_forward(): pl.pallas_call(functools.partial(_fwd_kernel, scale=scale, block=block),...  39.2 us
    dot_general x3, matrix products, contract_rows(): lax.dot_general(left, right, (((0,), (0,)), ((), ())), preferred_element_...  38.6 us
    all_to_all x1, waiting for transfers between devices, layer_body(): lax.all_to_all(grad_split, 'seq', split_axis=0, concat_axis=0, tiled=True)  36.2 us
    all_to_all x1, waiting for transfers between devices, layer_body(): lax.all_to_all(mixed_rows, 'seq', split_axis=0, concat_axis=0, tiled=True)  28.9 us
  transfers between devices with their start and end apart: 17, of which 8 were waited for; matrix products, arithmetic and copies ran while one was open for 38% of the time, Pallas kernels for 14%

profile of v12, /device:TPU:0, one launch (start us, length us, event | category | flops | bytes accessed | tf_op | source)
XLA Modules:
  0.0 661.5 jit_solution(3507224938389207446)
XLA Ops:
  7.9 1.7 maximum_bitcast_fusion.1
  10.4 3.0 collective-permute-start
  13.4 22.9 %collective-permute-done = bf16[384,1024]{1,0:T(8,128)(2,1)S(1)} collective-permute-done((bf16[384,1024]{1,0:T(8,128)(2,1)}, bf16[384,1024]{1,0:T(8,128)(2,1)S(1)}, u32[]{:S(2)}, u32[]{:S(2)}) %collective-permute-start) | collective-permute-done | bytes 786464 | tf_op jit(solution)/shard_map/ppermute | solution.py:207
  36.3 1.7 collective-permute-start.1
  42.3 25.3 %collective-permute-done.1 = bf16[384,1024]{1,0:T(8,128)(2,1)S(1)} collective-permute-done((bf16[384,1024]{1,0:T(8,128)(2,1)S(1)}, bf16[384,1024]{1,0:T(8,128)(2,1)S(1)}, u32[]{:S(2)}, u32[]{:S(2)}) %collective-permute-start.1) | collective-permute-done | bytes 786464 | tf_op jit(solution)/shard_map/ppermute | solution.py:207
  68.0 1.3 compare_and_fusion
  69.4 1.7 collective-permute-start.5
  71.2 2.4 copy.55.dq_ref
  74.2 2.2 bitcast_dynamic-update-slice_fusion.7
  76.4 35.1 %collective-permute-done.2 = bf16[384,1024]{1,0:T(8,128)(2,1)} collective-permute-done((bf16[384,1024]{1,0:T(8,128)(2,1)S(1)}, bf16[384,1024]{1,0:T(8,128)(2,1)}, u32[]{:S(2)}, u32[]{:S(2)}) %collective-permute-start.2) | collective-permute-done | bytes 786464 | tf_op jit(solution)/shard_map/ppermute | solution.py:207
  112.5 2.0 collective-permute-start.6
  115.4 2.1 bitcast_dynamic-update-slice_fusion.4
  117.5 6.8 %collective-permute-done.3 = bf16[384,1024]{1,0:T(8,128)(2,1)S(1)} collective-permute-done((bf16[384,1024]{1,0:T(8,128)(2,1)}, bf16[384,1024]{1,0:T(8,128)(2,1)S(1)}, u32[]{:S(2)}, u32[]{:S(2)}) %collective-permute-start.3) | collective-permute-done | bytes 786464 | tf_op jit(solution)/shard_map/ppermute | solution.py:207
  128.5 6.6 %gather_fusion = bf16[8,384,1024]{2,1,0:T(8,128)(2,1)} fusion(bf16[8,384,1024]{2,1,0:T(8,128)(2,1)} %bitcast_dynamic-update-slice_fusion, s32[1024]{0:T(1024)S(1)} %pad_clamp_fusion), kind=kCustom, calls=%fused_computation | custom fusion | bytes 12582944 | tf_op jit(solution)/shard_map/jit(_take)/gather | solution.py:212
  135.1 6.6 %bitcast_select_fusion = bf16[3072,1024]{1,0:T(8,128)(2,1)} fusion(bf16[8,384,1024]{2,1,0:T(8,128)(2,1)} %gather_fusion, pred[3072]{0:T(1024)(128)(4,1)S(1)} %broadcast_in_dim.77), kind=kLoop, calls=%fused_computation.23 | loop fusion | flops 3145728 | bytes 12585984 | tf_op jit(solution)/shard_map/jit(_take)/select_n | solution.py:212
  141.8 3.5 slice.144
  145.3 2.6 copy-done.1
  149.6 4.8 fusion.133
  155.0 4.1 copy.54
  159.2 4.7 slice_bitcast_fusion
  163.8 39.2 %shard_map.136 = (bf16[2,3072,64]{2,1,0:T(8,128)(2,1)}, f32[2,3072,1]{2,1,0:T(8,128)}) custom-call(s32[6]{0:T(128)} %get-tuple-element.65.lo_ref, s32[6]{0:T(128)} %get-tuple-element.64.hi_ref, bf16[2,3072,64]{2,1,0:T(8,128)(2,1)} %get-tuple-element.48.q_ref, bf16[2,3072,64]{2,1,0:T(8,128)(2,1)} %get-tuple-element.47.k_ref, ...), custom_call_target="tpu_custom_call" | custom-call | tf_op jit(solution)/shard_map/pallas_call | solution.py:75
  203.1 3.9 copy.75
  207.0 1.5 reshape.256
  208.5 8.0 %all-to-all-start = ((bf16[8,384,128]{2,1,0:T(8,128)(2,1)}), bf16[8,384,128]{2,1,0:T(8,128)(2,1)S(1)}, u32[]{:S(2)}, u32[]{:S(2)}) async-start(bf16[8,384,128]{2,1,0:T(8,128)(2,1)} %reshape.256), calls=%async_computation | async-start | bytes 1572864 | tf_op jit(solution)/shard_map/all_to_all | solution.py:279
  217.7 3.2 slice.151
  220.9 28.9 %all-to-all-done = bf16[8,384,128]{2,1,0:T(8,128)(2,1)S(1)} async-done(((bf16[8,384,128]{2,1,0:T(8,128)(2,1)}), bf16[8,384,128]{2,1,0:T(8,128)(2,1)S(1)}, u32[]{:S(2)}, u32[]{:S(2)}) %all-to-all-start) | async-done | bytes 786464 | tf_op jit(solution)/shard_map/all_to_all | solution.py:279
  249.8 4.1 fusion.130
  255.5 10.4 %fusion.126 = f32[384,4096]{1,0:T(8,128)} fusion(bf16[384,1024]{1,0:T(8,128)(2,1)} %fusion.45, bf16[8192,1024]{1,0:T(8,128)(2,1)} %all-gather.7.cloned.1.call-done), kind=kOutput, calls=%fused_computation.248 | convolution fusion | flops 3221225472 | bytes 15466496 | tf_op jit(solution)/shard_map/dot_general | solution.py:226
  267.2 20.2 %fusion.44 = (f32[]{:T(128)}, f32[]{:T(128)}, f32[384]{0:T(512)S(1)}, f32[384,1024]{1,0:T(8,128)S(1)}) fusion(f32[384]{0:T(512)S(1)} %fusion.49, f32[1024]{0:T(1024)S(1)} %get-tuple-element.54, f32[384,1024]{1,0:T(8,128)S(1)} %copy-done.9, f32[1024]{0:T(1024)S(1)} %get-tuple-element.55, f32[1024]{0:T(1024)S(1)} %get-tuple-element.56, ...), kind=kOutput, calls=%fused_computation.81 | convolution fusion | flops 3330145792 | bytes 19435016 | tf_op jit(solution)/shard_map/dot_general | solution.py:288
  287.7 1.7 fusion.40
  289.4 1.8 convert_reduce_fusion.3
  291.2 9.0 %convert_reduce_fusion.1 = (f32[4096]{0:T(1024)S(1)}, bf16[384,4096]{1,0:T(8,128)(2,1)S(1)}) fusion(f32[384,4096]{1,0:T(8,128)} %fusion.126, f32[4096]{0:T(1024)S(1)} %slice.156, bf16[384,1024]{1,0:T(8,128)(2,1)} %get-tuple-element.31, bf16[8192,1024]{1,0:T(8,128)(2,1)} %all-gather.7.cloned.1.call-done), kind=kOutput, calls=%fused_computation.37 | convolution fusion | flops 3241668608 | bytes 18644992 | tf_op jit(solution)/shard_map/dot_general | solution.py:226
  300.2 8.4 %multiply_reduce_fusion = (f32[1024]{0:T(1024)S(1)}, f32[384]{0:T(512)S(1)}, f32[384]{0:T(512)S(1)}, f32[]{:T(128)}, f32[1024]{0:T(1024)S(1)}, /*index=5*/f32[384,1024]{1,0:T(8,128)S(1)}) fusion(f32[384,1024]{1,0:T(8,128)S(1)} %get-tuple-element.39, f32[384]{0:T(512)S(1)} %add_rsqrt_fusion.1, f32[384]{0:T(512)S(1)} %broadcast_multiply_fusion.5, ...), kind=kOutput, calls=%fused_computation.89 | convolution fusion | flops 3229479936 | bytes 17069572 | tf_op jit(solution)/shard_map/dot_general | solution.py:309
  312.4 3.5 all-to-all-start.1
  317.0 2.7 convolution_bitcast_fusion
  319.7 2.3 copy.69
  322.0 36.2 %all-to-all-done.1 = bf16[8,384,128]{1,2,0:T(8,128)(2,1)S(1)} async-done(((bf16[8,384,128]{1,2,0:T(8,128)(2,1)}), bf16[8,384,128]{1,2,0:T(8,128)(2,1)S(1)}, u32[]{:S(2)}, u32[]{:S(2)}) %all-to-all-start.1) | async-done | bytes 786464 | tf_op jit(solution)/shard_map/all_to_all | solution.py:356
  358.2 4.8 all-to-all-start.3
  363.1 6.2 broadcast_select_fusion
  369.3 3.3 concatenate.33
  373.4 2.0 copy.60
  375.4 51.8 %shard_map.137 = (f32[2,3072,64]{2,1,0:T(8,128)}, f32[2,3072,64]{2,1,0:T(8,128)}, f32[2,3072,64]{2,1,0:T(8,128)}) custom-call(s32[6]{0:T(128)} %get-tuple-element.65.lo_ref, s32[6]{0:T(128)} %get-tuple-element.64.hi_ref, bf16[2,3072,64]{2,1,0:T(8,128)(2,1)} %get-tuple-element.48.q_ref, bf16[2,3072,64]{2,1,0:T(8,128)(2,1)} %get-tuple-element.47.k_ref, ...), custom_call_target="tpu_custom_call" | custom-call | tf_op jit(solution)/shard_map/pallas_call | solution.py:152
  427.2 5.8 convert_reduce_fusion
  433.0 4.8 copy.65
  437.8 5.6 fusion.134
  444.8 2.7 reduce_sum.265
  448.3 4.3 copy.72
  452.7 4.4 all-to-all-start.4
  457.2 7.0 %fusion.131 = (bf16[4096,1024]{1,0:T(8,128)(2,1)S(1)}, bf16[4096,1024]{1,0:T(8,128)(2,1)S(1)}) fusion(bf16[8192,1024]{1,0:T(8,128)(2,1)} %all-gather.7.cloned.1.call-done), kind=kLoop, calls=%fused_computation.252 | loop fusion | bytes 33554432 | tf_op jit(solution)/shard_map/slice | solution.py:257
  465.4 8.2 %fusion.135 = f32[3072,512]{1,0:T(8,128)} fusion(bf16[3072,1024]{1,0:T(8,128)(2,1)} %all-gather.11.cloned.1.call-done, bf16[512,1024]{1,0:T(8,128)(2,1)S(1)} %bitcast.194), kind=kOutput, calls=%fused_computation.256 | convolution fusion | flops 3221225472 | bytes 13631488 | tf_op jit(solution)/shard_map/dot_general | solution.py:226
  473.6 50.1 %all-to-all-done.4 = f32[8,1,83488]{2,1,0:T(1,128)} async-done(((f32[8,1,83488]{2,1,0:T(1,128)}), f32[8,1,83488]{2,1,0:T(1,128)}, u32[]{:S(2)}, u32[]{:S(2)}) %all-to-all-start.4) | async-done | bytes 2671648 | tf_op jit(solution)/shard_map/all_to_all | solution.py:398
  523.7 1.9 copy.89
  526.9 2.5 reshape.229
  530.1 3.1 pad_maximum_fusion.1
  533.3 16.1 %fusion.46 = f32[512,1024]{1,0:T(8,128)S(1)} fusion(bf16[3072,1024]{1,0:T(8,128)(2,1)} %all-gather.11.cloned.1.call-done, f32[3072,512]{1,0:T(8,128)} %fusion.135, bf16[3072,1024]{1,0:T(8,128)(2,1)} %all-gather.9.cloned.1.call-done, bf16[512,1024]{1,0:T(8,128)(2,1)S(1)} %bitcast.193, f32[512]{0:T(512)S(1)} %bitcast.208), kind=kOutput, calls=%fused_computation.106 | convolution fusion | flops 6459752448 | bytes 22022144 | tf_op jit(solution)/shard_map/dot_general | solution.py:220
  549.4 19.8 %fusion.32 = f32[512,1024]{1,0:T(8,128)S(1)} fusion(bf16[3072,1024]{1,0:T(8,128)(2,1)} %all-gather.9.cloned.1.call-done, f32[3072,512]{1,0:T(8,128)} %fusion.135, f32[512]{0:T(512)S(1)} %bitcast.209), kind=kOutput, calls=%fused_computation.59 | convolution fusion | flops 3325034496 | bytes 14682112 | tf_op jit(solution)/shard_map/dot_general | solution.py:220
  569.2 2.4 pad_maximum_fusion
  571.6 5.0 copy.62
  577.5 57.6 %all_to_all.32 = bf16[8,384,384]{1,2,0:T(8,128)(2,1)S(1)} all-to-all(bf16[8,384,384]{1,2,0:T(8,128)(2,1)S(1)} %copy.63), channel_id=1, replica_groups=mesh['fsdp'=4,'seq'=8] {'seq'}, dimensions={0} | all-to-all | bytes 4718592 | tf_op jit(solution)/shard_map/all_to_all | solution.py:445
  635.1 2.9 copy.64
  638.0 3.6 reshape.219
  641.7 7.0 %bitcast_add_fusion = f32[384,1024]{1,0:T(8,128)} fusion(f32[384,1024]{1,0:T(8,128)} %copy-done.4, bf16[384,3,1024]{2,0,1:T(8,128)(2,1)S(1)} %reshape.219, bf16[3,1024,1024]{2,1,0:T(8,128)(2,1)} %bitcast.173), kind=kOutput, calls=%fused_computation.86 | convolution fusion | flops 2416312320 | bytes 11796480 | tf_op jit(solution)/shard_map/tie,ide->td/dot_general | solution.py:452
  650.7 1.3 slice_reduce_fusion.3
  652.5 1.9 slice_bitcast_fusion.3
  (136 shorter events, 32.9 us)
Async XLA Ops:
  7.2 134.6 %all-gather.13.cloned.1.call-start = ((), (), s32[]{:S(2)}) async-start(), calls=%async_computation.12 | async-start | bytes 9191424 | tf_op jit(solution)/shard_map/all_gather | solution.py:242
  9.6 245.9 %all-gather.7.cloned.1.call-start = ((), (), s32[]{:S(2)}) async-start(), calls=%async_computation.7 | async-start | bytes 17301504 | tf_op jit(solution)/shard_map/all_gather | solution.py:245
  10.4 26.0 %collective-permute-start = (bf16[384,1024]{1,0:T(8,128)(2,1)}, bf16[384,1024]{1,0:T(8,128)(2,1)S(1)}, u32[]{:S(2)}, u32[]{:S(2)}) collective-permute-start(bf16[384,1024]{1,0:T(8,128)(2,1)} %param.9), channel_id=1, source_target_pairs={{2,0},{4,2},{6,4},{7,6},{5,7},{3,5},{1,3},{0,1},{10,8},{12,10},{14... | collective-permute-start | bytes 2359304 | tf_op jit(solution)/shard_map/ppermute | solution.py:207
  36.3 31.3 %collective-permute-start.1 = (bf16[384,1024]{1,0:T(8,128)(2,1)S(1)}, bf16[384,1024]{1,0:T(8,128)(2,1)S(1)}, u32[]{:S(2)}, u32[]{:S(2)}) collective-permute-start(bf16[384,1024]{1,0:T(8,128)(2,1)S(1)} %collective-permute-done), channel_id=1, source_target_pairs={{2,0},{4,2},{6,4},{7,6},{5,7},{3,5},{1,3},{0,1},{10,8},{12,10},{14... | collective-permute-start | bytes 2359304 | tf_op jit(solution)/shard_map/ppermute | solution.py:207
  38.0 31.3 %collective-permute-start.4 = (bf16[384,1024]{1,0:T(8,128)(2,1)}, bf16[384,1024]{1,0:T(8,128)(2,1)S(1)}, u32[]{:S(2)}, u32[]{:S(2)}) collective-permute-start(bf16[384,1024]{1,0:T(8,128)(2,1)} %param.9), channel_id=1, source_target_pairs={{0,2},{2,4},{4,6},{6,7},{7,5},{5,3},{3,1},{1,0},{8,10},{10,12},{12... | collective-permute-start | bytes 2359304 | tf_op jit(solution)/shard_map/ppermute | solution.py:203
  67.6 43.9 %collective-permute-start.2 = (bf16[384,1024]{1,0:T(8,128)(2,1)S(1)}, bf16[384,1024]{1,0:T(8,128)(2,1)}, u32[]{:S(2)}, u32[]{:S(2)}) collective-permute-start(bf16[384,1024]{1,0:T(8,128)(2,1)S(1)} %collective-permute-done.1), channel_id=1, source_target_pairs={{2,0},{4,2},{6,4},{7,6},{5,7},{3,5},{1,3},{0,1},{10,8},{12,10},{14... | collective-permute-start | bytes 2359304 | tf_op jit(solution)/shard_map/ppermute | solution.py:207
  69.4 43.1 %collective-permute-start.5 = (bf16[384,1024]{1,0:T(8,128)(2,1)S(1)}, bf16[384,1024]{1,0:T(8,128)(2,1)S(1)}, u32[]{:S(2)}, u32[]{:S(2)}) collective-permute-start(bf16[384,1024]{1,0:T(8,128)(2,1)S(1)} %collective-permute-done.4), channel_id=1, source_target_pairs={{0,2},{2,4},{4,6},{6,7},{7,5},{5,3},{3,1},{1,0},{8,10},{10,12},{12... | collective-permute-start | bytes 2359304 | tf_op jit(solution)/shard_map/ppermute | solution.py:203
  111.5 12.7 %collective-permute-start.3 = (bf16[384,1024]{1,0:T(8,128)(2,1)}, bf16[384,1024]{1,0:T(8,128)(2,1)S(1)}, u32[]{:S(2)}, u32[]{:S(2)}) collective-permute-start(bf16[384,1024]{1,0:T(8,128)(2,1)} %collective-permute-done.2), channel_id=1, source_target_pairs={{2,0},{4,2},{6,4},{7,6},{5,7},{3,5},{1,3},{0,1},{10,8},{12,10},{14... | collective-permute-start | bytes 2359304 | tf_op jit(solution)/shard_map/ppermute | solution.py:207
  112.5 13.2 %collective-permute-start.6 = (bf16[384,1024]{1,0:T(8,128)(2,1)S(1)}, bf16[384,1024]{1,0:T(8,128)(2,1)S(1)}, u32[]{:S(2)}, u32[]{:S(2)}) collective-permute-start(bf16[384,1024]{1,0:T(8,128)(2,1)S(1)} %collective-permute-done.5), channel_id=1, source_target_pairs={{0,2},{2,4},{4,6},{6,7},{7,5},{5,3},{3,1},{1,0},{8,10},{10,12},{12... | collective-permute-start | bytes 2359304 | tf_op jit(solution)/shard_map/ppermute | solution.py:203
  145.3 2.7 copy-start.1
  203.1 46.7 %copy-start.7 = (bf16[384,1024]{1,0:T(8,128)(2,1)S(1)}, bf16[384,1024]{1,0:T(8,128)(2,1)}, u32[]{:S(2)}) copy-start(bf16[384,1024]{1,0:T(8,128)(2,1)} %param.9) | copy-start | bytes 2359300
  208.5 41.3 %all-to-all-start = ((bf16[8,384,128]{2,1,0:T(8,128)(2,1)}), bf16[8,384,128]{2,1,0:T(8,128)(2,1)S(1)}, u32[]{:S(2)}, u32[]{:S(2)}) async-start(bf16[8,384,128]{2,1,0:T(8,128)(2,1)} %reshape.256), calls=%async_computation | async-start | bytes 1572864 | tf_op jit(solution)/shard_map/all_to_all | solution.py:279
  216.5 248.9 %all-gather.11.cloned.1.call-start = ((), (), s32[]{:S(2)}) async-start(), calls=%async_computation.10 | async-start | bytes 7077888 | tf_op jit(solution)/shard_map/all_gather | solution.py:285
  249.8 16.2 %copy-start.2 = (bf16[8,384,128]{2,1,0:T(8,128)(2,1)}, bf16[8,384,128]{2,1,0:T(8,128)(2,1)S(1)}, u32[]{:S(2)}) copy-start(bf16[8,384,128]{2,1,0:T(8,128)(2,1)S(1)} %all-to-all-done) | copy-start | bytes 2359300
  255.5 10.8 %copy-start = (bf16[8192,1024]{1,0:T(8,128)(2,1)S(1)}, bf16[8192,1024]{1,0:T(8,128)(2,1)}, u32[]{:S(2)}) copy-start(bf16[8192,1024]{1,0:T(8,128)(2,1)} %all-gather.7.cloned.1.call-done) | copy-start | bytes 50331652
  255.5 11.7 %copy-start.9 = (f32[384,1024]{1,0:T(8,128)S(1)}, f32[384,1024]{1,0:T(8,128)}, u32[]{:S(2)}) copy-start(f32[384,1024]{1,0:T(8,128)} %get-tuple-element.60) | copy-start | bytes 4718596
  267.2 20.5 %copy-start.5 = (bf16[384,1024]{1,0:T(8,128)(2,1)S(1)}, bf16[384,1024]{1,0:T(8,128)(2,1)}, u32[]{:S(2)}) copy-start(bf16[384,1024]{1,0:T(8,128)(2,1)} %param.10) | copy-start | bytes 2359300
  291.2 9.0 %copy-start.6 = (bf16[384,1024]{1,0:T(8,128)(2,1)S(1)}, bf16[384,1024]{1,0:T(8,128)(2,1)}, u32[]{:S(2)}) copy-start(bf16[384,1024]{1,0:T(8,128)(2,1)} %param.10) | copy-start | bytes 2359300
  300.2 10.1 %copy-start.8 = (bf16[8,128,1024]{2,1,0:T(8,128)(2,1)S(1)}, bf16[8,128,1024]{2,1,0:T(8,128)(2,1)}, u32[]{:S(2)}) copy-start(bf16[8,128,1024]{2,1,0:T(8,128)(2,1)} %slice.151) | copy-start | bytes 6291460
  308.6 8.1 %copy-start.3 = (bf16[8,384,128]{2,1,0:T(8,128)(2,1)S(1)}, bf16[8,384,128]{2,1,0:T(8,128)(2,1)}, u32[]{:S(2)}) copy-start(bf16[8,384,128]{2,1,0:T(8,128)(2,1)} %copy-done.2) | copy-start | bytes 2359300
  309.1 1.2 copy-start.4
  312.4 45.8 %all-to-all-start.1 = ((bf16[8,384,128]{1,2,0:T(8,128)(2,1)}), bf16[8,384,128]{1,2,0:T(8,128)(2,1)S(1)}, u32[]{:S(2)}, u32[]{:S(2)}) async-start(bf16[8,384,128]{1,2,0:T(8,128)(2,1)} %bitcast.30), calls=%async_computation.1 | async-start | bytes 1572864 | tf_op jit(solution)/shard_map/all_to_all | solution.py:356
  358.2 86.6 %all-to-all-start.3 = ((f32[4,1,8,32,1024]{4,3,2,1,0:T(8,128)}), f32[4,1,8,32,1024]{4,3,2,1,0:T(8,128)}, u32[]{:S(2)}, u32[]{:S(2)}) async-start(f32[4,1,8,32,1024]{4,3,2,1,0:T(8,128)} %copy.69), calls=%async_computation.3 | async-start | bytes 8388608 | tf_op jit(solution)/shard_map/all_to_all | solution.py:350
  363.1 170.1 %all-gather.9.cloned.1.call-start = ((), (), s32[]{:S(2)}) async-start(), calls=%async_computation.9 | async-start | bytes 7077888 | tf_op jit(solution)/shard_map/all_gather | solution.py:321
  452.7 71.0 %all-to-all-start.4 = ((f32[8,1,83488]{2,1,0:T(1,128)}), f32[8,1,83488]{2,1,0:T(1,128)}, u32[]{:S(2)}, u32[]{:S(2)}) async-start(f32[8,1,83488]{2,1,0:T(1,128)} %copy.72), calls=%async_computation.4 | async-start | bytes 5349376 | tf_op jit(solution)/shard_map/all_to_all | solution.py:398
  457.1 191.6 %reduce-scatter.3.cloned.1.call-start = ((), (), s32[]{:S(2)}) async-start(), calls=%async_computation.8 | async-start | bytes 2785280 | tf_op jit(solution)/shard_map/reduce_scatter | solution.py:216
  529.7 3.5 copy-start.10
  533.2 121.3 %reduce-scatter.5.cloned.1.call-start = ((), (), s32[]{:S(2)}) async-start(), calls=%async_computation.11 | async-start | bytes 5242880 | tf_op jit(solution)/shard_map/reduce_scatter | solution.py:335
Sparse Core Ops, SparseCore 0:
  11.5 104.1 all-gather.12
  118.7 133.1 all-gather.6
  255.6 111.8 all-gather.10
  369.6 100.3 all-gather.8
  533.3 30.6 reduce-scatter.2
  571.8 43.1 reduce-scatter.4
